TPU v7x, 16 devices: a whole 2x2x2 slice. The times are simulated.
16 devices in a mesh: ep: 4 (over z, y), dp: 4 (over x, core).
Axes of the slice: x: 2, y: 2, z: 2, core: 2. Of those that a mesh axis runs over, the one named last changes fastest.
Arguments:
- tokens: bfloat16 [8192, 384], P(('dp', 'ep'))
- dy_out: bfloat16 [8192, 384], P(('dp', 'ep'))
- dense_w1: bfloat16 [384, 384], replicated
- route_idx1: int32 [8192, 4], P(('dp', 'ep'))
- route_gate1: float32 [8192, 4], P(('dp', 'ep'))
- w_gate1: bfloat16 [16, 384, 672], P('ep')
- w_up1: bfloat16 [16, 384, 672], P('ep')
- w_down1: bfloat16 [16, 672, 384], P('ep')
- dense_w2: bfloat16 [384, 384], replicated
- route_idx2: int32 [8192, 4], P(('dp', 'ep'))
- route_gate2: float32 [8192, 4], P(('dp', 'ep'))
- w_gate2: bfloat16 [16, 384, 672], P('ep')
- w_up2: bfloat16 [16, 384, 672], P('ep')
- w_down2: bfloat16 [16, 672, 384], P('ep')
Outputs:
- output 1: bfloat16 [8192, 384], P(('dp', 'ep'))
- output 2: bfloat16 [384, 384], P(('dp', 'ep'))
- output 3: bfloat16 [16, 384, 672], P('ep', 'dp')
- output 4: bfloat16 [16, 384, 672], P('ep', 'dp')
- output 5: bfloat16 [16, 672, 384], P('ep', None, 'dp')
- output 6: bfloat16 [384, 384], P(('dp', 'ep'))
- output 7: bfloat16 [16, 384, 672], P('ep', 'dp')
- output 8: bfloat16 [16, 384, 672], P('ep', 'dp')
- output 9: bfloat16 [16, 672, 384], P('ep', None, 'dp')
All inputs are finite; a program needn't handle non-finite values.
Results may differ from a plain program's by a relative error of at most 0.02.
Values are sent between devices in bfloat16 or wider.
A program may use at most 1 GiB of HBM per device.

v0:
```python
import jax
import jax.numpy as jnp
from jax import lax
from jax.sharding import PartitionSpec as P


def copy_rows(route_idx, n_exp, capacity):
    flat_exp = route_idx.reshape(-1)
    n_copies = flat_exp.shape[0]
    order = jnp.argsort(flat_exp, stable=True).astype(jnp.int32)
    sorted_exp = jnp.take(flat_exp, order)
    counts = jnp.zeros((n_exp,), jnp.int32).at[flat_exp].add(1)
    starts = jnp.cumsum(counts, dtype=jnp.int32) - counts
    dest_row = sorted_exp * capacity + jnp.arange(n_copies, dtype=jnp.int32) - jnp.take(starts, sorted_exp)
    return jnp.zeros((n_copies,), jnp.int32).at[order].set(dest_row).reshape(route_idx.shape)


def row_fill(flat_pos, values, n_rows, empty):
    return jnp.full((n_rows,), empty, values.dtype).at[flat_pos.reshape(-1)].set(values.reshape(-1))


def dispatch(x_loc, dense_w, route_idx, n_exp):
    n_tok, top_k = route_idx.shape
    capacity = 2 * n_tok * top_k // n_exp
    mixed = (x_loc.astype(jnp.float32) + jnp.dot(x_loc, dense_w, preferred_element_type=jnp.float32)).astype(jnp.bfloat16)
    flat_pos = copy_rows(route_idx, n_exp, capacity)
    tok_ids = jnp.broadcast_to(jnp.arange(n_tok, dtype=jnp.int32)[:, None], (n_tok, top_k))
    row_tok = row_fill(flat_pos, tok_ids, n_exp * capacity, n_tok)
    send = jnp.take(mixed, row_tok, axis=0, mode='fill', fill_value=0).reshape(n_exp, capacity, -1)
    recv = lax.all_to_all(send, 'ep', 0, 1, tiled=True)
    return mixed, flat_pos, row_tok, recv


def expert_hidden(recv, w_gate, w_up):
    a_pre = jnp.einsum('ecd,edf->ecf', recv, w_gate, preferred_element_type=jnp.float32)
    b_pre = jnp.einsum('ecd,edf->ecf', recv, w_up, preferred_element_type=jnp.float32)
    hidden = (jax.nn.silu(a_pre) * b_pre).astype(jnp.bfloat16)
    return a_pre, b_pre, hidden


def combine(mixed, hidden, w_down, flat_pos, route_gate):
    expert_out = jnp.einsum('ecf,efd->ecd', hidden, w_down, preferred_element_type=jnp.float32).astype(jnp.bfloat16)
    returned = lax.all_to_all(expert_out, 'ep', 1, 0, tiled=True)
    returned = returned.reshape(-1, returned.shape[-1])
    picked = jnp.take(returned, flat_pos, axis=0)
    return (mixed.astype(jnp.float32) + jnp.sum(route_gate[:, :, None] * picked, axis=1)).astype(jnp.bfloat16)


def layer_backward(grad_y, x_loc, dense_w, route_gate, w_gate, w_up, w_down, n_exp, flat_pos, row_tok, recv, a_pre, b_pre, hidden):
    n_rows = row_tok.shape[0]
    capacity = n_rows // n_exp
    row_gate = row_fill(flat_pos, route_gate, n_rows, 0.0)
    grad_send = (jnp.take(grad_y, row_tok, axis=0, mode='fill', fill_value=0) * row_gate[:, None]).astype(jnp.bfloat16)
    grad_out = lax.all_to_all(grad_send.reshape(n_exp, capacity, -1), 'ep', 0, 1, tiled=True)
    grad_hidden = jnp.einsum('ecd,efd->ecf', grad_out, w_down, preferred_element_type=jnp.float32).astype(jnp.bfloat16)
    grad_down = jnp.einsum('ecf,ecd->efd', hidden, grad_out, preferred_element_type=jnp.float32)
    sigma_a = jax.nn.sigmoid(a_pre)
    hidden_wide = grad_hidden.astype(jnp.float32)
    grad_a = (hidden_wide * b_pre * sigma_a * (1.0 + a_pre * (1.0 - sigma_a))).astype(jnp.bfloat16)
    grad_b = (hidden_wide * a_pre * sigma_a).astype(jnp.bfloat16)
    grad_gate = jnp.einsum('ecd,ecf->edf', recv, grad_a, preferred_element_type=jnp.float32)
    grad_up = jnp.einsum('ecd,ecf->edf', recv, grad_b, preferred_element_type=jnp.float32)
    grad_recv = (jnp.einsum('ecf,edf->ecd', grad_a, w_gate, preferred_element_type=jnp.float32)
                 + jnp.einsum('ecf,edf->ecd', grad_b, w_up, preferred_element_type=jnp.float32)).astype(jnp.bfloat16)
    grad_back = lax.all_to_all(grad_recv, 'ep', 1, 0, tiled=True)
    grad_back = grad_back.reshape(-1, grad_back.shape[-1])
    grad_picked = jnp.take(grad_back, flat_pos, axis=0)
    grad_mixed = (grad_y.astype(jnp.float32) + jnp.sum(grad_picked, axis=1, dtype=jnp.float32)).astype(jnp.bfloat16)
    grad_dense = jnp.einsum('td,te->de', x_loc, grad_mixed, preferred_element_type=jnp.float32)
    grad_x = (grad_mixed.astype(jnp.float32) + jnp.einsum('te,de->td', grad_mixed, dense_w, preferred_element_type=jnp.float32)).astype(jnp.bfloat16)
    return grad_x, (grad_dense, grad_gate, grad_up, grad_down)


def reduce_grads(partials):
    grad_dense, grad_gate, grad_up, grad_down = [piece.astype(jnp.bfloat16) for piece in partials]
    return (lax.psum_scatter(grad_dense, ('dp', 'ep'), scatter_dimension=0, tiled=True),
            lax.psum_scatter(grad_gate, 'dp', scatter_dimension=1, tiled=True),
            lax.psum_scatter(grad_up, 'dp', scatter_dimension=1, tiled=True),
            lax.psum_scatter(grad_down, 'dp', scatter_dimension=2, tiled=True))


def solution(mesh):
    ep_size = mesh.shape['ep']
    tok_spec = P(('dp', 'ep'), None)
    exp_spec = P('ep', None, None)
    layer_specs = (P(None, None), tok_spec, tok_spec, exp_spec, exp_spec, exp_spec)
    grad_specs = (P(('dp', 'ep'), None), P('ep', 'dp', None), P('ep', 'dp', None), P('ep', None, 'dp'))

    def local_step(tokens, dy_out, dense_w1, route_idx1, route_gate1, w_gate1, w_up1, w_down1, dense_w2, route_idx2, route_gate2, w_gate2, w_up2, w_down2):
        n_exp = w_gate1.shape[0] * ep_size
        mixed_one, place_one, rowtok_one, recv_one = dispatch(tokens, dense_w1, route_idx1, n_exp)
        a_one, b_one, hid_one = expert_hidden(recv_one, w_gate1, w_up1)
        mid_tok = combine(mixed_one, hid_one, w_down1, place_one, route_gate1)
        mixed_two, place_two, rowtok_two, recv_two = dispatch(mid_tok, dense_w2, route_idx2, n_exp)
        a_two, b_two, hid_two = expert_hidden(recv_two, w_gate2, w_up2)
        grad_mid, parts_two = layer_backward(dy_out, mid_tok, dense_w2, route_gate2, w_gate2, w_up2, w_down2, n_exp, place_two, rowtok_two, recv_two, a_two, b_two, hid_two)
        grads_two = reduce_grads(parts_two)
        grad_tok, parts_one = layer_backward(grad_mid, tokens, dense_w1, route_gate1, w_gate1, w_up1, w_down1, n_exp, place_one, rowtok_one, recv_one, a_one, b_one, hid_one)
        grads_one = reduce_grads(parts_one)
        return (grad_tok,) + grads_one + grads_two

    return jax.shard_map(local_step, mesh=mesh, in_specs=(tok_spec, tok_spec) + layer_specs + layer_specs,
                         out_specs=(tok_spec,) + grad_specs + grad_specs, check_vma=False)
```

profile of v0, /device:TPU:0, one launch (start us, length us, event | category | flops | bytes accessed | tf_op | source)
XLA Modules:
  0.0 906.3 jit_solution(2677859713112036193)
XLA Ops:
  8.6 14.7 %scatter_custom_fusion.4 = s32[16]{0:T(128)S(1)} fusion(s32[2048]{0:T(1024)S(1)} %bitcast.140, s32[2048]{0:T(1024)S(1)} %broadcast.150, s32[]{:T(128)} %constant.42.clone.1), kind=kCustom, calls=%fused_computation.111 | custom fusion | flops 2048 | bytes 68 | tf_op jit(solution)/shard_map/scatter-add | solution.py:12
  24.2 5.0 sort.32
  29.3 11.8 %gather_fusion.2 = s32[2048]{0:T(1024)S(1)} fusion(s32[2048]{0:T(1024)S(1)} %reshape.208, s32[2048]{0:T(1024)S(1)} %broadcast_clamp_fusion.2), kind=kCustom, calls=%fused_computation.3.clone | custom fusion | bytes 24576 | tf_op jit(solution)/shard_map/jit(_take)/gather | solution.py:11
  41.1 10.2 %select_subtract_fusion = (s32[2048]{0:T(1024)S(1)}, s32[2048]{0:T(1024)S(1)}) fusion(s32[2048]{0:T(1024)S(1)} %gather_fusion.2, s32[]{:T(128)} %bitcast.39, s32[]{:T(128)} %bitcast.38, s32[]{:T(128)} %bitcast.37, s32[]{:T(128)} %bitcast.36, s32[]{:T(128)} %bitcast.35, s32[]{:T(128)} %bitcast.34, s32[]{:T(128)} %bitcast.33, s32[]{:T(128)} %bitcast.32, ...), kind=kLoop, calls=%fused_computation.86 | loop fusion | flops 96256 | bytes 32832 | tf_op jit(solution)/shard_map/sub | solution.py:14
  51.2 8.0 scatter_custom_fusion.5
  59.5 8.1 scatter_custom_fusion.6
  68.0 17.1 %gather_fusion.3 = bf16[4096,384]{1,0:T(8,128)(2,1)} fusion(bf16[512,384]{1,0:T(8,128)(2,1)S(1)} %fusion.12, s32[4096]{0:T(1024)S(1)} %fusion.18), kind=kCustom, calls=%fused_computation.4.clone | custom fusion | bytes 6307840 | tf_op jit(solution)/shard_map/jit(_take)/gather | solution.py:29
  88.6 6.2 all-to-all-start.1
  95.1 36.4 %all-to-all-done.1 = bf16[16,256,384]{2,1,0:T(8,128)(2,1)} async-done(((bf16[16,256,384]{2,1,0:T(8,128)(2,1)}), bf16[16,256,384]{2,1,0:T(8,128)(2,1)}, u32[]{:S(2)}, u32[]{:S(2)}) %all-to-all-start.1) | async-done | bytes 3145760 | tf_op jit(solution)/shard_map/all_to_all | solution.py:30
  137.2 10.9 %multiply_convert_fusion.1 = (bf16[4,1024,672]{1,2,0:T(8,128)(2,1)}, f32[4,1024,672]{1,2,0:T(8,128)}) fusion(f32[4,1024,672]{1,2,0:T(8,128)S(1)} %fusion.44, bf16[4,1024,384]{2,1,0:T(8,128)(2,1)S(1)} %bitcast.122, bf16[4,384,672]{1,2,0:T(8,128)(2,1)} %param.28), kind=kOutput, calls=%fused_computation.33 | convolution fusion | flops 2130444288 | bytes 32735232 | tf_op jit(solution)/shard_map/ecd,edf->ecf/dot_general | solution.py:36
  148.1 6.7 convolution_convert_fusion.2
  154.8 4.2 copy.69
  159.0 4.8 all-to-all-start.2
  164.3 14.7 %scatter_custom_fusion = s32[16]{0:T(128)S(1)} fusion(s32[2048]{0:T(1024)S(1)} %bitcast.139, s32[2048]{0:T(1024)S(1)} %broadcast.150, s32[]{:T(128)} %constant.42.clone.1), kind=kCustom, calls=%fused_computation.113 | custom fusion | flops 2048 | bytes 68 | tf_op jit(solution)/shard_map/scatter-add | solution.py:12
  179.2 5.0 sort.31
  184.3 11.8 %gather_fusion = s32[2048]{0:T(1024)S(1)} fusion(s32[2048]{0:T(1024)S(1)} %reshape.201, s32[2048]{0:T(1024)S(1)} %broadcast_clamp_fusion.3), kind=kCustom, calls=%fused_computation.clone | custom fusion | bytes 24576 | tf_op jit(solution)/shard_map/jit(_take)/gather | solution.py:11
  197.1 10.1 %select_subtract_fusion.1 = (s32[2048]{0:T(1024)S(1)}, s32[2048]{0:T(1024)S(1)}) fusion(s32[2048]{0:T(1024)S(1)} %gather_fusion, s32[]{:T(128)} %bitcast.17, s32[]{:T(128)} %bitcast.16, s32[]{:T(128)} %bitcast.15, s32[]{:T(128)} %bitcast.14, s32[]{:T(128)} %bitcast.13, s32[]{:T(128)} %bitcast.12, s32[]{:T(128)} %bitcast.11, s32[]{:T(128)} %bitcast.10, ...), kind=kLoop, calls=%fused_computation.87 | loop fusion | flops 96256 | bytes 32832 | tf_op jit(solution)/shard_map/sub | solution.py:14
  207.2 8.0 scatter_custom_fusion.1
  215.3 8.1 scatter_custom_fusion.2
  223.3 8.1 scatter_custom_fusion.3
  231.4 17.1 %gather_fusion.1 = bf16[4096,384]{1,0:T(8,128)(2,1)} fusion(bf16[512,384]{1,0:T(8,128)(2,1)S(1)} %copy-done.2, s32[4096]{0:T(1024)S(1)} %fusion.17), kind=kCustom, calls=%fused_computation.1.clone | custom fusion | bytes 6307840 | tf_op jit(solution)/shard_map/jit(_take)/gather | solution.py:53
  248.5 5.6 multiply_convert_fusion.3
  254.1 4.9 all-to-all-start
  260.2 4.2 copy.70
  264.4 11.2 %gather_fusion.4 = bf16[2048,384]{1,0:T(8,128)(2,1)} fusion(bf16[4096,384]{1,0:T(8,128)(2,1)} %bitcast.120, s32[2048]{0:T(1024)S(1)} %broadcast_clamp_fusion.1), kind=kCustom, calls=%fused_computation.2.clone | custom fusion | bytes 3153920 | tf_op jit(solution)/shard_map/jit(_take)/gather | solution.py:45
  279.5 4.7 multiply_reduce_fusion
  286.5 17.0 %gather_fusion.5 = bf16[4096,384]{1,0:T(8,128)(2,1)} fusion(bf16[512,384]{1,0:T(8,128)(2,1)S(1)} %fusion.13, s32[4096]{0:T(1024)S(1)} %fusion.17), kind=kCustom, calls=%fused_computation.5.clone | custom fusion | bytes 6307840 | tf_op jit(solution)/shard_map/jit(_take)/gather | solution.py:29
  307.0 4.7 all-to-all-start.3
  316.0 4.8 convolution_convert_fusion.1
  320.8 26.6 %all-to-all-done.3 = bf16[16,256,384]{2,1,0:T(8,128)(2,1)} async-done(((bf16[16,256,384]{2,1,0:T(8,128)(2,1)}), bf16[16,256,384]{2,1,0:T(8,128)(2,1)}, u32[]{:S(2)}, u32[]{:S(2)}) %all-to-all-start.3) | async-done | bytes 3145760 | tf_op jit(solution)/shard_map/all_to_all | solution.py:30
  349.9 5.7 fusion.45
  355.6 16.5 %fusion.4 = (bf16[4,1024,672]{1,2,0:T(8,128)(2,1)}, bf16[4,1024,672]{1,2,0:T(8,128)(2,1)}, f32[4,1024,672]{1,2,0:T(8,128)}) fusion(bf16[4,1024,672]{1,2,0:T(8,128)(2,1)} %convolution_convert_fusion.1, f32[4,1024,672]{1,2,0:T(8,128)} %fusion.45, bf16[4,1024,384]{2,1,0:T(8,128)(2,1)S(1)} %bitcast.126, bf16[4,384,672]{1,2,0:T(8,128)(2,1)S(1)} %copy-done), kind=kOutput, calls=%fused_computation.25 | convolution fusion | flops 2152464384 | bytes 43745280 | tf_op jit(solution)/shard_map/ecd,edf->ecf/dot_general | solution.py:35
  372.0 6.1 fusion.46
  378.1 6.2 add_convert_fusion.1
  384.3 4.1 copy.72
  388.4 4.7 all-to-all-start.4
  393.5 8.2 scatter_custom_fusion.7
  402.0 26.4 %all-to-all-done.4 = bf16[4,1024,384]{2,0,1:T(4,128)(2,1)} async-done(((bf16[4,1024,384]{2,0,1:T(4,128)(2,1)}), bf16[4,1024,384]{2,0,1:T(4,128)(2,1)}, u32[]{:S(2)}, u32[]{:S(2)}) %all-to-all-start.4) | async-done | bytes 3145760 | tf_op jit(solution)/shard_map/all_to_all | solution.py:65
  428.4 4.1 copy.73
  432.5 9.5 %gather_fusion.6 = bf16[2048,384]{1,0:T(8,128)(2,1)S(1)} fusion(bf16[4096,384]{1,0:T(8,128)(2,1)} %bitcast.118, s32[2048]{0:T(1024)S(1)} %broadcast_clamp_fusion), kind=kCustom, calls=%fused_computation.7.clone | custom fusion | bytes 3153920 | tf_op jit(solution)/shard_map/jit(_take)/gather | solution.py:67
  443.4 4.3 convert_reduce_fusion.1
  448.1 17.0 %gather_fusion.7 = bf16[4096,384]{1,0:T(8,128)(2,1)} fusion(bf16[512,384]{1,0:T(8,128)(2,1)S(1)} %fusion.14, s32[4096]{0:T(1024)S(1)} %fusion.18), kind=kCustom, calls=%fused_computation.6.clone | custom fusion | bytes 6307840 | tf_op jit(solution)/shard_map/jit(_take)/gather | solution.py:53
  468.6 38.8 %all_to_all.117 = bf16[16,256,384]{2,1,0:T(8,128)(2,1)S(1)} all-to-all(bf16[16,256,384]{2,1,0:T(8,128)(2,1)S(1)} %bitcast.136), channel_id=1, replica_groups=mesh['ep'=4,'dp'=4] {'ep'}, dimensions={0} | all-to-all | bytes 6291456 | tf_op jit(solution)/shard_map/all_to_all | solution.py:54
  507.8 14.6 %fusion.9 = (bf16[4,1024,672]{1,2,0:T(8,128)(2,1)}, bf16[4,1024,672]{1,2,0:T(8,128)(2,1)}) fusion(f32[4,1024,672]{1,2,0:T(8,128)} %copy-done.3, f32[4,1024,672]{1,2,0:T(8,128)} %get-tuple-element.85, bf16[4,1024,384]{2,1,0:T(8,128)(2,1)S(1)} %bitcast.137, bf16[4,672,384]{2,1,0:T(8,128)(2,1)} %param.29), kind=kOutput, calls=%fused_computation.30 | convolution fusion | flops 2155216896 | bytes 38240256 | tf_op jit(solution)/shard_map/ecd,efd->ecf/dot_general | solution.py:55
  522.4 5.7 fusion.47
  528.1 6.2 add_convert_fusion
  536.7 37.4 %all_to_all.118 = bf16[4,1024,384]{2,0,1:T(4,128)(2,1)S(1)} all-to-all(bf16[4,1024,384]{2,0,1:T(4,128)(2,1)S(1)} %copy.76), channel_id=1, replica_groups=mesh['ep'=4,'dp'=4] {'ep'}, dimensions={1} | all-to-all | bytes 6291456 | tf_op jit(solution)/shard_map/all_to_all | solution.py:65
  576.3 11.1 %gather_fusion.8 = bf16[2048,384]{1,0:T(8,128)(2,1)} fusion(bf16[4096,384]{1,0:T(8,128)(2,1)} %bitcast.119, s32[2048]{0:T(1024)S(1)} %broadcast_clamp_fusion.1), kind=kCustom, calls=%fused_computation.8.clone | custom fusion | bytes 3153920 | tf_op jit(solution)/shard_map/jit(_take)/gather | solution.py:67
  587.5 4.0 reshape.478
  591.5 4.3 convert_reduce_fusion
  599.3 11.7 %fusion.11 = bf16[4,672,384]{1,2,0:T(8,128)(2,1)} fusion(bf16[4,1024,384]{2,1,0:T(8,128)(2,1)} %bitcast.132, f32[4,1024,672]{1,2,0:T(8,128)} %fusion.45, f32[4,1024,672]{1,2,0:T(8,128)} %get-tuple-element.86), kind=kOutput, calls=%fused_computation.48 | convolution fusion | flops 2131476480 | bytes 27230208 | tf_op jit(solution)/shard_map/ecf,ecd->efd/dot_general | solution.py:56
  611.1 7.8 convolution_convert_fusion.4
  619.2 7.8 convolution_convert_fusion.3
  627.0 7.6 convolution_convert_fusion.5
  634.7 7.8 convolution_convert_fusion.7
  642.9 7.9 convolution_convert_fusion.6
  653.2 8.5 all-reduce.4.cloned.1.call-done
  663.5 43.5 %reduce-scatter.23.cloned.1.call-done = bf16[24,384]{1,0:T(8,128)(2,1)} async-done(((bf16[384,384]{1,0:T(8,128)(2,1)}), bf16[24,384]{1,0:T(8,128)(2,1)}) %reduce-scatter.23.cloned.1.call-update) | async-done | bytes 18448
  707.0 32.1 %reduce-scatter.21.cloned.1.call-done = bf16[4,672,96]{1,2,0:T(8,128)(2,1)} async-done(((bf16[4,672,384]{1,2,0:T(8,128)(2,1)}), bf16[4,672,96]{1,2,0:T(8,128)(2,1)}) %reduce-scatter.21.cloned.1.call-update) | async-done | bytes 516112 | tf_op jit(solution)/shard_map/reduce_scatter | solution.py:79
  739.0 31.9 %reduce-scatter.17.cloned.1.call-done = bf16[4,96,672]{2,1,0:T(8,128)(2,1)} async-done(((bf16[4,384,672]{2,1,0:T(8,128)(2,1)}), bf16[4,96,672]{2,1,0:T(8,128)(2,1)}) %reduce-scatter.17.cloned.1.call-update) | async-done | bytes 516112 | tf_op jit(solution)/shard_map/reduce_scatter | solution.py:77
  771.0 31.9 %reduce-scatter.19.cloned.1.call-done = bf16[4,96,672]{2,1,0:T(8,128)(2,1)} async-done(((bf16[4,384,672]{2,1,0:T(8,128)(2,1)}), bf16[4,96,672]{2,1,0:T(8,128)(2,1)}) %reduce-scatter.19.cloned.1.call-update) | async-done | bytes 516112 | tf_op jit(solution)/shard_map/reduce_scatter | solution.py:78
  802.9 31.9 %reduce-scatter.15.cloned.1.call-done = bf16[4,672,96]{1,2,0:T(8,128)(2,1)} async-done(((bf16[4,672,384]{1,2,0:T(8,128)(2,1)}), bf16[4,672,96]{1,2,0:T(8,128)(2,1)}) %reduce-scatter.15.cloned.1.call-update) | async-done | bytes 516112 | tf_op jit(solution)/shard_map/reduce_scatter | solution.py:79
  834.8 32.1 %reduce-scatter.11.cloned.1.call-done = bf16[4,96,672]{2,1,0:T(8,128)(2,1)} async-done(((bf16[4,384,672]{2,1,0:T(8,128)(2,1)}), bf16[4,96,672]{2,1,0:T(8,128)(2,1)}) %reduce-scatter.11.cloned.1.call-update) | async-done | bytes 516112 | tf_op jit(solution)/shard_map/reduce_scatter | solution.py:77
  866.9 32.0 %reduce-scatter.13.cloned.1.call-done = bf16[4,96,672]{2,1,0:T(8,128)(2,1)} async-done(((bf16[4,384,672]{2,1,0:T(8,128)(2,1)}), bf16[4,96,672]{2,1,0:T(8,128)(2,1)}) %reduce-scatter.13.cloned.1.call-update) | async-done | bytes 516112 | tf_op jit(solution)/shard_map/reduce_scatter | solution.py:78
  (150 shorter events, 50.3 us)
Async XLA Ops:
  7.2 348.4 %copy-start = (bf16[4,384,672]{1,2,0:T(8,128)(2,1)S(1)}, bf16[4,384,672]{1,2,0:T(8,128)(2,1)}, u32[]{:S(2)}) copy-start(bf16[4,384,672]{1,2,0:T(8,128)(2,1)} %param.33) | copy-start | bytes 6193156
  29.3 38.4 %copy-start.21 = (bf16[512,384]{1,0:T(8,128)(2,1)S(1)}, bf16[512,384]{1,0:T(8,128)(2,1)}, u32[]{:S(2)}) copy-start(bf16[512,384]{1,0:T(8,128)(2,1)} %param.22) | copy-start | bytes 1179652
  29.3 38.4 %copy-start.23 = (bf16[384,384]{1,0:T(8,128)(2,1)S(1)}, bf16[384,384]{1,0:T(8,128)(2,1)}, u32[]{:S(2)}) copy-start(bf16[384,384]{1,0:T(8,128)(2,1)} %param.24) | copy-start | bytes 884740
  59.3 8.3 copy-start.30
  67.6 17.5 %copy-start.25 = (pred[4096]{0:T(1024)(128)(4,1)}, pred[4096]{0:T(1024)(128)(4,1)S(1)}, u32[]{:S(2)}) copy-start(pred[4096]{0:T(1024)(128)(4,1)S(1)} %compare_and_fusion.2) | copy-start | bytes 12292
  88.6 6.2 copy-start.28
  88.6 43.0 %all-to-all-start.1 = ((bf16[16,256,384]{2,1,0:T(8,128)(2,1)}), bf16[16,256,384]{2,1,0:T(8,128)(2,1)}, u32[]{:S(2)}, u32[]{:S(2)}) async-start(bf16[16,256,384]{2,1,0:T(8,128)(2,1)} %bitcast.135), calls=%async_computation.1 | async-start | bytes 6291456 | tf_op jit(solution)/shard_map/all_to_all | solution.py:30
  131.6 2.5 copy-start.14
  134.0 3.2 copy-start.4
  137.1 11.0 %copy-start.3 = (f32[4,1024,672]{1,2,0:T(8,128)}, f32[4,1024,672]{1,2,0:T(8,128)S(1)}, u32[]{:S(2)}) copy-start(f32[4,1024,672]{1,2,0:T(8,128)S(1)} %fusion.44) | copy-start | bytes 33030148
  159.0 95.1 %all-to-all-start.2 = ((bf16[4,1024,384]{2,0,1:T(4,128)(2,1)}), bf16[4,1024,384]{2,0,1:T(4,128)(2,1)}, u32[]{:S(2)}, u32[]{:S(2)}) async-start(bf16[4,1024,384]{2,0,1:T(4,128)(2,1)} %copy.69), calls=%async_computation.2 | async-start | bytes 6291456 | tf_op jit(solution)/shard_map/all_to_all | solution.py:43
  184.3 11.8 %copy-start.29 = (f32[512,4]{0,1:T(4,128)S(1)}, f32[512,4]{0,1:T(4,128)}, u32[]{:S(2)}) copy-start(f32[512,4]{0,1:T(4,128)} %param.32) | copy-start | bytes 24580
  184.3 47.2 %copy-start.2 = (bf16[512,384]{1,0:T(8,128)(2,1)S(1)}, bf16[512,384]{1,0:T(8,128)(2,1)}, u32[]{:S(2)}) copy-start(bf16[512,384]{1,0:T(8,128)(2,1)} %param.23) | copy-start | bytes 1179652
  248.5 5.6 copy-start.27
  254.1 52.9 %all-to-all-start = ((bf16[16,256,384]{2,1,0:T(8,128)(2,1)}), bf16[16,256,384]{2,1,0:T(8,128)(2,1)}, u32[]{:S(2)}, u32[]{:S(2)}) async-start(bf16[16,256,384]{2,1,0:T(8,128)(2,1)} %bitcast.133), calls=%async_computation | async-start | bytes 6291456 | tf_op jit(solution)/shard_map/all_to_all | solution.py:54
  260.1 19.3 %copy-start.19 = (pred[512,4]{1,0:T(8,128)(4,1)}, pred[512,4]{1,0:T(8,128)(4,1)S(1)}, u32[]{:S(2)}) copy-start(pred[512,4]{1,0:T(8,128)(4,1)S(1)} %compare_and_fusion.1) | copy-start | bytes 6148
  284.2 0.9 copy-start.9
  307.0 40.3 %all-to-all-start.3 = ((bf16[16,256,384]{2,1,0:T(8,128)(2,1)}), bf16[16,256,384]{2,1,0:T(8,128)(2,1)}, u32[]{:S(2)}, u32[]{:S(2)}) async-start(bf16[16,256,384]{2,1,0:T(8,128)(2,1)} %bitcast.134), calls=%async_computation.3 | async-start | bytes 6291456 | tf_op jit(solution)/shard_map/all_to_all | solution.py:30
  311.7 4.3 copy-start.17
  314.1 1.8 copy-start.6
  347.3 2.5 copy-start.12
  349.7 5.8 copy-start.5
  372.0 6.1 copy-start.13
  388.4 40.0 %all-to-all-start.4 = ((bf16[4,1024,384]{2,0,1:T(4,128)(2,1)}), bf16[4,1024,384]{2,0,1:T(4,128)(2,1)}, u32[]{:S(2)}, u32[]{:S(2)}) async-start(bf16[4,1024,384]{2,0,1:T(4,128)(2,1)} %copy.72), calls=%async_computation.4 | async-start | bytes 6291456 | tf_op jit(solution)/shard_map/all_to_all | solution.py:65
  393.0 268.7 %all-reduce.4.cloned.1.call-start = ((), (), s32[]{:S(2)}) async-start(), calls=%async_computation.20 | async-start | bytes 589824
  442.0 5.6 copy-start.18
  447.7 17.5 %copy-start.11 = (f32[512,384]{1,0:T(8,128)}, f32[512,384]{1,0:T(8,128)S(1)}, u32[]{:S(2)}) copy-start(f32[512,384]{1,0:T(8,128)S(1)} %convert_reduce_fusion.1) | copy-start | bytes 2359300
  448.1 17.1 %copy-start.26 = (pred[4096]{0:T(1024)(128)(4,1)S(1)}, pred[4096]{0:T(1024)(128)(4,1)}, u32[]{:S(2)}) copy-start(pred[4096]{0:T(1024)(128)(4,1)} %copy-done.25) | copy-start | bytes 12292
  507.8 14.6 %copy-start.16 = (bf16[4,4,256,384]{3,2,1,0:T(8,128)(2,1)}, bf16[4,4,256,384]{3,2,1,0:T(8,128)(2,1)S(1)}, u32[]{:S(2)}) copy-start(bf16[4,4,256,384]{3,2,1,0:T(8,128)(2,1)S(1)} %copy.75) | copy-start | bytes 9437188
  507.8 14.6 %copy-start.15 = (bf16[4,384,672]{1,2,0:T(8,128)(2,1)S(1)}, bf16[4,384,672]{1,2,0:T(8,128)(2,1)}, u32[]{:S(2)}) copy-start(bf16[4,384,672]{1,2,0:T(8,128)(2,1)} %param.27) | copy-start | bytes 6193156
  522.4 5.7 copy-start.31
  587.5 4.0 copy-start.20
  587.5 8.3 copy-start.22
  587.5 9.5 %copy-start.10 = (f32[512,384]{1,0:T(8,128)S(1)}, f32[512,384]{1,0:T(8,128)}, u32[]{:S(2)}) copy-start(f32[512,384]{1,0:T(8,128)} %copy-done.9) | copy-start | bytes 2359300
  595.8 15.2 %copy-start.7 = (f32[512,384]{1,0:T(8,128)}, f32[512,384]{1,0:T(8,128)S(1)}, u32[]{:S(2)}) copy-start(f32[512,384]{1,0:T(8,128)S(1)} %convert_reduce_fusion) | copy-start | bytes 2359300
  596.9 110.1 %reduce-scatter.23.cloned.1.call-start = ((), (), s32[]{:S(2)}) async-start(), calls=%async_computation.21 | async-start | bytes 313344
  599.2 139.8 %reduce-scatter.21.cloned.1.call-start = ((), (), s32[]{:S(2)}) async-start(), calls=%async_computation.19 | async-start | bytes 2949120 | tf_op jit(solution)/shard_map/reduce_scatter | solution.py:79
  611.0 159.9 %reduce-scatter.17.cloned.1.call-start = ((), (), s32[]{:S(2)}) async-start(), calls=%async_computation.17 | async-start | bytes 2949120 | tf_op jit(solution)/shard_map/reduce_scatter | solution.py:77
  618.9 184.0 %reduce-scatter.19.cloned.1.call-start = ((), (), s32[]{:S(2)}) async-start(), calls=%async_computation.18 | async-start | bytes 2949120 | tf_op jit(solution)/shard_map/reduce_scatter | solution.py:78
  627.0 207.8 %reduce-scatter.15.cloned.1.call-start = ((), (), s32[]{:S(2)}) async-start(), calls=%async_computation.16 | async-start | bytes 2949120 | tf_op jit(solution)/shard_map/reduce_scatter | solution.py:79
  634.7 232.2 %reduce-scatter.11.cloned.1.call-start = ((), (), s32[]{:S(2)}) async-start(), calls=%async_computation.14 | async-start | bytes 2949120 | tf_op jit(solution)/shard_map/reduce_scatter | solution.py:77
  642.5 8.3 copy-start.32
  642.6 9.5 %copy-start.8 = (f32[512,384]{1,0:T(8,128)S(1)}, f32[512,384]{1,0:T(8,128)}, u32[]{:S(2)}) copy-start(f32[512,384]{1,0:T(8,128)} %copy-done.7) | copy-start | bytes 2359300
  642.6 9.5 %copy-start.24 = (bf16[384,384]{1,0:T(8,128)(2,1)S(1)}, bf16[384,384]{1,0:T(8,128)(2,1)}, u32[]{:S(2)}) copy-start(bf16[384,384]{1,0:T(8,128)(2,1)} %param.24) | copy-start | bytes 884740
  642.6 256.3 %reduce-scatter.13.cloned.1.call-start = ((), (), s32[]{:S(2)}) async-start(), calls=%async_computation.15 | async-start | bytes 2949120 | tf_op jit(solution)/shard_map/reduce_scatter | solution.py:78
  642.9 256.0 %copy-start.1 = (bf16[4,384,672]{1,2,0:T(8,128)(2,1)S(1)}, bf16[4,384,672]{1,2,0:T(8,128)(2,1)}, u32[]{:S(2)}) copy-start(bf16[4,384,672]{1,2,0:T(8,128)(2,1)} %param.33) | copy-start | bytes 6193156
Sparse Core Ops, SparseCore 0:
  597.0 64.6 all-reduce.3
  666.1 40.7 reduce-scatter.22
  710.1 28.9 reduce-scatter.20
  742.0 28.9 reduce-scatter.16
  773.9 28.9 reduce-scatter.18
  805.8 28.9 reduce-scatter.14
  837.9 28.9 reduce-scatter.10
  870.0 28.9 reduce-scatter.12
where the time goes:
time: 913 us; the launch traced here: 906 us
  waiting for transfers between devices  333 us (36%)
  local copies, waits for them, and re-layouts  221 us (24%)
  matrix products  144 us (16%)
  other arithmetic  89.5 us (10%)
  blocking collectives  76.2 us (8%)
  starting transfers between devices  26.2 us (3%)
  between operations  16.1 us (2%)
    reduce_scatter x2, waiting for transfers between devices, reduce_grads(): lax.psum_scatter(grad_gate, 'dp', scatter_dimension=1, tiled=True)  64 us
    reduce_scatter x2, waiting for transfers between devices, reduce_grads(): lax.psum_scatter(grad_down, 'dp', scatter_dimension=2, tiled=True)  64 us
    reduce_scatter x2, waiting for transfers between devices, reduce_grads(): lax.psum_scatter(grad_up, 'dp', scatter_dimension=1, tiled=True)  64 us
    all_to_all x2, waiting for transfers between devices, dispatch(): recv = lax.all_to_all(send, 'ep', 0, 1, tiled=True)  63 us
    unnamed x10, waiting for transfers between devices  52.1 us
    all_to_all x1, blocking collectives, layer_backward(): lax.all_to_all(grad_send.reshape(n_exp, capacity, -1), 'ep', 0, 1, tiled=...  38.8 us
    all_to_all x1, blocking collectives, layer_backward(): grad_back = lax.all_to_all(grad_recv, 'ep', 1, 0, tiled=True)  37.4 us
    gather x2, local copies, waits for them, and re-layouts, dispatch(): jnp.take(mixed, row_tok, axis=0, mode='fill', fill_value=0)  34.1 us
  transfers between devices with their start and end apart: 13, of which 11 were waited for; matrix products, arithmetic and copies ran while one was open for 23% of the time, Pallas kernels for 0%

commit v1 on v0

v1 whole, which is shorter than its diff:
```python
import functools

import jax
import jax.numpy as jnp
from jax import lax
from jax.experimental import pallas as pl
from jax.experimental.pallas import tpu as pltpu
from jax.sharding import PartitionSpec as P

BF16 = jnp.bfloat16
F32 = jnp.float32
N_EP = 4
N_LOC = 4
TOK = 512
D = 384
FF = 672
CAP = 256
SLOTS = 5 * CAP
VMEM = pl.BlockSpec(memory_space=pltpu.VMEM)
SMEM = pl.BlockSpec(memory_space=pltpu.SMEM)


def mm(a, b, dims=((1,), (0,))):
    return lax.dot_general(a, b, (dims, ((), ())), preferred_element_type=F32)


def route_kernel(pack_ref, rank_ref, gate_ref, off_ref):
    me = lax.axis_index('ep')
    before = (lax.broadcasted_iota(jnp.int32, (TOK, TOK), 0) < lax.broadcasted_iota(jnp.int32, (TOK, TOK), 1)).astype(BF16)
    for layer in range(2):
        running = [jnp.int32(0)] * N_LOC
        last = [jnp.int32(0)] * N_LOC
        for src in range(N_EP):
            ids = pack_ref[src, 4 * layer:4 * layer + 4, :]
            gates = pack_ref[src, 8 + 4 * layer:12 + 4 * layer, :]
            member, gate = [], []
            for exp in range(N_LOC):
                match = ids == (me * N_LOC + exp).astype(F32)
                member.append(jnp.sum(match.astype(F32), axis=0, keepdims=True))
                gate.append(jnp.sum(jnp.where(match, gates, 0.0), axis=0, keepdims=True))
            member = jnp.concatenate(member, axis=0)
            gate = jnp.concatenate(gate + [jnp.zeros((4, TOK), F32)], axis=0)
            rank = mm(member.astype(BF16), before)
            rank = jnp.where(member > 0.5, rank, -1.0).astype(jnp.int32)
            rank_ref[layer, src, 0:4, :] = rank
            gate_ref[layer, src * TOK:(src + 1) * TOK, :] = jnp.transpose(gate)
            for exp in range(N_LOC):
                count = jnp.max(rank[exp:exp + 1, :]) + 1
                off_ref[layer * N_LOC + exp, src] = running[exp]
                last[exp] = running[exp] + count
                running[exp] = running[exp] + (count + 15) // 16 * 16
        for exp in range(N_LOC):
            off_ref[layer * N_LOC + exp, 4] = (last[exp] + CAP - 1) // CAP
            for pad in range(5, 8):
                off_ref[layer * N_LOC + exp, pad] = 0


def route(pack_all):
    return pl.pallas_call(
        route_kernel,
        out_shape=(jax.ShapeDtypeStruct((2, N_EP, 8, TOK), jnp.int32),
                   jax.ShapeDtypeStruct((2, N_EP * TOK, 8), F32),
                   jax.ShapeDtypeStruct((8, 8), jnp.int32)),
        in_specs=[VMEM], out_specs=(VMEM, VMEM, SMEM),
        name='route')(pack_all)


def pick(rank_ref, src, exp):
    row = rank_ref[src, pl.ds(exp, 1), :]
    return (lax.broadcasted_iota(jnp.int32, (CAP, TOK), 0) == row).astype(BF16)


def gate_column(gate_ref, src, exp):
    block = gate_ref[src * TOK:(src + 1) * TOK, :]
    lane = lax.broadcasted_iota(jnp.int32, block.shape, 1)
    return jnp.sum(jnp.where(lane == exp, block, 0.0), axis=1, keepdims=True)


def offset(off_ref, row, src):
    return pl.multiple_of(off_ref[row, src], 16)


def forward_kernel(layer, off_ref, rank_ref, gate_ref, u_ref, wg_ref, wu_ref, wd_ref, out_ref, x_scr, o_scr, acc):
    exp = pl.program_id(0)
    row = layer * N_LOC + exp

    @pl.when(exp == 0)
    def _():
        acc[...] = jnp.zeros_like(acc)

    for src in range(N_EP):
        x_scr[pl.ds(offset(off_ref, row, src), CAP), :] = mm(pick(rank_ref, src, exp), u_ref[src * TOK:(src + 1) * TOK, :]).astype(BF16)
    x_scr[pl.ds(offset(off_ref, row, 3) + CAP, CAP), :] = jnp.zeros((CAP, D), BF16)

    @pl.loop(0, off_ref[row, 4])
    def _(blk):
        rows = pl.ds(pl.multiple_of(blk * CAP, CAP), CAP)
        x_blk = x_scr[rows, :]
        a_pre = mm(x_blk, wg_ref[0])
        b_pre = mm(x_blk, wu_ref[0])
        hidden = (jax.nn.silu(a_pre) * b_pre).astype(BF16)
        o_scr[rows, :] = mm(hidden, wd_ref[0]).astype(BF16)

    o_scr[pl.ds(pl.multiple_of(off_ref[row, 4] * CAP, CAP), CAP), :] = jnp.zeros((CAP, D), BF16)

    for src in range(N_EP):
        tok_out = mm(pick(rank_ref, src, exp), o_scr[pl.ds(offset(off_ref, row, src), CAP), :], ((0,), (0,)))
        acc[src * TOK:(src + 1) * TOK, :] += gate_column(gate_ref, src, exp) * tok_out

    @pl.when(exp == N_LOC - 1)
    def _():
        out_ref[...] = acc[...].astype(BF16)


def expert_forward(layer, off, rank, gate, u_all, w_gate, w_up, w_down):
    weight = pl.BlockSpec((1, D, FF), lambda e: (e, 0, 0))
    return pl.pallas_call(
        functools.partial(forward_kernel, layer),
        grid=(N_LOC,),
        out_shape=jax.ShapeDtypeStruct((N_EP * TOK, D), BF16),
        in_specs=[SMEM, VMEM, VMEM, VMEM, weight, weight, pl.BlockSpec((1, FF, D), lambda e: (e, 0, 0))],
        out_specs=VMEM,
        scratch_shapes=[pltpu.VMEM((SLOTS, D), BF16), pltpu.VMEM((SLOTS, D), BF16), pltpu.VMEM((N_EP * TOK, D), F32)],
        compiler_params=pltpu.CompilerParams(vmem_limit_bytes=56 * 1024 * 1024),
        cost_estimate=pl.CostEstimate(flops=14_000_000_000, bytes_accessed=10_000_000, transcendentals=0),
        name='expert_forward')(off, rank, gate, u_all, w_gate, w_up, w_down)


def backward_kernel(layer, off_ref, rank_ref, gate_ref, u_ref, dy_ref, wg_ref, wu_ref, wd_ref,
                    out_ref, gg_ref, gu_ref, gd_ref, x_scr, d_scr, gx_scr, acc, gg, gu, gd):
    exp = pl.program_id(0)
    row = layer * N_LOC + exp

    @pl.when(exp == 0)
    def _():
        acc[...] = jnp.zeros_like(acc)

    for src in range(N_EP):
        sel = pick(rank_ref, src, exp)
        toks = slice(src * TOK, (src + 1) * TOK)
        rows = pl.ds(offset(off_ref, row, src), CAP)
        x_scr[rows, :] = mm(sel, u_ref[toks, :]).astype(BF16)
        scaled = (gate_column(gate_ref, src, exp) * dy_ref[toks, :].astype(F32)).astype(BF16)
        d_scr[rows, :] = mm(sel, scaled).astype(BF16)
    tail = pl.ds(offset(off_ref, row, 3) + CAP, CAP)
    x_scr[tail, :] = jnp.zeros((CAP, D), BF16)
    d_scr[tail, :] = jnp.zeros((CAP, D), BF16)
    gg[...] = jnp.zeros_like(gg)
    gu[...] = jnp.zeros_like(gu)
    gd[...] = jnp.zeros_like(gd)

    @pl.loop(0, off_ref[row, 4])
    def _(blk):
        rows = pl.ds(pl.multiple_of(blk * CAP, CAP), CAP)
        x_blk = x_scr[rows, :]
        d_blk = d_scr[rows, :]
        a_pre = mm(x_blk, wg_ref[0])
        b_pre = mm(x_blk, wu_ref[0])
        grad_h = mm(d_blk, wd_ref[0], ((1,), (1,))).astype(BF16).astype(F32)
        sigma = jax.nn.sigmoid(a_pre)
        swish = a_pre * sigma
        hidden = (swish * b_pre).astype(BF16)
        grad_a = (grad_h * b_pre * sigma * (1.0 + a_pre * (1.0 - sigma))).astype(BF16)
        grad_b = (grad_h * swish).astype(BF16)
        gx_scr[rows, :] = (mm(grad_a, wg_ref[0], ((1,), (1,))) + mm(grad_b, wu_ref[0], ((1,), (1,)))).astype(BF16)
        gg[...] += mm(x_blk, grad_a, ((0,), (0,)))
        gu[...] += mm(x_blk, grad_b, ((0,), (0,)))
        gd[...] += mm(d_blk, hidden, ((0,), (0,)))

    gx_scr[pl.ds(pl.multiple_of(off_ref[row, 4] * CAP, CAP), CAP), :] = jnp.zeros((CAP, D), BF16)
    gg_ref[0] = gg[...].astype(BF16)
    gu_ref[0] = gu[...].astype(BF16)
    gd_ref[0] = gd[...].astype(BF16)

    for src in range(N_EP):
        acc[src * TOK:(src + 1) * TOK, :] += mm(pick(rank_ref, src, exp), gx_scr[pl.ds(offset(off_ref, row, src), CAP), :], ((0,), (0,)))

    @pl.when(exp == N_LOC - 1)
    def _():
        out_ref[...] = acc[...].astype(BF16)


def expert_backward(layer, off, rank, gate, u_all, dy_all, w_gate, w_up, w_down):
    weight = pl.BlockSpec((1, D, FF), lambda e: (e, 0, 0))
    grad = jax.ShapeDtypeStruct((N_LOC, D, FF), BF16)
    return pl.pallas_call(
        functools.partial(backward_kernel, layer),
        grid=(N_LOC,),
        out_shape=(jax.ShapeDtypeStruct((N_EP * TOK, D), BF16), grad, grad, grad),
        in_specs=[SMEM, VMEM, VMEM, VMEM, VMEM, weight, weight, pl.BlockSpec((1, FF, D), lambda e: (e, 0, 0))],
        out_specs=(VMEM, weight, weight, weight),
        scratch_shapes=[pltpu.VMEM((SLOTS, D), BF16)] * 3 + [pltpu.VMEM((N_EP * TOK, D), F32)] + [pltpu.VMEM((D, FF), F32)] * 3,
        compiler_params=pltpu.CompilerParams(vmem_limit_bytes=56 * 1024 * 1024),
        cost_estimate=pl.CostEstimate(flops=40_000_000_000, bytes_accessed=20_000_000, transcendentals=0),
        name='expert_backward')(off, rank, gate, u_all, dy_all, w_gate, w_up, w_down)


def remote(src, dst, sems, slot, target):
    send, recv = sems
    return pltpu.make_async_remote_copy(src_ref=src, dst_ref=dst, send_sem=send.at[slot], recv_sem=recv.at[slot],
                                        device_id=target, device_id_type=pl.DeviceIdType.MESH)


class Place:
    def __init__(self):
        ep, dp = lax.axis_index('ep'), lax.axis_index('dp')
        self.z, self.y = ep // 2, ep % 2
        self.x, self.c = dp // 2, dp % 2
        self.me = ep
        self.y_ep = self.z * 2 + 1 - self.y
        self.z_ep = (1 - self.z) * 2 + self.y
        self.d_ep = (1 - self.z) * 2 + 1 - self.y
        self.to_y, self.to_z = {'ep': self.y_ep}, {'ep': self.z_ep}
        self.to_c, self.to_x = {'dp': self.x * 2 + 1 - self.c}, {'dp': (1 - self.x) * 2 + self.c}


def greet(targets):
    barrier = pltpu.get_barrier_semaphore()
    for target in targets:
        pl.semaphore_signal(barrier, inc=1, device_id=target, device_id_type=pl.DeviceIdType.MESH)
    pl.semaphore_wait(barrier, len(targets))


HALF = TOK // 2
TOP_ROWS, LOW_ROWS = pl.ds(0, HALF), pl.ds(HALF, HALF)


class Spread:
    def __init__(self, at, own, every, sems):
        self.direct = [remote(own.at[TOP_ROWS], every.at[at.me, TOP_ROWS], sems, 0, at.to_y),
                       remote(own.at[LOW_ROWS], every.at[at.me, LOW_ROWS], sems, 1, at.to_z),
                       remote(own.at[LOW_ROWS], every.at[at.me, LOW_ROWS], sems, 2, at.to_y),
                       remote(own.at[TOP_ROWS], every.at[at.me, TOP_ROWS], sems, 3, at.to_z)]
        self.onward = [remote(every.at[at.y_ep, TOP_ROWS], every.at[at.y_ep, TOP_ROWS], sems, 4, at.to_z),
                       remote(every.at[at.z_ep, LOW_ROWS], every.at[at.z_ep, LOW_ROWS], sems, 5, at.to_y)]

    def start(self):
        for copy in self.direct:
            copy.start()

    def forward(self):
        for first, then in zip(self.direct, self.onward):
            first.wait_recv()
            then.start()

    def finish(self):
        for copy in self.direct[2:] + self.onward:
            copy.wait_recv()
        for copy in self.direct + self.onward:
            copy.wait_send()


class Collect:
    def __init__(self, at, part, got, mix_scr, sems):
        self.at, self.part, self.got, self.mix_scr = at, part, got, mix_scr
        self.direct = [remote(part.at[at.d_ep, TOP_ROWS], got.at[0], sems, 0, at.to_y),
                       remote(part.at[at.d_ep, LOW_ROWS], got.at[1], sems, 1, at.to_z),
                       remote(part.at[at.y_ep, TOP_ROWS], got.at[2], sems, 2, at.to_y),
                       remote(part.at[at.z_ep, LOW_ROWS], got.at[3], sems, 3, at.to_z)]
        self.summed = [remote(mix_scr.at[0], got.at[4], sems, 4, at.to_z),
                       remote(mix_scr.at[1], got.at[5], sems, 5, at.to_y)]

    def start(self):
        for copy in self.direct:
            copy.start()

    def forward(self):
        at = self.at
        for step, (ep, rows) in enumerate(((at.z_ep, TOP_ROWS), (at.y_ep, LOW_ROWS))):
            self.direct[step].wait_recv()
            self.mix_scr[step] = (self.part[ep, rows].astype(F32) + self.got[step].astype(F32)).astype(BF16)
            self.summed[step].start()

    def finish(self, base):
        for copy in self.direct[2:] + self.summed:
            copy.wait_recv()
        me, got = self.at.me, self.got
        top = self.part[me, TOP_ROWS].astype(F32) + got[2].astype(F32) + got[4].astype(F32)
        low = self.part[me, LOW_ROWS].astype(F32) + got[3].astype(F32) + got[5].astype(F32)
        return (base[TOP_ROWS].astype(F32) + top).astype(BF16), (base[LOW_ROWS].astype(F32) + low).astype(BF16)

    def drain(self):
        for copy in self.direct + self.summed:
            copy.wait_send()


N_GRAD = 3 * N_LOC
ROWS_DP = D // 4


class Reduce:
    def __init__(self, at, grads, outs, got_c, own, got_x, pair_sems, own_sem, x_sems):
        self.at, self.outs, self.got_c, self.own, self.got_x = at, outs, got_c, own, got_x
        self.pair, self.load, self.along = [], [], []
        for k in range(N_GRAD):
            grad = grads[k % 3].at[k // 3]
            self.pair.append(remote(grad.at[:, 1 - at.c], got_c.at[k], pair_sems, k, at.to_c))
            self.load.append(pltpu.make_async_copy(grad.at[:, at.c], own.at[k], own_sem.at[k]))
            self.along.append(remote(got_c.at[k, 1 - at.x], got_x.at[k], x_sems, k, at.to_x))

    def start(self):
        for pair, load in zip(self.pair, self.load):
            pair.start()
            load.start()

    def forward(self, ks):
        for k in ks:
            self.pair[k].wait_recv()
            self.load[k].wait()
            for side in range(2):
                self.got_c[k, side] = (self.got_c[k, side].astype(F32) + self.own[k, side].astype(F32)).astype(BF16)
            self.along[k].start()

    def finish(self):
        x = self.at.x
        for k in range(N_GRAD):
            self.along[k].wait_recv()
            self.outs[k % 3][k // 3] = (self.got_c[k, x].astype(F32) + self.got_x[k].astype(F32)).astype(BF16)
        for k in range(N_GRAD):
            self.pair[k].wait_send()
            self.along[k].wait_send()


REDUCE_SCRATCH = [pltpu.VMEM((N_GRAD, 2, ROWS_DP, FF), BF16), pltpu.VMEM((N_GRAD, 2, ROWS_DP, FF), BF16),
                  pltpu.VMEM((N_GRAD, ROWS_DP, FF), BF16)] + [pltpu.SemaphoreType.DMA((N_GRAD,))] * 5
COLLECT_SCRATCH = [pltpu.VMEM((6, HALF, D), BF16), pltpu.VMEM((2, HALF, D), BF16)] + [pltpu.SemaphoreType.DMA((6,))] * 2
SPREAD_SEMS = [pltpu.SemaphoreType.DMA((6,))] * 2
ANY = pl.BlockSpec(memory_space=pl.ANY)


def call(kernel, name, ident, ins, in_specs, outs, scratch):
    return pl.pallas_call(
        kernel, out_shape=outs, in_specs=in_specs, out_specs=jax.tree.map(lambda _: VMEM, outs), scratch_shapes=scratch,
        compiler_params=pltpu.CompilerParams(collective_id=ident, has_side_effects=True, vmem_limit_bytes=48 * 1024 * 1024),
        name=name)(*ins)


def block(*shape, dtype=BF16):
    return jax.ShapeDtypeStruct(shape, dtype)


def entry_kernel(u_ref, pack_ref, every, packs, s_send, s_recv, p_send, p_recv):
    at = Place()
    greet([at.to_y, at.to_z])
    small = [remote(pack_ref, packs.at[at.me], (p_send, p_recv), 0, at.to_y),
             remote(pack_ref, packs.at[at.me], (p_send, p_recv), 1, at.to_z),
             remote(packs.at[at.y_ep], packs.at[at.y_ep], (p_send, p_recv), 2, at.to_z)]
    small[0].start()
    small[1].start()
    spread = Spread(at, u_ref, every, (s_send, s_recv))
    spread.start()
    every[at.me] = u_ref[...]
    packs[at.me] = pack_ref[...]
    small[0].wait_recv()
    small[2].start()
    spread.forward()
    small[1].wait_recv()
    small[2].wait_recv()
    spread.finish()
    for copy in small:
        copy.wait_send()


def middle_kernel(part, u_ref, dense_ref, mid_ref, every, got, mix_scr, c_send, c_recv, u_scr, s_send, s_recv):
    at = Place()
    greet([at.to_y, at.to_z])
    collect = Collect(at, part, got, mix_scr, (c_send, c_recv))
    collect.start()
    collect.forward()
    top, low = collect.finish(u_ref)
    mid_ref[TOP_ROWS] = top
    mid_ref[LOW_ROWS] = low
    u_scr[TOP_ROWS] = (top.astype(F32) + mm(top, dense_ref[...])).astype(BF16)
    u_scr[LOW_ROWS] = (low.astype(F32) + mm(low, dense_ref[...])).astype(BF16)
    spread = Spread(at, u_scr, every, (s_send, s_recv))
    spread.start()
    every[at.me] = u_scr[...]
    collect.drain()
    spread.forward()
    spread.finish()


def dense_grad(x_ref, top, low):
    return mm(x_ref[TOP_ROWS], top, ((0,), (0,))) + mm(x_ref[LOW_ROWS], low, ((0,), (0,)))


def write_slabs(slabs, value):
    for k in range(16):
        slabs[k // 8, k // 4 % 2, k // 2 % 2, k % 2] = value[24 * k:24 * k + 24].astype(BF16)


def turn_kernel(part, dy_ref, dense_ref, mid_ref, ga, gb, gc, grad_ref, every, slabs, oa, ob, oc,
                got, mix_scr, c_send, c_recv, s_send, s_recv, got_c, own, got_x, pair_send, pair_recv, own_sem, x_send, x_recv, g_scr):
    at = Place()
    greet([at.to_y, at.to_z, at.to_c, at.to_x])
    collect = Collect(at, part, got, mix_scr, (c_send, c_recv))
    collect.start()
    reduce = Reduce(at, (ga, gb, gc), (oa, ob, oc), got_c, own, got_x, (pair_send, pair_recv), own_sem, (x_send, x_recv))
    reduce.start()
    reduce.forward(range(6))
    collect.forward()
    reduce.forward(range(6, N_GRAD))
    top, low = collect.finish(dy_ref)
    for rows, half in ((TOP_ROWS, top), (LOW_ROWS, low)):
        g_scr[rows] = (half.astype(F32) + mm(half, dense_ref[...], ((1,), (1,)))).astype(BF16)
    spread = Spread(at, g_scr, every, (s_send, s_recv))
    spread.start()
    grad_ref[...] = g_scr[...]
    every[at.me] = g_scr[...]
    write_slabs(slabs, dense_grad(mid_ref, top, low))
    collect.drain()
    spread.forward()
    spread.finish()
    reduce.finish()


def exit_kernel(part, dy_ref, dense_ref, tok_ref, slabs_two, ga, gb, gc, dx_ref, dense_out, oa, ob, oc,
                got, mix_scr, c_send, c_recv, got_c, own, got_x, pair_send, pair_recv, own_sem, x_send, x_recv,
                slab_c, slab_z, slab_y, slab_x, sum_c, sum_z, sum_y, s_send, s_recv, slabs_one):
    at = Place()
    greet([at.to_y, at.to_z, at.to_c, at.to_x])
    collect = Collect(at, part, got, mix_scr, (c_send, c_recv))
    collect.start()
    reduce = Reduce(at, (ga, gb, gc), (oa, ob, oc), got_c, own, got_x, (pair_send, pair_recv), own_sem, (x_send, x_recv))
    reduce.start()
    reduce.forward(range(6))
    collect.forward()
    reduce.forward(range(6, N_GRAD))
    top, low = collect.finish(dy_ref)
    write_slabs(slabs_one, dense_grad(tok_ref, top, low))
    sems = (s_send, s_recv)
    to_c = [remote(slabs.at[:, 1 - at.c], slab_c.at[k], sems, k, at.to_c) for k, slabs in enumerate((slabs_one, slabs_two))]
    for copy in to_c:
        copy.start()
    for rows, half in ((TOP_ROWS, top), (LOW_ROWS, low)):
        dx_ref[rows] = (half.astype(F32) + mm(half, dense_ref[...], ((1,), (1,)))).astype(BF16)
    for k, slabs in enumerate((slabs_one, slabs_two)):
        to_c[k].wait_recv()
        for side in range(2):
            sum_c[k, side] = (slabs[side, at.c].astype(F32) + slab_c[k, side].astype(F32)).astype(BF16)
    to_z = remote(sum_c.at[:, :, 1 - at.z], slab_z, sems, 2, at.to_z)
    to_z.start()
    to_z.wait_recv()
    for k in range(2):
        for side in range(2):
            sum_z[k, side] = (sum_c[k, side, at.z].astype(F32) + slab_z[k, side].astype(F32)).astype(BF16)
    to_y = remote(sum_z.at[:, :, 1 - at.y], slab_y, sems, 3, at.to_y)
    to_y.start()
    to_y.wait_recv()
    for k in range(2):
        for side in range(2):
            sum_y[side, k] = (sum_z[k, side, at.y].astype(F32) + slab_y[k, side].astype(F32)).astype(BF16)
    to_x = remote(sum_y.at[1 - at.x], slab_x, sems, 4, at.to_x)
    to_x.start()
    reduce.finish()
    to_x.wait_recv()
    dense_out[...] = (sum_y[at.x].astype(F32) + slab_x[...].astype(F32)).astype(BF16)
    collect.drain()
    for copy in to_c + [to_z, to_y, to_x]:
        copy.wait_send()


def by_owner(grad):
    return grad.reshape(N_LOC, 2, 2, ROWS_DP, FF)


REDUCED = (block(N_LOC, ROWS_DP, FF),) * 3


def mix(x_loc, dense_w):
    return (x_loc.astype(F32) + jnp.dot(x_loc, dense_w, preferred_element_type=F32)).astype(BF16)


def rows_of(every):
    return every.reshape(N_EP * TOK, D)


def per_source(part):
    return part.reshape(N_EP, TOK, D)


def solution(mesh):
    tok_spec = P(('dp', 'ep'), None)
    exp_spec = P('ep', None, None)
    layer_specs = (P(None, None), tok_spec, tok_spec, exp_spec, exp_spec, exp_spec)
    grad_specs = (P(('dp', 'ep'), None), P('ep', 'dp', None), P('ep', 'dp', None), P('ep', None, 'dp'))

    def local_step(tokens, dy_out, dense_w1, route_idx1, route_gate1, w_gate1, w_up1, w_down1, dense_w2, route_idx2, route_gate2, w_gate2, w_up2, w_down2):
        pack = jnp.concatenate([route_idx1.T.astype(F32), route_idx2.T.astype(F32), route_gate1.T, route_gate2.T], axis=0)
        mixed_one = mix(tokens, dense_w1)
        u_one, packs = call(entry_kernel, 'entry', 0, (mixed_one, pack), [VMEM, VMEM],
                            (block(N_EP, TOK, D), block(N_EP, 16, TOK, dtype=F32)),
                            SPREAD_SEMS + [pltpu.SemaphoreType.DMA((3,))] * 2)
        rank, gate, off = route(packs)
        dy_later, off = lax.optimization_barrier((dy_out, off))
        dy_all = lax.all_gather(dy_later, 'ep', axis=0, tiled=True)
        part = expert_forward(0, off, rank[0], gate[0], rows_of(u_one), w_gate1, w_up1, w_down1)
        mid_tok, u_two = call(middle_kernel, 'middle', 1, (per_source(part), mixed_one, dense_w2), [VMEM] * 3,
                              (block(TOK, D), block(N_EP, TOK, D)),
                              COLLECT_SCRATCH + [pltpu.VMEM((TOK, D), BF16)] + SPREAD_SEMS)
        part, *grads = expert_backward(1, off, rank[1], gate[1], rows_of(u_two), dy_all, w_gate2, w_up2, w_down2)
        grad_mid, dy_mid, slabs, *reduced_two = call(
            turn_kernel, 'turn', 2, (per_source(part), dy_out, dense_w2, mid_tok) + tuple(map(by_owner, grads)), [VMEM] * 4 + [ANY] * 3,
            (block(TOK, D), block(N_EP, TOK, D), block(2, 2, 2, 2, 24, D)) + REDUCED,
            COLLECT_SCRATCH + SPREAD_SEMS + REDUCE_SCRATCH + [pltpu.VMEM((TOK, D), BF16)])
        part, *grads = expert_backward(0, off, rank[0], gate[0], rows_of(u_one), rows_of(dy_mid), w_gate1, w_up1, w_down1)
        slab = lambda *lead: pltpu.VMEM(lead + (24, D), BF16)
        grad_tok, dense, *reduced_one = call(
            exit_kernel, 'exit', 3, (per_source(part), grad_mid, dense_w1, tokens, slabs) + tuple(map(by_owner, grads)), [VMEM] * 5 + [ANY] * 3,
            (block(TOK, D), block(2, 24, D)) + REDUCED,
            COLLECT_SCRATCH + REDUCE_SCRATCH
            + [slab(2, 2, 2, 2), slab(2, 2, 2), slab(2, 2), slab(2), slab(2, 2, 2, 2), slab(2, 2, 2), slab(2, 2)]
            + [pltpu.SemaphoreType.DMA((5,))] * 2 + [slab(2, 2, 2, 2)])

        def grads_of(k, reduced):
            return (dense[k], reduced[0], reduced[1], jnp.swapaxes(reduced[2], 1, 2))

        return (grad_tok,) + grads_of(0, reduced_one) + grads_of(1, reduced_two)

    return jax.shard_map(local_step, mesh=mesh, in_specs=(tok_spec, tok_spec) + layer_specs + layer_specs,
                         out_specs=(tok_spec,) + grad_specs + grad_specs, check_vma=False)
```

time: 913 us -> 277 us (0.30)
  waiting for transfers between devices: 333 us -> 0.02 us
  Pallas kernels: 0 us -> 231 us
  local copies, waits for them, and re-layouts: 221 us -> 29.2 us
  matrix products: 144 us -> 1.64 us
  other arithmetic: 89.5 us -> 1.59 us
  blocking collectives: 76.2 us -> 0 us
  starting transfers between devices: 26.2 us -> 0.04 us
    pallas_call x0 -> x8, Pallas kernels: none -> 231 us  [the longest x4 143 us: call(): pl.pallas_call(kernel, out_shape=outs, in_specs=in_specs, out_specs=jax.t...]
    reduce_scatter x6 -> x0, waiting for transfers between devices: 192 us -> none  [the longest x2 64 us: reduce_grads(): lax.psum_scatter(grad_gate, 'dp', scatter_dimension=1, tiled=True)]
    dot_general x23 -> x1, matrix products: 144 us -> 1.64 us  [mix(): jnp.dot(x_loc, dense_w, preferred_element_type=F32)]
    gather x14 -> x0, local copies, waits for them, and re-layouts: 134 us -> none  [the longest x2 34.1 us: dispatch(): jnp.take(mixed, row_tok, axis=0, mode='fill', fill_value=0)]
    all_to_all x5 -> x0, waiting for transfers between devices: 89.4 us -> none  [the longest x2 63 us: dispatch(): recv = lax.all_to_all(send, 'ep', 0, 1, tiled=True)]
    all_to_all x2 -> x0, blocking collectives: 76.2 us -> none  [the longest x1 38.8 us: layer_backward(): lax.all_to_all(grad_send.reshape(n_exp, capacity, -1), 'ep', 0, 1, tiled=...]
    unnamed x10 -> x1, waiting for transfers between devices: 52.1 us -> 0.02 us
    scatter x6 -> x0, local copies, waits for them, and re-layouts: 48.5 us -> none  [the longest x4 32.4 us: row_fill(): jnp.full((n_rows,), empty, values.dtype).at[flat_pos.reshape(-1)]]
  transfers between devices with their start and end apart: 13 -> 1, of which waited for: 11 -> 0; matrix products, arithmetic and copies ran while one was open for 23% -> 6% of each run, Pallas kernels for 0% -> 17%
where the time goes in v1:
time: 277 us
  Pallas kernels  231 us (83%)
  local copies, waits for them, and re-layouts  29.2 us (11%)
  between operations  14.2 us (5%)
    pallas_call x4, Pallas kernels, call(): pl.pallas_call(kernel, out_shape=outs, in_specs=in_specs, out_specs=jax.t...  143 us
    pallas_call x2, Pallas kernels, expert_backward(): pl.pallas_call(functools.partial(backward_kernel, layer), grid=(N_LOC,),...  67.5 us
    unnamed x39, local copies, waits for them, and re-layouts  26.4 us
    pallas_call x1, Pallas kernels, expert_forward(): pl.pallas_call(functools.partial(forward_kernel, layer), grid=(N_LOC,), o...  17.4 us
  transfers between devices with their start and end apart: 1, of which 0 were waited for; matrix products, arithmetic and copies ran while one was open for 6% of the time, Pallas kernels for 17%

profile of v1, /device:TPU:0, one launch (start us, length us, event | category | flops | bytes accessed | tf_op | source)
XLA Modules:
  0.0 277.5 jit_solution(13406843858719924097)
XLA Ops:
  7.2 0.0 copy-start.11
  7.2 0.0 all-gather.2.cloned.1.call-start
  7.2 0.9 convert_bitcast_fusion
  8.1 1.6 fusion.u_ref
  9.7 0.7 pad_maximum_fusion.pack_ref
  10.5 19.5 %entry.1 = (bf16[4,512,384]{2,1,0:T(8,128)(2,1)S(1)}, f32[4,16,512]{2,1,0:T(8,128)S(1)}) custom-call(bf16[512,384]{1,0:T(8,128)(2,1)S(1)} %fusion.u_ref, f32[16,512]{1,0:T(8,128)S(1)} %pad_maximum_fusion.pack_ref), custom_call_target="tpu_custom_call" | custom-call | tf_op jit(solution)/shard_map/entry/pallas_call | solution.py:332
  30.0 0.0 copy-start.6
  30.0 0.6 copy-done.6
  30.6 0.0 copy-start.7
  30.6 1.2 copy-done.7
  31.8 3.3 %route.1 = (s32[2,4,8,512]{3,2,1,0:T(8,128)}, f32[2,2048,8]{2,1,0:T(8,128)}, s32[8,8]{1,0:T(8,128)}) custom-call(f32[4,16,512]{2,1,0:T(8,128)} %copy-done.6), custom_call_target="tpu_custom_call" | custom-call | tf_op jit(solution)/shard_map/route/pallas_call | solution.py:59
  35.1 0.0 all-gather.2.cloned.1.call-update
  35.1 0.0 copy-done.11
  35.1 2.6 copy.23.wg_ref
  37.7 0.0 copy-start.12
  37.7 4.3 %copy.24.wu_ref = bf16[4,384,672]{2,1,0:T(8,128)(2,1)} copy(bf16[4,384,672]{1,2,0:T(8,128)(2,1)} %param.20) | data formatting | bytes 4128768 | tf_op args[6]
  42.0 0.0 copy-done.12
  42.0 2.6 copy.25.wg_ref
  44.6 0.0 copy-start.13
  44.6 0.0 copy-start.10
  44.6 4.3 %copy.26.wu_ref = bf16[4,384,672]{2,1,0:T(8,128)(2,1)} copy(bf16[4,384,672]{1,2,0:T(8,128)(2,1)} %param.26) | data formatting | bytes 4128768 | tf_op args[12]
  48.9 0.0 copy-done.13
  48.9 0.7 slice_bitcast_fusion.2
  49.6 0.0 copy-done.10
  49.6 1.5 slice_bitcast_fusion
  51.1 0.0 copy-start.3
  51.1 17.4 %expert_forward.1 = bf16[2048,384]{1,0:T(8,128)(2,1)} custom-call(s32[8,8]{1,0:T(8,128)} %get-tuple-element.39.off_ref, s32[4,8,512]{2,1,0:T(8,128)} %get-tuple-element.68.rank_ref, f32[2048,8]{1,0:T(8,128)} %get-tuple-element.66.gate_ref, bf16[2048,384]{1,0:T(8,128)(2,1)} %bitcast.38, bf16[4,384,672]{2,1,0:T(8,128)(2,1)} %copy.23.wg_ref, ...), custom_call_target="tpu_custom_call" | custom-call | flops 14000000000 | bytes 10000000 | tf_op jit(solution)/shard_map/expert_forward/pallas_call | solution.py:117
  68.5 0.0 copy-done.3
  68.5 0.0 copy-start.2
  68.5 1.4 copy-done.2
  69.9 30.9 %middle.1 = (bf16[512,384]{1,0:T(8,128)(2,1)S(1)}, bf16[4,512,384]{2,1,0:T(8,128)(2,1)S(1)}) custom-call(bf16[4,512,384]{2,1,0:T(8,128)(2,1)S(1)} %bitcast.35, bf16[512,384]{1,0:T(8,128)(2,1)S(1)} %fusion.u_ref, bf16[384,384]{1,0:T(8,128)(2,1)S(1)} %copy-done.3), custom_call_target="tpu_custom_call" | custom-call | tf_op jit(solution)/shard_map/middle/pallas_call | solution.py:332
  100.8 0.0 copy-start.9
  100.8 1.1 copy-done.9
  101.9 0.0 all-gather.2.cloned.1.call-done.dy_ref
  101.9 0.0 copy-start
  101.9 36.3 %expert_backward.2 = (bf16[2048,384]{1,0:T(8,128)(2,1)}, bf16[4,384,672]{2,1,0:T(8,128)(2,1)}, bf16[4,384,672]{2,1,0:T(8,128)(2,1)}, bf16[4,384,672]{2,1,0:T(8,128)(2,1)}) custom-call(s32[8,8]{1,0:T(8,128)} %get-tuple-element.39.off_ref, s32[4,8,512]{2,1,0:T(8,128)} %get-tuple-element.67.rank_ref, f32[2048,8]{1,0:T(8,128)} %get-tuple-element.65.gate_ref, ...), custom_call_target="tpu_custom_call" | custom-call | flops 40000000000 | bytes 20000000 | tf_op jit(solution)/shard_map/expert_backward/pallas_call | solution.py:186
  138.3 0.0 copy-done
  138.3 44.7 %turn.1 = (bf16[512,384]{1,0:T(8,128)(2,1)S(1)}, bf16[4,512,384]{2,1,0:T(8,128)(2,1)S(1)}, bf16[2,2,2,2,24,384]{5,4,3,2,1,0:T(8,128)(2,1)S(1)}, bf16[4,96,672]{2...) custom-call(bf16[4,512,384]{2,1,0:T(8,128)(2,1)} %bitcast.48, ...), custom_call_target="tpu_custom_call" | custom-call | tf_op jit(solution)/shard_map/turn/pallas_call | solution.py:332
  183.0 0.0 copy-start.8
  183.0 1.2 copy-done.8
  184.2 0.0 copy-start.4
  184.2 0.0 copy-start.5
  184.2 31.1 %expert_backward.3 = (bf16[2048,384]{1,0:T(8,128)(2,1)}, bf16[4,384,672]{2,1,0:T(8,128)(2,1)}, bf16[4,384,672]{2,1,0:T(8,128)(2,1)}, bf16[4,384,672]{2,1,0:T(8,128)(2,1)}) custom-call(s32[8,8]{1,0:T(8,128)} %get-tuple-element.39.off_ref, s32[4,8,512]{2,1,0:T(8,128)} %get-tuple-element.68.rank_ref, f32[2048,8]{1,0:T(8,128)} %get-tuple-element.66.gate_ref, ...), custom_call_target="tpu_custom_call" | custom-call | flops 40000000000 | bytes 20000000 | tf_op jit(solution)/shard_map/expert_backward/pallas_call | solution.py:186
  215.4 0.0 copy-done.4
  215.4 0.0 copy-done.5
  215.4 0.0 copy-start.1
  215.4 1.4 copy-done.1
  216.8 47.6 %exit.1 = (bf16[512,384]{1,0:T(8,128)(2,1)S(1)}, bf16[2,24,384]{2,1,0:T(8,128)(2,1)S(1)}, bf16[4,96,672]{2,1,0:T(8,128)(2,1)S(1)}, bf16[4,96,672]{2,1,0:T(8,128)(2,1)S(1)}, bf16[4,96,672]{2,1,0:T(8,128)(2,1)S(1)}) custom-call(bf16[4,512,384]{2,1,0:T(8,128)(2,1)S(1)} %bitcast.34, bf16[512,384]{1,0:T(8,128)(2,1)S(1)} %get-tuple-element.52.dy_ref, ...), custom_call_target="tpu_custom_call" | custom-call | tf_op jit(solution)/shard_map/exit/pallas_call | solution.py:332
  264.4 0.6 slice_bitcast_fusion.4
  265.0 0.7 copy.36
  265.7 0.8 copy.37
  266.5 0.8 copy.38
  267.4 0.8 copy.39
  268.2 0.8 copy.40
  269.0 0.8 copy.41
  269.8 0.8 copy.42
Async XLA Ops:
  7.2 27.9 %copy-start.11 = (bf16[4,384,672]{1,2,0:T(8,128)(2,1)S(1)}, bf16[4,384,672]{1,2,0:T(8,128)(2,1)}, u32[]{:S(2)}) copy-start(bf16[4,384,672]{1,2,0:T(8,128)(2,1)} %param.19) | copy-start | bytes 6193156
  7.2 94.8 %all-gather.2.cloned.1.call-start = ((), (), s32[]{:S(2)}) async-start(), calls=%async_computation | async-start | bytes 1966080 | tf_op jit(solution)/shard_map/all_gather | solution.py:496
  30.0 0.7 copy-start.6
  30.6 1.2 copy-start.7
  37.7 4.3 %copy-start.12 = (bf16[4,384,672]{1,2,0:T(8,128)(2,1)S(1)}, bf16[4,384,672]{1,2,0:T(8,128)(2,1)}, u32[]{:S(2)}) copy-start(bf16[4,384,672]{1,2,0:T(8,128)(2,1)} %param.25) | copy-start | bytes 6193156
  44.6 4.3 %copy-start.13 = (s32[2,4,8,512]{3,2,1,0:T(8,128)S(1)}, s32[2,4,8,512]{3,2,1,0:T(8,128)}, u32[]{:S(2)}) copy-start(s32[2,4,8,512]{3,2,1,0:T(8,128)} %get-tuple-element.40) | copy-start | bytes 393220
  44.6 5.0 %copy-start.10 = (f32[2,2048,8]{2,1,0:T(8,128)S(1)}, f32[2,2048,8]{2,1,0:T(8,128)}, u32[]{:S(2)}) copy-start(f32[2,2048,8]{2,1,0:T(8,128)} %get-tuple-element.41) | copy-start | bytes 393220
  51.1 17.4 %copy-start.3 = (bf16[384,384]{1,0:T(8,128)(2,1)S(1)}, bf16[384,384]{1,0:T(8,128)(2,1)}, u32[]{:S(2)}) copy-start(bf16[384,384]{1,0:T(8,128)(2,1)} %dense_ref.4) | copy-start | bytes 884740
  68.5 1.4 copy-start.2
  100.8 1.2 copy-start.9
  101.9 36.3 %copy-start = (bf16[512,384]{1,0:T(8,128)(2,1)S(1)}, bf16[512,384]{1,0:T(8,128)(2,1)}, u32[]{:S(2)}) copy-start(bf16[512,384]{1,0:T(8,128)(2,1)} %dy_ref.1) | copy-start | bytes 1179652
  183.0 1.2 copy-start.8
  184.2 31.2 %copy-start.4 = (bf16[512,384]{1,0:T(8,128)(2,1)S(1)}, bf16[512,384]{1,0:T(8,128)(2,1)}, u32[]{:S(2)}) copy-start(bf16[512,384]{1,0:T(8,128)(2,1)} %tok_ref.1) | copy-start | bytes 1179652
  184.2 31.2 %copy-start.5 = (bf16[384,384]{1,0:T(8,128)(2,1)S(1)}, bf16[384,384]{1,0:T(8,128)(2,1)}, u32[]{:S(2)}) copy-start(bf16[384,384]{1,0:T(8,128)(2,1)} %dense_ref.5) | copy-start | bytes 884740
  215.4 1.4 copy-start.1
Sparse Core Ops, SparseCore 0:
  35.2 26.8 all-gather.1

commit v2 on v1

v2 whole, which is shorter than its diff:
```python
import functools

import jax
import jax.numpy as jnp
from jax import lax
from jax.experimental import pallas as pl
from jax.experimental.pallas import tpu as pltpu
from jax.sharding import PartitionSpec as P

BF16 = jnp.bfloat16
F32 = jnp.float32
N_EP = 4
N_LOC = 4
TOK = 512
D = 384
FF = 672
CAP = 256
SLOTS = 5 * CAP
ROWS_DP = D // 4
VMEM = pl.BlockSpec(memory_space=pltpu.VMEM)
SMEM = pl.BlockSpec(memory_space=pltpu.SMEM)


def block(*shape, dtype=BF16):
    return jax.ShapeDtypeStruct(shape, dtype)


def mm(a, b, dims=((1,), (0,))):
    return lax.dot_general(a, b, (dims, ((), ())), preferred_element_type=F32)


NT = ((1,), (1,))
TN = ((0,), (0,))


def route_into(packs, rank_ref, gate_ref, off_ref, me):
    before = (lax.broadcasted_iota(jnp.int32, (TOK, TOK), 0) < lax.broadcasted_iota(jnp.int32, (TOK, TOK), 1)).astype(BF16)
    for layer in range(2):
        running = [jnp.int32(0)] * N_LOC
        last = [jnp.int32(0)] * N_LOC
        for src in range(N_EP):
            ids = packs[src, 4 * layer:4 * layer + 4, :]
            gates = packs[src, 8 + 4 * layer:12 + 4 * layer, :]
            member, gate = [], []
            for exp in range(N_LOC):
                match = ids == (me * N_LOC + exp).astype(F32)
                member.append(jnp.sum(match.astype(F32), axis=0, keepdims=True))
                gate.append(jnp.sum(jnp.where(match, gates, 0.0), axis=0, keepdims=True))
            member = jnp.concatenate(member, axis=0)
            gate = jnp.concatenate(gate + [jnp.zeros((4, TOK), F32)], axis=0)
            rank = mm(member.astype(BF16), before)
            rank = jnp.where(member > 0.5, rank, -1.0).astype(jnp.int32)
            rank_ref[layer, src, 0:4, :] = rank
            gate_ref[layer, src] = jnp.transpose(gate)
            for exp in range(N_LOC):
                count = jnp.max(rank[exp:exp + 1, :]) + 1
                off_ref[layer * N_LOC + exp, src] = running[exp]
                last[exp] = running[exp] + count
                running[exp] = running[exp] + (count + 15) // 16 * 16
        for exp in range(N_LOC):
            off_ref[layer * N_LOC + exp, 4] = (last[exp] + CAP - 1) // CAP
            for pad in range(5, 8):
                off_ref[layer * N_LOC + exp, pad] = 0


def pick(layer, rank_ref, src, exp):
    row = rank_ref[layer, src, pl.ds(exp, 1), :]
    return (lax.broadcasted_iota(jnp.int32, (CAP, TOK), 0) == row).astype(BF16)


def gate_column(layer, gate_ref, src, exp):
    slab = gate_ref[layer, src]
    lane = lax.broadcasted_iota(jnp.int32, slab.shape, 1)
    return jnp.sum(jnp.where(lane == exp, slab, 0.0), axis=1, keepdims=True)


def offset(off_ref, row, src):
    return pl.multiple_of(off_ref[row, src], 16)


def forward_kernel(layer, off_ref, rank_ref, gate_ref, u_ref, wg_ref, wu_ref, wd_ref, out_ref, x_scr, o_scr, acc):
    acc[...] = jnp.zeros_like(acc)

    @pl.loop(0, N_LOC)
    def _(exp):
        row = layer * N_LOC + exp
        for src in range(N_EP):
            x_scr[pl.ds(offset(off_ref, row, src), CAP), :] = mm(pick(layer, rank_ref, src, exp), u_ref[src]).astype(BF16)
        x_scr[pl.ds(offset(off_ref, row, 3) + CAP, CAP), :] = jnp.zeros((CAP, D), BF16)

        @pl.loop(0, off_ref[row, 4])
        def _(blk):
            rows = pl.ds(pl.multiple_of(blk * CAP, CAP), CAP)
            x_blk = x_scr[rows, :]
            a_pre = mm(x_blk, wg_ref[exp], NT)
            b_pre = mm(x_blk, wu_ref[exp], NT)
            hidden = (jax.nn.silu(a_pre) * b_pre).astype(BF16)
            o_scr[rows, :] = mm(hidden, wd_ref[exp]).astype(BF16)

        o_scr[pl.ds(pl.multiple_of(off_ref[row, 4] * CAP, CAP), CAP), :] = jnp.zeros((CAP, D), BF16)
        for src in range(N_EP):
            tok_out = mm(pick(layer, rank_ref, src, exp), o_scr[pl.ds(offset(off_ref, row, src), CAP), :], TN)
            acc[src] += gate_column(layer, gate_ref, src, exp) * tok_out

    out_ref[...] = acc[...].astype(BF16)


def plain(kernel, name, ins, outs, scratch, flops):
    return pl.pallas_call(
        kernel, out_shape=outs, in_specs=[SMEM] + [VMEM] * (len(ins) - 1), out_specs=jax.tree.map(lambda _: VMEM, outs),
        scratch_shapes=scratch, compiler_params=pltpu.CompilerParams(vmem_limit_bytes=24 * 1024 * 1024),
        cost_estimate=pl.CostEstimate(flops=flops, bytes_accessed=10_000_000, transcendentals=0), name=name)(*ins)


def expert_forward(layer, routes, u_all, weights):
    return plain(functools.partial(forward_kernel, layer), 'expert_forward', routes + (u_all,) + weights, block(N_EP, TOK, D),
                 [pltpu.VMEM((SLOTS, D), BF16)] * 2 + [pltpu.VMEM((N_EP, TOK, D), F32)], 14_000_000_000)


def backward_kernel(layer, first, count, n_dy, carried, off_ref, rank_ref, gate_ref, u_ref, *refs):
    dy_refs, refs = refs[:n_dy], refs[n_dy:]
    before, refs = refs[:carried], refs[carried:]
    wg_ref, wu_ref, wd_ref, out_ref, gg_ref, gu_ref, gd_ref, x_scr, d_scr, gx_scr, acc, gg, gu, gd = refs
    acc[...] = before[0][...] if carried else jnp.zeros_like(acc)

    @pl.loop(first, first + count)
    def _(exp):
        row = layer * N_LOC + exp
        for src in range(N_EP):
            sel = pick(layer, rank_ref, src, exp)
            rows = pl.ds(offset(off_ref, row, src), CAP)
            x_scr[rows, :] = mm(sel, u_ref[src]).astype(BF16)
            dy = dy_refs[src][...] if n_dy > 1 else dy_refs[0][src]
            scaled = (gate_column(layer, gate_ref, src, exp) * dy.astype(F32)).astype(BF16)
            d_scr[rows, :] = mm(sel, scaled).astype(BF16)
        tail = pl.ds(offset(off_ref, row, 3) + CAP, CAP)
        x_scr[tail, :] = jnp.zeros((CAP, D), BF16)
        d_scr[tail, :] = jnp.zeros((CAP, D), BF16)
        gg[...] = jnp.zeros_like(gg)
        gu[...] = jnp.zeros_like(gu)
        gd[...] = jnp.zeros_like(gd)

        @pl.loop(0, off_ref[row, 4])
        def _(blk):
            rows = pl.ds(pl.multiple_of(blk * CAP, CAP), CAP)
            x_blk = x_scr[rows, :]
            d_blk = d_scr[rows, :]
            a_pre = mm(x_blk, wg_ref[exp], NT)
            b_pre = mm(x_blk, wu_ref[exp], NT)
            grad_h = mm(d_blk, wd_ref[exp], NT).astype(BF16).astype(F32)
            sigma = jax.nn.sigmoid(a_pre)
            swish = a_pre * sigma
            hidden = (swish * b_pre).astype(BF16)
            grad_a = (grad_h * b_pre * sigma * (1.0 + a_pre * (1.0 - sigma))).astype(BF16)
            grad_b = (grad_h * swish).astype(BF16)
            gx_scr[rows, :] = (mm(grad_a, wg_ref[exp]) + mm(grad_b, wu_ref[exp])).astype(BF16)
            gg[...] += mm(x_blk, grad_a, TN)
            gu[...] += mm(x_blk, grad_b, TN)
            gd[...] += mm(d_blk, hidden, TN)

        gx_scr[pl.ds(pl.multiple_of(off_ref[row, 4] * CAP, CAP), CAP), :] = jnp.zeros((CAP, D), BF16)
        for grad_ref, grad in ((gg_ref, gg), (gu_ref, gu), (gd_ref, gd)):
            for owner in range(4):
                grad_ref[exp - first, owner // 2, owner % 2] = grad[ROWS_DP * owner:ROWS_DP * owner + ROWS_DP].astype(BF16)
        for src in range(N_EP):
            acc[src] += mm(pick(layer, rank_ref, src, exp), gx_scr[pl.ds(offset(off_ref, row, src), CAP), :], TN)

    out_ref[...] = acc[...].astype(out_ref.dtype)


def expert_backward(layer, first, count, routes, u_all, dys, weights, carried=(), out_type=BF16):
    grad = block(count, 2, 2, ROWS_DP, FF)
    return plain(functools.partial(backward_kernel, layer, first, count, len(dys), len(carried)), 'expert_backward',
                 routes + (u_all,) + dys + carried + weights, (block(N_EP, TOK, D, dtype=out_type), grad, grad, grad),
                 [pltpu.VMEM((SLOTS, D), BF16)] * 3 + [pltpu.VMEM((N_EP, TOK, D), F32)] + [pltpu.VMEM((D, FF), F32)] * 3,
                 9_000_000_000 * count)


def remote(src, dst, sems, slot, target):
    send, recv = sems
    return pltpu.make_async_remote_copy(src_ref=src, dst_ref=dst, send_sem=send.at[slot], recv_sem=recv.at[slot],
                                        device_id=target, device_id_type=pl.DeviceIdType.MESH)


class Place:
    def __init__(self):
        ep, dp = lax.axis_index('ep'), lax.axis_index('dp')
        self.me = ep
        self.z, self.y = ep // 2, ep % 2
        self.x, self.c = dp // 2, dp % 2
        self.to_y, self.to_z = {'ep': self.z * 2 + 1 - self.y}, {'ep': (1 - self.z) * 2 + self.y}
        self.to_c, self.to_x = {'dp': self.x * 2 + 1 - self.c}, {'dp': (1 - self.x) * 2 + self.c}


def greet(targets):
    barrier = pltpu.get_barrier_semaphore()
    for target in targets:
        pl.semaphore_signal(barrier, inc=1, device_id=target, device_id_type=pl.DeviceIdType.MESH)
    pl.semaphore_wait(barrier, len(targets))


HALF = TOK // 2
TOP_ROWS, LOW_ROWS = pl.ds(0, HALF), pl.ds(HALF, HALF)


class Spread:
    def __init__(self, at, own, every, sems):
        self.direct = [remote(own.at[TOP_ROWS], every.at[1, TOP_ROWS], sems, 0, at.to_y),
                       remote(own.at[LOW_ROWS], every.at[2, LOW_ROWS], sems, 1, at.to_z),
                       remote(own.at[LOW_ROWS], every.at[1, LOW_ROWS], sems, 2, at.to_y),
                       remote(own.at[TOP_ROWS], every.at[2, TOP_ROWS], sems, 3, at.to_z)]
        self.onward = [remote(every.at[1, TOP_ROWS], every.at[3, TOP_ROWS], sems, 4, at.to_z),
                       remote(every.at[2, LOW_ROWS], every.at[3, LOW_ROWS], sems, 5, at.to_y)]

    def start(self):
        for copy in self.direct:
            copy.start()

    def forward(self):
        for first, then in zip(self.direct, self.onward):
            first.wait_recv()
            then.start()

    def finish(self):
        for copy in self.direct[2:] + self.onward:
            copy.wait_recv()
        for copy in self.direct + self.onward:
            copy.wait_send()


class Collect:
    def __init__(self, at, part, got, mix_scr, sems):
        self.part, self.got, self.mix_scr = part, got, mix_scr
        self.direct = [remote(part.at[3, TOP_ROWS], got.at[0], sems, 0, at.to_y),
                       remote(part.at[3, LOW_ROWS], got.at[1], sems, 1, at.to_z),
                       remote(part.at[1, TOP_ROWS], got.at[2], sems, 2, at.to_y),
                       remote(part.at[2, LOW_ROWS], got.at[3], sems, 3, at.to_z)]
        self.summed = [remote(mix_scr.at[0], got.at[4], sems, 4, at.to_z),
                       remote(mix_scr.at[1], got.at[5], sems, 5, at.to_y)]

    def start(self):
        for copy in self.direct:
            copy.start()

    def forward(self):
        for step, (slot, rows) in enumerate(((2, TOP_ROWS), (1, LOW_ROWS))):
            self.direct[step].wait_recv()
            self.mix_scr[step] = (self.part[slot, rows].astype(F32) + self.got[step].astype(F32)).astype(BF16)
            self.summed[step].start()

    def finish(self, base):
        for copy in self.direct[2:] + self.summed:
            copy.wait_recv()
        got = self.got
        top = self.part[0, TOP_ROWS].astype(F32) + got[2].astype(F32) + got[4].astype(F32)
        low = self.part[0, LOW_ROWS].astype(F32) + got[3].astype(F32) + got[5].astype(F32)
        return (base[TOP_ROWS].astype(F32) + top).astype(BF16), (base[LOW_ROWS].astype(F32) + low).astype(BF16)

    def drain(self):
        for copy in self.direct + self.summed:
            copy.wait_send()


class Halve:
    def __init__(self, at, grads, first, got, sems):
        self.at, self.grads, self.first, self.got = at, grads, first, got
        self.pair = [remote(grads[k // 2].at[first + k % 2, :, 1 - at.c], got.at[k], sems, k, at.to_c) for k in range(6)]

    def start(self):
        for copy in self.pair:
            copy.start()

    def total(self, mat, side):
        return jnp.concatenate([self.grads[mat][self.first + exp, side, self.at.c].astype(F32) + self.got[2 * mat + exp, side].astype(F32)
                                for exp in range(2)], axis=1).astype(BF16)

    def wait(self, mat):
        for exp in range(2):
            self.pair[2 * mat + exp].wait_recv()

    def drain(self):
        for copy in self.pair:
            copy.wait_send()


def store_pair(out, first, keep, got):
    total = (keep.astype(F32) + got.astype(F32)).astype(BF16)
    for exp in range(2):
        out[first + exp] = total[:, FF * exp:FF * exp + FF]


class Across:
    def __init__(self, at, halve, keep, send, got, sems):
        self.at, self.halve, self.keep, self.send, self.got = at, halve, keep, send, got
        self.along = [remote(send.at[mat], got.at[mat], sems, mat, at.to_x) for mat in range(3)]

    def forward(self, mat):
        self.halve.wait(mat)
        self.send[mat] = self.halve.total(mat, 1 - self.at.x)
        self.along[mat].start()
        self.keep[mat] = self.halve.total(mat, self.at.x)

    def finish(self, outs, first):
        for mat in range(3):
            self.along[mat].wait_recv()
            store_pair(outs[mat], first, self.keep[mat], self.got[mat])
        for copy in self.along:
            copy.wait_send()


def sems(count):
    return [pltpu.SemaphoreType.DMA((count,))] * 2


PACKED = (3, ROWS_DP, 2 * FF)
COLLECT_SCRATCH = [pltpu.VMEM((6, HALF, D), BF16), pltpu.VMEM((2, HALF, D), BF16)] + sems(6)
HALVE_SCRATCH = [pltpu.VMEM((6, 2, ROWS_DP, FF), BF16)] + sems(6)
ACROSS_SCRATCH = [pltpu.VMEM(PACKED, BF16)] * 3 + sems(3)


def call(kernel, name, ident, ins, outs, scratch):
    return pl.pallas_call(
        kernel, out_shape=outs, in_specs=[VMEM] * len(ins), scratch_shapes=scratch,
        out_specs=jax.tree.map(lambda o: SMEM if o.shape == (8, 8) else VMEM, outs),
        compiler_params=pltpu.CompilerParams(collective_id=ident, has_side_effects=True, vmem_limit_bytes=24 * 1024 * 1024),
        cost_estimate=pl.CostEstimate(flops=10_000_000_000, bytes_accessed=4_000_000, transcendentals=0), name=name)(*ins)


def entry_kernel(u_ref, pack_ref, every, rank_ref, gate_ref, off_ref, packs, s_send, s_recv, p_send, p_recv):
    at = Place()
    greet([at.to_y, at.to_z])
    small = [remote(pack_ref, packs.at[1], (p_send, p_recv), 0, at.to_y),
             remote(pack_ref, packs.at[2], (p_send, p_recv), 1, at.to_z),
             remote(packs.at[1], packs.at[3], (p_send, p_recv), 2, at.to_z)]
    small[0].start()
    small[1].start()
    spread = Spread(at, u_ref, every, (s_send, s_recv))
    spread.start()
    every[0] = u_ref[...]
    packs[0] = pack_ref[...]
    small[0].wait_recv()
    small[2].start()
    spread.forward()
    small[1].wait_recv()
    small[2].wait_recv()
    route_into(packs, rank_ref, gate_ref, off_ref, at.me)
    spread.finish()
    for copy in small:
        copy.wait_send()


def middle_kernel(part, u_ref, dense_ref, mid_ref, every, got, mix_scr, c_send, c_recv, u_scr, s_send, s_recv):
    at = Place()
    greet([at.to_y, at.to_z])
    collect = Collect(at, part, got, mix_scr, (c_send, c_recv))
    collect.start()
    collect.forward()
    top, low = collect.finish(u_ref)
    for rows, half in ((TOP_ROWS, top), (LOW_ROWS, low)):
        u_scr[rows] = (half.astype(F32) + mm(half, dense_ref[...])).astype(BF16)
    spread = Spread(at, u_scr, every, (s_send, s_recv))
    spread.start()
    mid_ref[TOP_ROWS] = top
    mid_ref[LOW_ROWS] = low
    every[0] = u_scr[...]
    collect.drain()
    spread.forward()
    spread.finish()


def dense_grad(x_ref, top, low):
    return mm(x_ref[TOP_ROWS], top, TN) + mm(x_ref[LOW_ROWS], low, TN)


def write_slabs(slabs, value):
    for k in range(16):
        slabs[k // 8, k // 4 % 2, k // 2 % 2, k % 2] = value[24 * k:24 * k + 24].astype(BF16)


def turn_kernel(part, dy_ref, dense_ref, mid_ref, ga, gb, gc, grad_ref, every, slabs, oa, ob, oc, later_keep, later_send,
                got, mix_scr, c_send, c_recv, s_send, s_recv, got_a, a_send, a_recv, got_b, b_send, b_recv,
                keep, send, got_x, x_send, x_recv, g_scr):
    at = Place()
    greet([at.to_y, at.to_z, at.to_c, at.to_x])
    collect = Collect(at, part, got, mix_scr, (c_send, c_recv))
    collect.start()
    now = Halve(at, (ga, gb, gc), 0, got_a, (a_send, a_recv))
    later = Halve(at, (ga, gb, gc), 2, got_b, (b_send, b_recv))
    now.start()
    later.start()
    across = Across(at, now, keep, send, got_x, (x_send, x_recv))
    for mat in range(3):
        across.forward(mat)
    collect.forward()
    for mat in range(3):
        later.wait(mat)
        later_send[mat] = later.total(mat, 1 - at.x)
        later_keep[mat] = later.total(mat, at.x)
    top, low = collect.finish(dy_ref)
    for rows, half in ((TOP_ROWS, top), (LOW_ROWS, low)):
        g_scr[rows] = (half.astype(F32) + mm(half, dense_ref[...], NT)).astype(BF16)
    spread = Spread(at, g_scr, every, (s_send, s_recv))
    spread.start()
    grad_ref[...] = g_scr[...]
    every[0] = g_scr[...]
    write_slabs(slabs, dense_grad(mid_ref, top, low))
    collect.drain()
    spread.forward()
    now.drain()
    later.drain()
    across.finish((oa, ob, oc), 0)
    spread.finish()


def pair_kernel(ga, gb, gc, later_keep, later_send, got_b, b_send, b_recv):
    at = Place()
    greet([at.to_c])
    later = Halve(at, (ga, gb, gc), 0, got_b, (b_send, b_recv))
    later.start()
    for mat in range(3):
        later.wait(mat)
        later_send[mat] = later.total(mat, 1 - at.x)
        later_keep[mat] = later.total(mat, at.x)
    later.drain()


def exit_kernel(part, dy_ref, dense_ref, tok_ref, slabs_two, ga, gb, gc, two_keep, two_got, one_keep, one_got, da, db, dc,
                dx_ref, dense_one, dense_two, oa, ob, oc, ta, tb, tc,
                got, mix_scr, c_send, c_recv, got_a, a_send, a_recv, keep, send, got_x, x_send, x_recv,
                slab_c, slab_z, slab_y, slab_x, sum_c, sum_z, sum_y, s_send, s_recv, slabs_one):
    at = Place()
    greet([at.to_y, at.to_z, at.to_c, at.to_x])
    collect = Collect(at, part, got, mix_scr, (c_send, c_recv))
    collect.start()
    now = Halve(at, (ga, gb, gc), 0, got_a, (a_send, a_recv))
    now.start()
    across = Across(at, now, keep, send, got_x, (x_send, x_recv))
    for mat in range(3):
        across.forward(mat)
    collect.forward()
    for mat, (out, done) in enumerate(((ta, da), (tb, db), (tc, dc))):
        store_pair(out, 2, two_keep[mat], two_got[mat])
        out[0:2] = done[...]
    for mat, out in enumerate((oa, ob, oc)):
        store_pair(out, 0, one_keep[mat], one_got[mat])
    top, low = collect.finish(dy_ref)
    write_slabs(slabs_one, dense_grad(tok_ref, top, low))
    pair = (s_send, s_recv)
    to_c = [remote(slabs.at[:, 1 - at.c], slab_c.at[k], pair, k, at.to_c) for k, slabs in enumerate((slabs_one, slabs_two))]
    for copy in to_c:
        copy.start()
    for rows, half in ((TOP_ROWS, top), (LOW_ROWS, low)):
        dx_ref[rows] = (half.astype(F32) + mm(half, dense_ref[...], NT)).astype(BF16)
    for k, slabs in enumerate((slabs_one, slabs_two)):
        to_c[k].wait_recv()
        for side in range(2):
            sum_c[k, side] = (slabs[side, at.c].astype(F32) + slab_c[k, side].astype(F32)).astype(BF16)
    to_z = remote(sum_c.at[:, :, 1 - at.z], slab_z, pair, 2, at.to_z)
    to_z.start()
    to_z.wait_recv()
    for k in range(2):
        for side in range(2):
            sum_z[k, side] = (sum_c[k, side, at.z].astype(F32) + slab_z[k, side].astype(F32)).astype(BF16)
    to_y = remote(sum_z.at[:, :, 1 - at.y], slab_y, pair, 3, at.to_y)
    to_y.start()
    to_y.wait_recv()
    for k in range(2):
        for side in range(2):
            sum_y[side, k] = (sum_z[k, side, at.y].astype(F32) + slab_y[k, side].astype(F32)).astype(BF16)
    to_x = remote(sum_y.at[1 - at.x], slab_x, pair, 4, at.to_x)
    to_x.start()
    across.finish((oa, ob, oc), 2)
    to_x.wait_recv()
    for k, out in enumerate((dense_one, dense_two)):
        out[...] = (sum_y[at.x, k].astype(F32) + slab_x[k].astype(F32)).astype(BF16)
    collect.drain()
    now.drain()
    for copy in to_c + [to_z, to_y, to_x]:
        copy.wait_send()


def store_kernel(*refs):
    count = len(refs) // 2
    copies = [pltpu.make_async_copy(refs[k], refs[count + k], refs[-1].at[k]) for k in range(count)]
    for copy in copies:
        copy.start()
    for copy in copies:
        copy.wait()


def store_all(values):
    return pl.pallas_call(
        store_kernel, out_shape=[block(*value.shape) for value in values], in_specs=[VMEM] * len(values),
        out_specs=[pl.BlockSpec(memory_space=pl.ANY)] * len(values), scratch_shapes=[pltpu.SemaphoreType.DMA((len(values),))],
        compiler_params=pltpu.CompilerParams(vmem_limit_bytes=1024 * 1024),
        cost_estimate=pl.CostEstimate(flops=1_000_000_000, bytes_accessed=4_000_000, transcendentals=0), name='store')(*values)


def mix(x_loc, dense_w):
    return (x_loc.astype(F32) + jnp.dot(x_loc, dense_w, preferred_element_type=F32)).astype(BF16)


def stored(w_gate, w_up, w_down):
    return jnp.swapaxes(w_gate, 1, 2), jnp.swapaxes(w_up, 1, 2), w_down


def along_x(sent):
    return lax.ppermute(sent, 'dp', [(0, 2), (2, 0), (1, 3), (3, 1)])


def solution(mesh):
    tok_spec = P(('dp', 'ep'), None)
    exp_spec = P('ep', None, None)
    layer_specs = (P(None, None), tok_spec, tok_spec, exp_spec, exp_spec, exp_spec)
    grad_specs = (P(('dp', 'ep'), None), P('ep', 'dp', None), P('ep', 'dp', None), P('ep', None, 'dp'))

    def local_step(tokens, dy_out, dense_w1, route_idx1, route_gate1, w_gate1, w_up1, w_down1, dense_w2, route_idx2, route_gate2, w_gate2, w_up2, w_down2):
        weights_one, weights_two = stored(w_gate1, w_up1, w_down1), stored(w_gate2, w_up2, w_down2)
        tok_block, all_block = block(TOK, D), block(N_EP, TOK, D)
        pack = jnp.concatenate([route_idx1.T.astype(F32), route_idx2.T.astype(F32), route_gate1.T, route_gate2.T], axis=0)
        mixed_one = mix(tokens, dense_w1)
        u_one, rank, gate, off = call(
            entry_kernel, 'entry', 0, (mixed_one, pack),
            (all_block, block(2, N_EP, 8, TOK, dtype=jnp.int32), block(2, N_EP, TOK, 8, dtype=F32), block(8, 8, dtype=jnp.int32)),
            [pltpu.VMEM((N_EP, 16, TOK), F32)] + sems(6) + sems(3))
        routes = (off, rank, gate)
        dy_later, u_one = lax.optimization_barrier((dy_out, u_one))
        dy_all = (dy_out,) + tuple(lax.ppermute(dy_later, 'ep', [(k, k ^ flip) for k in range(N_EP)]) for flip in (1, 2, 3))
        part = expert_forward(0, routes, u_one, weights_one)
        mid_tok, u_two = call(middle_kernel, 'middle', 1, (part, mixed_one, dense_w2), (tok_block, all_block),
                              COLLECT_SCRATCH + [pltpu.VMEM((TOK, D), BF16)] + sems(6))
        part, *grads = expert_backward(1, 0, 4, routes, u_two, dy_all, weights_two)
        grad_mid, dy_mid, slabs, *done_two, keep_two, send_two = call(
            turn_kernel, 'turn', 2, (part, dy_out, dense_w2, mid_tok) + tuple(grads),
            (tok_block, all_block, block(2, 2, 2, 2, 24, D)) + (block(2, ROWS_DP, FF),) * 3 + (block(*PACKED),) * 2,
            COLLECT_SCRATCH + sems(6) + HALVE_SCRATCH * 2 + ACROSS_SCRATCH + [pltpu.VMEM((TOK, D), BF16)])
        got_two = along_x(send_two)
        part, *grads = expert_backward(0, 0, 2, routes, u_one, (dy_mid,), weights_one, out_type=F32)
        got_two, grads = lax.optimization_barrier((got_two, grads))
        keep_one, send_one = call(pair_kernel, 'pair', 4, tuple(grads), (block(*PACKED),) * 2, HALVE_SCRATCH)
        got_one = along_x(send_one)
        part, *grads = expert_backward(0, 2, 2, routes, u_one, (dy_mid,), weights_one, carried=(part,))
        slab = lambda *lead: pltpu.VMEM(lead + (24, D), BF16)
        grad_tok, dense_one, dense_two, *reduced = store_all(call(
            exit_kernel, 'exit', 3, (part, grad_mid, dense_w1, tokens, slabs) + tuple(grads) + (keep_two, got_two, keep_one, got_one) + tuple(done_two),
            (tok_block, block(24, D), block(24, D)) + (block(N_LOC, ROWS_DP, FF),) * 6,
            COLLECT_SCRATCH + HALVE_SCRATCH + ACROSS_SCRATCH
            + [slab(2, 2, 2, 2), slab(2, 2, 2), slab(2, 2), slab(2), slab(2, 2, 2, 2), slab(2, 2, 2), slab(2, 2)]
            + sems(5) + [slab(2, 2, 2, 2)]))

        def shaped(gate_up_down):
            return gate_up_down[0], gate_up_down[1], jnp.swapaxes(gate_up_down[2], 1, 2)

        return (grad_tok, dense_one) + shaped(reduced[:3]) + (dense_two,) + shaped(reduced[3:])

    return jax.shard_map(local_step, mesh=mesh, in_specs=(tok_spec, tok_spec) + layer_specs + layer_specs,
                         out_specs=(tok_spec,) + grad_specs + grad_specs, check_vma=False)
```

time: 277 us -> 208 us (0.75)
  Pallas kernels: 231 us -> 194 us
  local copies, waits for them, and re-layouts: 29.2 us -> 0.06 us
  between operations: 14.2 us -> 1.04 us
  starting transfers between devices: 0.04 us -> 5.51 us
  waiting for transfers between devices: 0.02 us -> 3.47 us
    pallas_call x8 -> x10, Pallas kernels: 231 us -> 194 us  [the longest x5 108 us: call(): pl.pallas_call(kernel, out_shape=outs, in_specs=[VMEM] * len(ins), scratc...]
    unnamed x39 -> x20, local copies, waits for them, and re-layouts: 26.4 us -> 0.06 us
    ppermute x0 -> x5, starting transfers between devices: none -> 5.51 us  [the longest x3 3.52 us: local_step(): lax.ppermute(dy_later, 'ep', [(k, k ^ flip) for k in range(N_EP)])]
    ppermute x0 -> x5, waiting for transfers between devices: none -> 3.47 us  [the longest x2 3.46 us: along_x(): return lax.ppermute(sent, 'dp', [(0, 2), (2, 0), (1, 3), (3, 1)])]
    squeeze x3 -> x0, local copies, waits for them, and re-layouts: 2.78 us -> none  [the longest x1 1.5 us: local_step(): gate[1]]
  transfers between devices with their start and end apart: 1 -> 5, of which waited for: 0 -> 1; matrix products, arithmetic and copies ran while one was open for 6% -> 0% of each run, Pallas kernels for 17% -> 37%
where the time goes in v2:
time: 208 us; the launch traced here: 207 us
  Pallas kernels  194 us (93%)
  starting transfers between devices  5.51 us (3%)
  waiting for transfers between devices  3.47 us (2%)
    pallas_call x5, Pallas kernels, call(): pl.pallas_call(kernel, out_shape=outs, in_specs=[VMEM] * len(ins), scratc...  108 us
    pallas_call x4, Pallas kernels, plain(): pl.pallas_call(kernel, out_shape=outs, in_specs=[SMEM] + [VMEM] * (len(in...  83.4 us
  transfers between devices with their start and end apart: 5, of which 1 were waited for; matrix products, arithmetic and copies ran while one was open for 0% of the time, Pallas kernels for 37%

profile of v2, /device:TPU:0, one launch (start us, length us, event | category | flops | bytes accessed | tf_op | source)
XLA Modules:
  0.0 206.6 jit_solution(16111928955575647820)
XLA Ops:
  0.6 0.7 convert_bitcast_fusion
  1.4 1.6 fusion.u_ref
  3.0 0.7 pad_maximum_fusion.pack_ref
  3.7 0.0 copy-start.6
  3.7 0.0 copy-start.3
  3.7 0.0 copy-start.4
  3.7 0.0 copy-start.5
  3.7 20.1 %entry.1 = (bf16[4,512,384]{2,1,0:T(8,128)(2,1)S(1)}, s32[2,4,8,512]{3,2,1,0:T(8,128)S(1)}, f32[2,4,512,8]{3,2,1,0:T(8,128)S(1)}, s32[8,8]{1,0:T(8,128)S(1)}) custom-call(bf16[512,384]{1,0:T(8,128)(2,1)S(1)} %fusion.u_ref, f32[16,512]{1,0:T(8,128)S(1)} %pad_maximum_fusion.pack_ref), custom_call_target="tpu_custom_call" | custom-call | flops 10000000000 | bytes 4000000 | tf_op jit(solution)/shard_map/entry/pallas_call | solution.py:322
  23.9 0.0 copy-done.6
  23.9 0.5 collective-permute-start
  24.4 1.5 collective-permute-start.1
  26.0 1.5 collective-permute-start.2
  27.4 0.0 copy-done.3
  27.4 0.0 copy-done.4
  27.4 0.0 copy-done.5
  27.4 0.0 copy-start.8
  27.4 16.4 %expert_forward.1.part = bf16[4,512,384]{2,1,0:T(8,128)(2,1)S(1)} custom-call(s32[8,8]{1,0:T(8,128)S(1)} %get-tuple-element.61.off_ref, s32[2,4,8,512]{3,2,1,0:T(8,128)S(1)} %get-tuple-element.62.rank_ref, f32[2,4,512,8]{3,2,1,0:T(8,128)S(1)} %get-tuple-element.63.gate_ref, bf16[4,512,384]{2,1,0:T(8,128)(2,1)S(1)} %get-tuple-element.65.u_ref, ...), custom_call_target="tpu_custom_call" | custom-call | flops 14000000000 | bytes 10000000 | tf_op jit(solution)/shard_map/expert_forward/pallas_call | solution.py:109
  43.9 0.0 copy-done.8
  43.9 0.0 copy-start
  43.9 0.0 copy-start.1
  43.9 0.0 copy-start.2
  43.9 26.6 %middle.1 = (bf16[512,384]{1,0:T(8,128)(2,1)S(1)}, bf16[4,512,384]{2,1,0:T(8,128)(2,1)S(1)}) custom-call(bf16[4,512,384]{2,1,0:T(8,128)(2,1)S(1)} %expert_forward.1.part, bf16[512,384]{1,0:T(8,128)(2,1)S(1)} %fusion.u_ref, bf16[384,384]{1,0:T(8,128)(2,1)S(1)} %copy-done.8), custom_call_target="tpu_custom_call" | custom-call | flops 10000000000 | bytes 4000000 | tf_op jit(solution)/shard_map/middle/pallas_call | solution.py:322
  70.5 0.0 collective-permute-done.refs_1_
  70.5 0.0 collective-permute-done.1.refs_2_
  70.5 0.0 collective-permute-done.2.refs_3_
  70.5 0.0 copy-done
  70.5 0.0 copy-done.1
  70.5 0.0 copy-done.2
  70.5 32.8 %expert_backward.3 = (bf16[4,512,384]{2,1,0:T(8,128)(2,1)S(1)}, bf16[4,2,2,96,672]{4,3,2,1,0:T(8,128)(2,1)S(1)}, bf16[4,2,2,96,672]{4,3,2,1,0:T(8,128)(2,1)S(1)}, bf16[4,2,2,96,672]{4,3,2,1,0:T(8,128)(2,1)S(1)}) custom-call(s32[8,8]{1,0:T(8,128)S(1)} %get-tuple-element.61.off_ref, s32[2,4,8,512]{3,2,1,0:T(8,128)S(1)} %get-tuple-element.62.rank_ref, ...), custom_call_target="tpu_custom_call" | custom-call | flops 35999997952 | bytes 10000000 | tf_op jit(solution)/shard_map/expert_backward/pallas_call | solution.py:109
  103.4 29.9 %turn.1 = (bf16[512,384]{1,0:T(8,128)(2,1)S(1)}, bf16[4,512,384]{2,1,0:T(8,128)(2,1)S(1)}, bf16[2,2,2,2,24,384]{5,4,3,2,1,0:T(8,128)(2,1)S(1)}, bf16[2,96,672]{2...) custom-call(bf16[4,512,384]{2,1,0:T(8,128)(2,1)S(1)} %get-tuple-elem, ...), custom_call_target="tpu_custom_call" | custom-call | flops 10000000000 | bytes 4000000 | tf_op jit(solution)/shard_map/turn/pallas_call | solution.py:322
  133.3 1.5 collective-permute-start.3
  134.8 18.1 %expert_backward.4 = (f32[4,512,384]{2,1,0:T(8,128)S(1)}, bf16[2,2,2,96,672]{4,3,2,1,0:T(8,128)(2,1)S(1)}, bf16[2,2,2,96,672]{4,3,2,1,0:T(8,128)(2,1)S(1)}, bf16[2,2,2,96,672]{4,3,2,1,0:T(8,128)(2,1)S(1)}) custom-call(s32[8,8]{1,0:T(8,128)S(1)} %get-tuple-element.61.off_ref, s32[2,4,8,512]{3,2,1,0:T(8,128)S(1)} %get-tuple-element.62.rank_ref, ...), custom_call_target="tpu_custom_call" | custom-call | flops 17999998976 | bytes 10000000 | tf_op jit(solution)/shard_map/expert_backward/pallas_call | solution.py:109
  152.9 0.0 collective-permute-done.3.two_got
  152.9 4.0 %pair.1 = (bf16[3,96,1344]{2,1,0:T(8,128)(2,1)S(1)}, bf16[3,96,1344]{2,1,0:T(8,128)(2,1)S(1)}) custom-call(bf16[2,2,2,96,672]{4,3,2,1,0:T(8,128)(2,1)S(1)} %get-tuple-element.87.ga, bf16[2,2,2,96,672]{4,3,2,1,0:T(8,128)(2,1)S(1)} %get-tuple-element.88.gb, bf16[2,2,2,96,672]{4,3,2,1,0:T(8,128)(2,1)S(1)} %get-tuple-element.89.gc), custom_call_target="tpu_custom_call" | custom-call | flops 10000000000 | bytes 4000000 | tf_op jit(solution)/shard_map/pair/pallas_call | solution.py:322
  156.9 0.5 collective-permute-start.4
  157.4 0.0 copy-start.7
  157.4 0.0 copy-start.9
  157.4 16.1 %expert_backward.5 = (bf16[4,512,384]{2,1,0:T(8,128)(2,1)S(1)}, bf16[2,2,2,96,672]{4,3,2,1,0:T(8,128)(2,1)S(1)}, bf16[2,2,2,96,672]{4,3,2,1,0:T(8,128)(2,1)S(1)}, bf16[2,2,2,96,672]{4,3,2,1,0:T(8,128)(2,1)S(1)}) custom-call(s32[8,8]{1,0:T(8,128)S(1)} %get-tuple-element.61.off_ref, s32[2,4,8,512]{3,2,1,0:T(8,128)S(1)} %get-tuple-element.62.rank_ref, ...), custom_call_target="tpu_custom_call" | custom-call | flops 17999998976 | bytes 10000000 | tf_op jit(solution)/shard_map/expert_backward/pallas_call | solution.py:109
  173.5 3.5 %collective-permute-done.4.one_got = bf16[3,96,1344]{2,1,0:T(8,128)(2,1)S(1)} collective-permute-done((bf16[3,96,1344]{2,1,0:T(8,128)(2,1)S(1)}, bf16[3,96,1344]{2,1,0:T(8,128)(2,1)S(1)}, u32[]{:S(2)}, u32[]{:S(2)}) %collective-permute-start.4) | collective-permute-done | bytes 774176 | tf_op jit(solution)/shard_map/ppermute | solution.py:508
  176.9 0.0 copy-done.7
  176.9 0.0 copy-done.9
  176.9 27.5 %exit.1 = (bf16[512,384]{1,0:T(8,128)(2,1)S(1)}, bf16[24,384]{1,0:T(8,128)(2,1)S(1)}, bf16[24,384]{1,0:T(8,128)(2,1)S(1)}, bf16[4,96,672]{2,1,0:T(8,128)(2,1)S(1...) custom-call(bf16[4,512,384]{2,1,0:T(8,128)(2,1)S(1)} %get-tuple-elem, ...), custom_call_target="tpu_custom_call" | custom-call | flops 10000000000 | bytes 4000000 | tf_op jit(solution)/shard_map/exit/pallas_call | solution.py:322
  204.4 2.0 store.1
Async XLA Ops:
  3.7 20.2 %copy-start.6 = (bf16[512,384]{1,0:T(8,128)(2,1)S(1)}, bf16[512,384]{1,0:T(8,128)(2,1)}, u32[]{:S(2)}) copy-start(bf16[512,384]{1,0:T(8,128)(2,1)} %dy_ref.1) | copy-start | bytes 1179652
  3.7 23.7 %copy-start.3 = (bf16[4,384,672]{1,2,0:T(8,128)(2,1)S(1)}, bf16[4,384,672]{1,2,0:T(8,128)(2,1)}, u32[]{:S(2)}) copy-start(bf16[4,384,672]{1,2,0:T(8,128)(2,1)} %param.19) | copy-start | bytes 6193156
  3.7 23.7 %copy-start.4 = (bf16[4,384,672]{1,2,0:T(8,128)(2,1)S(1)}, bf16[4,384,672]{1,2,0:T(8,128)(2,1)}, u32[]{:S(2)}) copy-start(bf16[4,384,672]{1,2,0:T(8,128)(2,1)} %param.20) | copy-start | bytes 6193156
  3.7 23.7 %copy-start.5 = (bf16[4,672,384]{2,1,0:T(8,128)(2,1)S(1)}, bf16[4,672,384]{2,1,0:T(8,128)(2,1)}, u32[]{:S(2)}) copy-start(bf16[4,672,384]{2,1,0:T(8,128)(2,1)} %refs_4_.1) | copy-start | bytes 6193156
  23.9 46.6 %collective-permute-start = (bf16[512,384]{1,0:T(8,128)(2,1)S(1)}, bf16[512,384]{1,0:T(8,128)(2,1)S(1)}, u32[]{:S(2)}, u32[]{:S(2)}) collective-permute-start(bf16[512,384]{1,0:T(8,128)(2,1)S(1)} %copy-done.6), channel_id=1, source_target_pairs={{0,4},{4,0},{8,12},{12,8},{1,5},{5,1},{9,13},{13,9},{2,6},{6,2},{1... | collective-permute-start | bytes 1179656 | tf_op jit(solution)/shard_map/ppermute | solution.py:528
  24.4 46.1 %collective-permute-start.1 = (bf16[512,384]{1,0:T(8,128)(2,1)S(1)}, bf16[512,384]{1,0:T(8,128)(2,1)S(1)}, u32[]{:S(2)}, u32[]{:S(2)}) collective-permute-start(bf16[512,384]{1,0:T(8,128)(2,1)S(1)} %copy-done.6), channel_id=1, source_target_pairs={{0,8},{4,12},{8,0},{12,4},{1,9},{5,13},{9,1},{13,5},{2,10},{6,14},... | collective-permute-start | bytes 1179656 | tf_op jit(solution)/shard_map/ppermute | solution.py:528
  26.0 44.5 %collective-permute-start.2 = (bf16[512,384]{1,0:T(8,128)(2,1)S(1)}, bf16[512,384]{1,0:T(8,128)(2,1)S(1)}, u32[]{:S(2)}, u32[]{:S(2)}) collective-permute-start(bf16[512,384]{1,0:T(8,128)(2,1)S(1)} %copy-done.6), channel_id=1, source_target_pairs={{0,12},{4,8},{8,4},{12,0},{1,13},{5,9},{9,5},{13,1},{2,14},{6,10},... | collective-permute-start | bytes 1179656 | tf_op jit(solution)/shard_map/ppermute | solution.py:528
  27.4 16.4 %copy-start.8 = (bf16[384,384]{1,0:T(8,128)(2,1)S(1)}, bf16[384,384]{1,0:T(8,128)(2,1)}, u32[]{:S(2)}) copy-start(bf16[384,384]{1,0:T(8,128)(2,1)} %dense_ref.4) | copy-start | bytes 884740
  43.9 26.7 %copy-start = (bf16[4,384,672]{1,2,0:T(8,128)(2,1)S(1)}, bf16[4,384,672]{1,2,0:T(8,128)(2,1)}, u32[]{:S(2)}) copy-start(bf16[4,384,672]{1,2,0:T(8,128)(2,1)} %param.25) | copy-start | bytes 6193156
  43.9 26.7 %copy-start.1 = (bf16[4,384,672]{1,2,0:T(8,128)(2,1)S(1)}, bf16[4,384,672]{1,2,0:T(8,128)(2,1)}, u32[]{:S(2)}) copy-start(bf16[4,384,672]{1,2,0:T(8,128)(2,1)} %param.26) | copy-start | bytes 6193156
  43.9 26.7 %copy-start.2 = (bf16[4,672,384]{2,1,0:T(8,128)(2,1)S(1)}, bf16[4,672,384]{2,1,0:T(8,128)(2,1)}, u32[]{:S(2)}) copy-start(bf16[4,672,384]{2,1,0:T(8,128)(2,1)} %refs_6_.1) | copy-start | bytes 6193156
  133.3 19.6 %collective-permute-start.3 = (bf16[3,96,1344]{2,1,0:T(8,128)(2,1)S(1)}, bf16[3,96,1344]{2,1,0:T(8,128)(2,1)S(1)}, u32[]{:S(2)}, u32[]{:S(2)}) collective-permute-start(bf16[3,96,1344]{2,1,0:T(8,128)(2,1)S(1)} %get-tuple-element.82), channel_id=1, source_target_pairs={{0,2},{2,0},{1,3},{3,1},{4,6},{6,4},{5,7},{7,5},{8,10},{10,8},{9,1... | collective-permute-start | bytes 2322440 | tf_op jit(solution)/shard_map/ppermute | solution.py:508
  156.9 20.0 %collective-permute-start.4 = (bf16[3,96,1344]{2,1,0:T(8,128)(2,1)S(1)}, bf16[3,96,1344]{2,1,0:T(8,128)(2,1)S(1)}, u32[]{:S(2)}, u32[]{:S(2)}) collective-permute-start(bf16[3,96,1344]{2,1,0:T(8,128)(2,1)S(1)} %get-tuple-element.91), channel_id=1, source_target_pairs={{0,2},{2,0},{1,3},{3,1},{4,6},{6,4},{5,7},{7,5},{8,10},{10,8},{9,1... | collective-permute-start | bytes 2322440 | tf_op jit(solution)/shard_map/ppermute | solution.py:508
  157.4 19.5 %copy-start.7 = (bf16[512,384]{1,0:T(8,128)(2,1)S(1)}, bf16[512,384]{1,0:T(8,128)(2,1)}, u32[]{:S(2)}) copy-start(bf16[512,384]{1,0:T(8,128)(2,1)} %tok_ref.1) | copy-start | bytes 1179652
  157.4 19.5 %copy-start.9 = (bf16[384,384]{1,0:T(8,128)(2,1)S(1)}, bf16[384,384]{1,0:T(8,128)(2,1)}, u32[]{:S(2)}) copy-start(bf16[384,384]{1,0:T(8,128)(2,1)} %dense_ref.5) | copy-start | bytes 884740

commit v3 on v2

v3 whole, which is shorter than its diff:
```python
import functools

import jax
import jax.numpy as jnp
from jax import lax
from jax.experimental import pallas as pl
from jax.experimental.pallas import tpu as pltpu
from jax.sharding import PartitionSpec as P

BF16 = jnp.bfloat16
F32 = jnp.float32
N_EP = 4
N_LOC = 4
TOK = 512
D = 384
FF = 672
CAP = 256
SLOTS = 5 * CAP
ROWS_DP = D // 4
VMEM = pl.BlockSpec(memory_space=pltpu.VMEM)
SMEM = pl.BlockSpec(memory_space=pltpu.SMEM)


def block(*shape, dtype=BF16):
    return jax.ShapeDtypeStruct(shape, dtype)


def mm(a, b, dims=((1,), (0,))):
    return lax.dot_general(a, b, (dims, ((), ())), preferred_element_type=F32)


NT = ((1,), (1,))
TN = ((0,), (0,))


def route_into(packs, rank_ref, gate_ref, off_ref, me):
    before = (lax.broadcasted_iota(jnp.int32, (TOK, TOK), 0) < lax.broadcasted_iota(jnp.int32, (TOK, TOK), 1)).astype(BF16)
    for layer in range(2):
        running = [jnp.int32(0)] * N_LOC
        last = [jnp.int32(0)] * N_LOC
        for src in range(N_EP):
            ids = packs[src, 4 * layer:4 * layer + 4, :]
            gates = packs[src, 8 + 4 * layer:12 + 4 * layer, :]
            member, gate = [], []
            for exp in range(N_LOC):
                match = ids == (me * N_LOC + exp).astype(F32)
                member.append(jnp.sum(match.astype(F32), axis=0, keepdims=True))
                gate.append(jnp.sum(jnp.where(match, gates, 0.0), axis=0, keepdims=True))
            member = jnp.concatenate(member, axis=0)
            gate = jnp.concatenate(gate + [jnp.zeros((4, TOK), F32)], axis=0)
            rank = mm(member.astype(BF16), before)
            rank = jnp.where(member > 0.5, rank, -1.0).astype(jnp.int32)
            rank_ref[layer, src, 0:4, :] = rank
            gate_ref[layer, src] = jnp.transpose(gate)
            for exp in range(N_LOC):
                count = jnp.max(rank[exp:exp + 1, :]) + 1
                off_ref[layer * N_LOC + exp, src] = running[exp]
                last[exp] = running[exp] + count
                running[exp] = running[exp] + (count + 15) // 16 * 16
        for exp in range(N_LOC):
            halves = (last[exp] + CAP // 2 - 1) // (CAP // 2)
            off_ref[layer * N_LOC + exp, 4] = halves // 2
            off_ref[layer * N_LOC + exp, 5] = halves % 2
            off_ref[layer * N_LOC + exp, 6] = halves * (CAP // 2)
            off_ref[layer * N_LOC + exp, 7] = (halves + 1) // 2


def pick(layer, rank_ref, src, exp):
    row = rank_ref[layer, src, pl.ds(exp, 1), :]
    return (lax.broadcasted_iota(jnp.int32, (CAP, TOK), 0) == row).astype(BF16)


def gate_column(layer, gate_ref, src, exp):
    slab = gate_ref[layer, src]
    lane = lax.broadcasted_iota(jnp.int32, slab.shape, 1)
    return jnp.sum(jnp.where(lane == exp, slab, 0.0), axis=1, keepdims=True)


def offset(off_ref, row, src):
    return pl.multiple_of(off_ref[row, src], 16)


def scatter_gated(layer, rank_ref, gate_ref, o_ref, src):
    total = None
    for exp in range(N_LOC):
        term = gate_column(layer, gate_ref, src, exp) * mm(pick(layer, rank_ref, src, exp), o_ref[exp, src], TN)
        total = term if total is None else total + term
    return total.astype(BF16)


def scatter_plain(layer, rank_ref, g_refs, src):
    sel = jnp.concatenate([pick(layer, rank_ref, src, exp) for exp in range(N_LOC)], axis=0)
    per = N_LOC // len(g_refs)
    rows = [g_refs[exp // per][exp % per, src] for exp in range(N_LOC)]
    return mm(sel, jnp.concatenate(rows, axis=0), TN).astype(BF16)


def gather_rows(layer, rank_ref, pad_ref, src, toks):
    @pl.loop(0, N_LOC)
    def _(exp):
        pad_ref[exp, src] = mm(pick(layer, rank_ref, src, exp), toks[...]).astype(BF16)


def gather_scaled(layer, rank_ref, gate_ref, pad_ref, src, toks):
    @pl.loop(0, N_LOC)
    def _(exp):
        scaled = (gate_column(layer, gate_ref, src, exp) * toks[...].astype(F32)).astype(BF16)
        pad_ref[exp, src] = mm(pick(layer, rank_ref, src, exp), scaled).astype(BF16)


def packed(off_ref, row, pad_ref, exp, scr):
    for src in range(N_EP):
        scr[pl.ds(offset(off_ref, row, src), CAP), :] = pad_ref[exp, src]
    scr[pl.ds(offset(off_ref, row, 3) + CAP, CAP), :] = jnp.zeros((CAP, D), BF16)


def over_rows(off_ref, row, step):
    @pl.loop(0, off_ref[row, 4])
    def _(blk):
        step(pl.ds(pl.multiple_of(blk * CAP, CAP), CAP))

    @pl.when(off_ref[row, 5] == 1)
    def _():
        step(pl.ds(pl.multiple_of(off_ref[row, 4] * CAP, CAP), CAP // 2))


def tail_of(off_ref, row, size):
    return pl.ds(pl.multiple_of(off_ref[row, 6], CAP // 2), size)


def unpacked(off_ref, row, scr, out_ref, exp):
    for src in range(N_EP):
        out_ref[exp, src] = scr[pl.ds(offset(off_ref, row, src), CAP), :]


def forward_kernel(layer, off_ref, x_ref, wg_ref, wu_ref, wd_ref, out_ref, x_scr, o_scr):
    @pl.loop(0, N_LOC)
    def _(exp):
        row = layer * N_LOC + exp
        packed(off_ref, row, x_ref, exp, x_scr)

        def step(rows):
            x_blk = x_scr[rows, :]
            a_pre = mm(x_blk, wg_ref[exp], NT)
            b_pre = mm(x_blk, wu_ref[exp], NT)
            hidden = (jax.nn.silu(a_pre) * b_pre).astype(BF16)
            o_scr[rows, :] = mm(hidden, wd_ref[exp]).astype(BF16)

        over_rows(off_ref, row, step)
        o_scr[tail_of(off_ref, row, CAP), :] = jnp.zeros((CAP, D), BF16)
        unpacked(off_ref, row, o_scr, out_ref, exp)


def plain(kernel, name, ins, outs, scratch, grant, flops):
    return pl.pallas_call(
        kernel, out_shape=outs, in_specs=[SMEM] + [VMEM] * (len(ins) - 1), out_specs=jax.tree.map(lambda _: VMEM, outs),
        scratch_shapes=scratch, compiler_params=pltpu.CompilerParams(vmem_limit_bytes=grant * 1024 * 1024),
        cost_estimate=pl.CostEstimate(flops=flops, bytes_accessed=10_000_000, transcendentals=0), name=name)(*ins)


def expert_forward(layer, off, x_pad, weights):
    return plain(functools.partial(forward_kernel, layer), 'expert_forward', (off, x_pad) + weights, block(N_LOC, N_EP, CAP, D),
                 [pltpu.VMEM((SLOTS, D), BF16)] * 2, 8, 10_000_000_000)


def backward_kernel(layer, first, count, off_ref, x_ref, d_ref, wg_ref, wu_ref, wd_ref, out_ref, grad_ref, left, right, gx_scr):
    x_scr, d_scr = left.at[0], left.at[1]

    @pl.loop(first, first + count)
    def _(exp):
        row = layer * N_LOC + exp
        packed(off_ref, row, x_ref, exp, x_scr)
        packed(off_ref, row, d_ref, exp, d_scr)

        def step(rows):
            x_blk = x_scr[rows, :]
            a_pre = mm(x_blk, wg_ref[exp], NT)
            b_pre = mm(x_blk, wu_ref[exp], NT)
            grad_h = mm(d_scr[rows, :], wd_ref[exp], NT).astype(BF16).astype(F32)
            sigma = jax.nn.sigmoid(a_pre)
            swish = a_pre * sigma
            grad_a = (grad_h * b_pre * sigma * (1.0 + a_pre * (1.0 - sigma))).astype(BF16)
            grad_b = (grad_h * swish).astype(BF16)
            right[0, rows, :] = grad_a
            right[1, rows, :] = grad_b
            right[2, rows, :] = (swish * b_pre).astype(BF16)
            gx_scr[rows, :] = (mm(grad_a, wg_ref[exp]) + mm(grad_b, wu_ref[exp])).astype(BF16)

        over_rows(off_ref, row, step)
        gx_scr[tail_of(off_ref, row, CAP), :] = jnp.zeros((CAP, D), BF16)
        unpacked(off_ref, row, gx_scr, out_ref, exp - first)
        right[:, tail_of(off_ref, row, CAP // 2), :] = jnp.zeros((3, CAP // 2, FF), BF16)

        def weight_grads(depth):
            @pl.loop(0, 3)
            def _(mat):
                grad = mm(left[mat // 2, 0:depth, :], right[mat, 0:depth, :], TN).astype(BF16)
                for owner in range(4):
                    grad_ref[exp - first, mat, owner // 2, owner % 2] = grad[ROWS_DP * owner:ROWS_DP * owner + ROWS_DP]

        for blocks in range(1, 5):
            pl.when(off_ref[row, 7] == blocks)(functools.partial(weight_grads, blocks * CAP))

        @pl.when(off_ref[row, 7] == 0)
        def _():
            grad_ref[exp - first] = jnp.zeros(grad_ref.shape[1:], BF16)


def expert_backward(layer, first, count, off, x_pad, d_pad, weights):
    return plain(functools.partial(backward_kernel, layer, first, count), 'expert_backward',
                 (off, x_pad, d_pad) + weights, (block(count, N_EP, CAP, D), block(count, 3, 2, 2, ROWS_DP, FF)),
                 [pltpu.VMEM((2, SLOTS, D), BF16), pltpu.VMEM((3, N_EP * CAP + CAP // 2, FF), BF16), pltpu.VMEM((SLOTS, D), BF16)], 14, 9_000_000_000 * count)


def remote(src, dst, sems, slot, target):
    send, recv = sems
    return pltpu.make_async_remote_copy(src_ref=src, dst_ref=dst, send_sem=send.at[slot], recv_sem=recv.at[slot],
                                        device_id=target, device_id_type=pl.DeviceIdType.MESH)


class Place:
    def __init__(self):
        ep, dp = lax.axis_index('ep'), lax.axis_index('dp')
        self.me = ep
        self.z, self.y = ep // 2, ep % 2
        self.x, self.c = dp // 2, dp % 2
        self.to_y, self.to_z = {'ep': self.z * 2 + 1 - self.y}, {'ep': (1 - self.z) * 2 + self.y}
        self.to_d = {'ep': (1 - self.z) * 2 + 1 - self.y}
        self.to_c, self.to_x = {'dp': self.x * 2 + 1 - self.c}, {'dp': (1 - self.x) * 2 + self.c}


def greet(targets):
    barrier = pltpu.get_barrier_semaphore()
    for target in targets:
        pl.semaphore_signal(barrier, inc=1, device_id=target, device_id_type=pl.DeviceIdType.MESH)
    pl.semaphore_wait(barrier, len(targets))


HALF = TOK // 2
TOP_ROWS, LOW_ROWS = pl.ds(0, HALF), pl.ds(HALF, HALF)


class Spread:
    def __init__(self, at, own, every, sems):
        self.direct = [remote(own.at[TOP_ROWS], every.at[1, TOP_ROWS], sems, 0, at.to_y),
                       remote(own.at[LOW_ROWS], every.at[2, LOW_ROWS], sems, 1, at.to_z),
                       remote(own.at[LOW_ROWS], every.at[1, LOW_ROWS], sems, 2, at.to_y),
                       remote(own.at[TOP_ROWS], every.at[2, TOP_ROWS], sems, 3, at.to_z)]
        self.onward = [remote(every.at[1, TOP_ROWS], every.at[3, TOP_ROWS], sems, 4, at.to_z),
                       remote(every.at[2, LOW_ROWS], every.at[3, LOW_ROWS], sems, 5, at.to_y)]

    def start(self):
        for copy in self.direct:
            copy.start()

    def forward(self):
        for first, then in zip(self.direct, self.onward):
            first.wait_recv()
            then.start()

    def arrived(self, slot):
        for copy in ((), self.direct[2:3], self.direct[3:4], self.onward)[slot]:
            copy.wait_recv()

    def finish(self):
        for copy in self.direct + self.onward:
            copy.wait_send()


class Collect:
    def __init__(self, at, part, got, mix_scr, sems):
        self.part, self.got, self.mix_scr = part, got, mix_scr
        self.direct = [remote(part.at[3, TOP_ROWS], got.at[0], sems, 0, at.to_y),
                       remote(part.at[3, LOW_ROWS], got.at[1], sems, 1, at.to_z),
                       remote(part.at[1, TOP_ROWS], got.at[2], sems, 2, at.to_y),
                       remote(part.at[2, LOW_ROWS], got.at[3], sems, 3, at.to_z)]
        self.summed = [remote(mix_scr.at[0], got.at[4], sems, 4, at.to_z),
                       remote(mix_scr.at[1], got.at[5], sems, 5, at.to_y)]

    def start(self, slot_sum):
        self.part[3] = slot_sum(3)
        self.direct[0].start()
        self.direct[1].start()
        self.part[1] = slot_sum(1)
        self.direct[2].start()
        self.part[2] = slot_sum(2)
        self.direct[3].start()

    def forward(self):
        for step, (slot, rows) in enumerate(((2, TOP_ROWS), (1, LOW_ROWS))):
            self.direct[step].wait_recv()
            self.mix_scr[step] = (self.part[slot, rows].astype(F32) + self.got[step].astype(F32)).astype(BF16)
            self.summed[step].start()

    def finish(self, base):
        for copy in self.direct[2:] + self.summed:
            copy.wait_recv()
        got = self.got
        top = self.part[0, TOP_ROWS].astype(F32) + got[2].astype(F32) + got[4].astype(F32)
        low = self.part[0, LOW_ROWS].astype(F32) + got[3].astype(F32) + got[5].astype(F32)
        return (base[TOP_ROWS].astype(F32) + top).astype(BF16), (base[LOW_ROWS].astype(F32) + low).astype(BF16)

    def summed_gone(self):
        for copy in self.summed:
            copy.wait_send()

    def drain(self):
        for copy in self.direct:
            copy.wait_send()


class Halve:
    def __init__(self, at, grads, first, got, sems):
        self.at, self.grads, self.first, self.got = at, grads, first, got
        self.pair = [remote(grads.at[first + k % 2, k // 2, :, 1 - at.c], got.at[k], sems, k, at.to_c) for k in range(6)]

    def start(self):
        for copy in self.pair:
            copy.start()

    def total(self, mat, side):
        return jnp.concatenate([self.grads[self.first + exp, mat, side, self.at.c].astype(F32) + self.got[2 * mat + exp, side].astype(F32)
                                for exp in range(2)], axis=1).astype(BF16)

    def wait(self, mat):
        for exp in range(2):
            self.pair[2 * mat + exp].wait_recv()

    def drain(self):
        for copy in self.pair:
            copy.wait_send()


def store_pair(out, first, keep, got):
    total = (keep.astype(F32) + got.astype(F32)).astype(BF16)
    for exp in range(2):
        out[first + exp] = total[:, FF * exp:FF * exp + FF]


class Across:
    def __init__(self, at, halve, keep, send, got, sems):
        self.at, self.halve, self.keep, self.send, self.got = at, halve, keep, send, got
        self.along = [remote(send.at[mat], got.at[mat], sems, mat, at.to_x) for mat in range(3)]

    def forward(self, mat):
        self.halve.wait(mat)
        self.send[mat] = self.halve.total(mat, 1 - self.at.x)
        self.along[mat].start()
        self.keep[mat] = self.halve.total(mat, self.at.x)

    def finish(self, outs, first):
        for mat in range(3):
            self.along[mat].wait_recv()
            store_pair(outs[mat], first, self.keep[mat], self.got[mat])
        for copy in self.along:
            copy.wait_send()


def sems(count):
    return [pltpu.SemaphoreType.DMA((count,))] * 2


PACKED = (3, ROWS_DP, 2 * FF)
COLLECT_SCRATCH = [pltpu.VMEM((N_EP, TOK, D), BF16), pltpu.VMEM((6, HALF, D), BF16), pltpu.VMEM((2, HALF, D), BF16)] + sems(6)
HALVE_SCRATCH = [pltpu.VMEM((6, 2, ROWS_DP, FF), BF16)] + sems(6)
ACROSS_SCRATCH = [pltpu.VMEM(PACKED, BF16)] * 3 + sems(3)


ANY = pl.BlockSpec(memory_space=pl.ANY)


def call(kernel, name, ident, ins, outs, scratch, grant):
    return pl.pallas_call(
        kernel, out_shape=outs, scratch_shapes=scratch,
        in_specs=[SMEM if value.shape == (8, 8) else VMEM for value in ins],
        out_specs=jax.tree.map(lambda o: SMEM if o.shape == (8, 8) else VMEM, outs),
        compiler_params=pltpu.CompilerParams(collective_id=ident, has_side_effects=True, vmem_limit_bytes=grant * 1024 * 1024),
        cost_estimate=pl.CostEstimate(flops=10_000_000_000, bytes_accessed=4_000_000, transcendentals=0), name=name)(*ins)


def entry_kernel(own, pack_ref, x_pad, rank_ref, gate_ref, off_ref, packs, every, s_send, s_recv, p_send, p_recv):
    at = Place()
    greet([at.to_y, at.to_z])
    small = [remote(pack_ref, packs.at[1], (p_send, p_recv), 0, at.to_y),
             remote(pack_ref, packs.at[2], (p_send, p_recv), 1, at.to_z),
             remote(packs.at[1], packs.at[3], (p_send, p_recv), 2, at.to_z)]
    small[0].start()
    small[1].start()
    spread = Spread(at, own, every, (s_send, s_recv))
    spread.start()
    packs[0] = pack_ref[...]
    small[0].wait_recv()
    small[2].start()
    small[1].wait_recv()
    small[2].wait_recv()
    route_into(packs, rank_ref, gate_ref, off_ref, at.me)
    spread.forward()
    gather_rows(0, rank_ref, x_pad, 0, own)
    for src in range(1, N_EP):
        spread.arrived(src)
        gather_rows(0, rank_ref, x_pad, src, every.at[src])
    spread.finish()
    for copy in small:
        copy.wait_send()


def middle_kernel(o_ref, u_ref, dense_ref, rank_ref, gate_ref, dy_own, dy_y, dy_z, mid_ref, x_pad, d_pad,
                  part, got, mix_scr, c_send, c_recv, u_scr, every, s_send, s_recv, dy_d, d_send, d_recv):
    at = Place()
    greet([at.to_y, at.to_z])
    collect = Collect(at, part, got, mix_scr, (c_send, c_recv))

    def slot_sum(src):
        return scatter_gated(0, rank_ref, gate_ref, o_ref, src)

    collect.start(slot_sum)
    collect.forward()
    onward = [remote(dy_y.at[TOP_ROWS], dy_d.at[TOP_ROWS], (d_send, d_recv), 0, at.to_z),
              remote(dy_z.at[LOW_ROWS], dy_d.at[LOW_ROWS], (d_send, d_recv), 1, at.to_y)]
    part[0] = slot_sum(0)
    for src, dy_ref in ((0, dy_own), (1, dy_y)):
        gather_scaled(1, rank_ref, gate_ref, d_pad, src, dy_ref)
    collect.summed_gone()
    for copy in onward:
        copy.start()
    top, low = collect.finish(u_ref)
    for rows, half in ((TOP_ROWS, top), (LOW_ROWS, low)):
        u_scr[rows] = (half.astype(F32) + mm(half, dense_ref[...])).astype(BF16)
    spread = Spread(at, u_scr, every, (s_send, s_recv))
    spread.start()
    mid_ref[TOP_ROWS] = top
    mid_ref[LOW_ROWS] = low
    gather_rows(1, rank_ref, x_pad, 0, u_scr)
    gather_scaled(1, rank_ref, gate_ref, d_pad, 2, dy_z)
    spread.forward()
    for copy in onward:
        copy.wait_recv()
    gather_scaled(1, rank_ref, gate_ref, d_pad, 3, dy_d)
    collect.drain()
    for copy in onward:
        copy.wait_send()
    for src in range(1, N_EP):
        spread.arrived(src)
        gather_rows(1, rank_ref, x_pad, src, every.at[src])
    spread.finish()


def dense_grad(x_ref, top, low):
    return mm(x_ref[TOP_ROWS], top, TN) + mm(x_ref[LOW_ROWS], low, TN)


def write_slabs(slabs, value):
    for k in range(16):
        slabs[k // 8, k // 4 % 2, k // 2 % 2, k % 2] = value[24 * k:24 * k + 24].astype(BF16)


class DenseReduce:
    def __init__(self, at, slabs, got_c, sum_c, got_p, sum_p, got_x, sems):
        self.at, self.slabs, self.got_c, self.sum_c, self.got_p, self.sum_p, self.got_x = at, slabs, got_c, sum_c, got_p, sum_p, got_x
        self.pair = remote(slabs.at[:, 1 - at.c], got_c, sems, 0, at.to_c)
        self.plane = [remote(sum_c.at[:, z, y], got_p.at[k], sems, 1 + k, to) for k, (z, y, to) in enumerate((
            (at.z, 1 - at.y, at.to_y), (1 - at.z, at.y, at.to_z), (1 - at.z, 1 - at.y, at.to_d)))]
        self.along = remote(sum_p.at[1 - at.x], got_x, sems, 4, at.to_x)

    def start(self):
        self.pair.start()

    def to_plane(self):
        self.pair.wait_recv()
        for side in range(2):
            self.sum_c[side] = (self.slabs[side, self.at.c].astype(F32) + self.got_c[side].astype(F32)).astype(BF16)
        for copy in self.plane:
            copy.start()

    def to_x(self):
        for copy in self.plane:
            copy.wait_recv()
        for side in range(2):
            total = self.sum_c[side, self.at.z, self.at.y].astype(F32)
            for k in range(3):
                total = total + self.got_p[k, side].astype(F32)
            self.sum_p[side] = total.astype(BF16)
        self.along.start()

    def finish(self, out):
        self.along.wait_recv()
        out[...] = (self.sum_p[self.at.x].astype(F32) + self.got_x[...].astype(F32)).astype(BF16)
        for copy in [self.pair, self.along] + self.plane:
            copy.wait_send()


def dense_scratch():
    slab = lambda *lead: pltpu.VMEM(lead + (24, D), BF16)
    return [slab(2, 2, 2), slab(2, 2, 2), slab(3, 2), slab(2), slab()] + sems(5)


def turn_kernel(gx_ref, dy_ref, dense_ref, mid_ref, rank_ref, gate_ref, grads,
                grad_ref, d_pad, slabs, oa, ob, oc, later_keep, later_send,
                part, got, mix_scr, c_send, c_recv, s_send, s_recv, got_a, a_send, a_recv, got_b, b_send, b_recv,
                keep, send, got_x, x_send, x_recv, g_scr, every):
    at = Place()
    greet([at.to_y, at.to_z, at.to_c, at.to_x])
    now = Halve(at, grads, 0, got_a, (a_send, a_recv))
    later = Halve(at, grads, 2, got_b, (b_send, b_recv))
    now.start()
    collect = Collect(at, part, got, mix_scr, (c_send, c_recv))

    def slot_sum(src):
        return scatter_plain(1, rank_ref, (gx_ref,), src)

    collect.start(slot_sum)
    later.start()
    across = Across(at, now, keep, send, got_x, (x_send, x_recv))
    across.forward(0)
    collect.forward()
    across.forward(1)
    across.forward(2)
    part[0] = slot_sum(0)
    for mat in range(3):
        later.wait(mat)
        later_send[mat] = later.total(mat, 1 - at.x)
        later_keep[mat] = later.total(mat, at.x)
    top, low = collect.finish(dy_ref)
    for rows, half in ((TOP_ROWS, top), (LOW_ROWS, low)):
        g_scr[rows] = (half.astype(F32) + mm(half, dense_ref[...], NT)).astype(BF16)
    spread = Spread(at, g_scr, every, (s_send, s_recv))
    spread.start()
    grad_ref[...] = g_scr[...]
    gather_scaled(0, rank_ref, gate_ref, d_pad, 0, g_scr)
    write_slabs(slabs, dense_grad(mid_ref, top, low))
    spread.forward()
    collect.summed_gone()
    collect.drain()
    now.drain()
    later.drain()
    for src in range(1, N_EP):
        spread.arrived(src)
        if src == 3:
            across.finish((oa, ob, oc), 0)
        gather_scaled(0, rank_ref, gate_ref, d_pad, src, every.at[src])
    spread.finish()


def pair_kernel(grads, later_keep, later_send, got_b, b_send, b_recv):
    at = Place()
    greet([at.to_c])
    later = Halve(at, grads, 0, got_b, (b_send, b_recv))
    later.start()
    for mat in range(3):
        later.wait(mat)
        later_send[mat] = later.total(mat, 1 - at.x)
        later_keep[mat] = later.total(mat, at.x)
    later.drain()


def exit_kernel(gx_a, gx_b, dy_ref, dense_ref, tok_ref, slabs_two, rank_ref, grads, two_keep, two_got, da, db, dc,
                dx_ref, dense_one, dense_two, oa, ob, oc, ta, tb, tc,
                part, got, mix_scr, c_send, c_recv, got_a, a_send, a_recv, keep, send, got_x, x_send, x_recv, slabs_one, *dense):
    at = Place()
    greet([at.to_y, at.to_z, at.to_d, at.to_c, at.to_x])
    now = Halve(at, grads, 0, got_a, (a_send, a_recv))
    now.start()
    half = len(dense) // 2
    first, second = [DenseReduce(at, slabs, *dense[k * half:k * half + 5], dense[k * half + 5:k * half + 7])
                     for k, slabs in enumerate((slabs_one, slabs_two))]
    second.start()
    collect = Collect(at, part, got, mix_scr, (c_send, c_recv))

    def slot_sum(src):
        return scatter_plain(0, rank_ref, (gx_a, gx_b), src)

    collect.start(slot_sum)
    across = Across(at, now, keep, send, got_x, (x_send, x_recv))
    across.forward(0)
    collect.forward()
    second.to_plane()
    across.forward(1)
    across.forward(2)
    part[0] = slot_sum(0)
    for mat, (out, done) in enumerate(((ta, da), (tb, db), (tc, dc))):
        store_pair(out, 2, two_keep[mat], two_got[mat])
        out[0:2] = done[...]
    top, low = collect.finish(dy_ref)
    write_slabs(slabs_one, dense_grad(tok_ref, top, low))
    first.start()
    second.to_x()
    for rows, part_rows in ((TOP_ROWS, top), (LOW_ROWS, low)):
        dx_ref[rows] = (part_rows.astype(F32) + mm(part_rows, dense_ref[...], NT)).astype(BF16)
    first.to_plane()
    collect.summed_gone()
    collect.drain()
    now.drain()
    first.to_x()
    across.finish((oa, ob, oc), 0)
    second.finish(dense_two)
    first.finish(dense_one)


def store_kernel(count, keep, got, *refs):
    values, outs, made, sem = refs[:count], refs[count:2 * count], refs[-2], refs[-1]
    copies = [pltpu.make_async_copy(values[k], outs[k] if k < count - 3 else outs[k].at[2:4], sem.at[k]) for k in range(count)]
    for copy in copies:
        copy.start()
    for mat in range(3):
        store_pair(made.at[mat], 0, keep[mat], got[mat])
        copies.append(pltpu.make_async_copy(made.at[mat], outs[count - 3 + mat].at[0:2], sem.at[count + mat]))
        copies[-1].start()
    for copy in copies:
        copy.wait()


def store_all(keep, got, values):
    count = len(values)
    outs = [block(*value.shape) for value in values[:-3]] + [block(N_LOC, ROWS_DP, FF)] * 3
    return pl.pallas_call(
        functools.partial(store_kernel, count),
        out_shape=outs, in_specs=[VMEM] * (2 + count), out_specs=[ANY] * count,
        scratch_shapes=[pltpu.VMEM((3, 2, ROWS_DP, FF), BF16), pltpu.SemaphoreType.DMA((count + 3,))],
        compiler_params=pltpu.CompilerParams(vmem_limit_bytes=4 * 1024 * 1024),
        cost_estimate=pl.CostEstimate(flops=1_000_000_000, bytes_accessed=4_000_000, transcendentals=0), name='store')(keep, got, *values)


def stored(w_gate, w_up, w_down):
    return jnp.swapaxes(w_gate, 1, 2), jnp.swapaxes(w_up, 1, 2), w_down


def along_x(sent):
    return lax.ppermute(sent, 'dp', [(0, 2), (2, 0), (1, 3), (3, 1)])


def solution(mesh):
    tok_spec = P(('dp', 'ep'), None)
    exp_spec = P('ep', None, None)
    layer_specs = (P(None, None), tok_spec, tok_spec, exp_spec, exp_spec, exp_spec)
    grad_specs = (P(('dp', 'ep'), None), P('ep', 'dp', None), P('ep', 'dp', None), P('ep', None, 'dp'))

    def local_step(tokens, dy_out, dense_w1, route_idx1, route_gate1, w_gate1, w_up1, w_down1, dense_w2, route_idx2, route_gate2, w_gate2, w_up2, w_down2):
        weights_one, weights_two = stored(w_gate1, w_up1, w_down1), stored(w_gate2, w_up2, w_down2)
        tok_block, all_block = block(TOK, D), block(N_EP, TOK, D)
        padded = block(N_LOC, N_EP, CAP, D)
        every = pltpu.VMEM((N_EP, TOK, D), BF16)
        own = pltpu.VMEM((TOK, D), BF16)
        pack = jnp.concatenate([route_idx1.T.astype(F32), route_idx2.T.astype(F32), route_gate1.T, route_gate2.T], axis=0)
        mixed_one = (tokens.astype(F32) + jnp.dot(tokens, dense_w1, preferred_element_type=F32)).astype(BF16)
        x_one, rank, gate, off = call(
            entry_kernel, 'entry', 0, (mixed_one, pack),
            (padded, block(2, N_EP, 8, TOK, dtype=jnp.int32), block(2, N_EP, TOK, 8, dtype=F32), block(8, 8, dtype=jnp.int32)),
            [pltpu.VMEM((N_EP, 16, TOK), F32), every] + sems(6) + sems(3), 12)
        dy_later, x_one = lax.optimization_barrier((dy_out, x_one))
        dy_all = (dy_out,) + tuple(lax.ppermute(dy_later, 'ep', [(k, k ^ flip) for k in range(N_EP)]) for flip in (1, 2))
        outs = expert_forward(0, off, x_one, weights_one)
        mid_tok, x_two, d_two = call(middle_kernel, 'middle', 1, (outs, mixed_one, dense_w2, rank, gate) + dy_all,
                                     (tok_block, padded, padded), COLLECT_SCRATCH + [own, every] + sems(6) + [own] + sems(2), 12)
        gx, grads = expert_backward(1, 0, 4, off, x_two, d_two, weights_two)
        grad_mid, d_one, slabs, *done_two, keep_two, send_two = call(
            turn_kernel, 'turn', 2, (gx, dy_out, dense_w2, mid_tok, rank, gate, grads),
            (tok_block, padded, block(2, 2, 2, 2, 24, D)) + (block(2, ROWS_DP, FF),) * 3 + (block(*PACKED),) * 2,
            COLLECT_SCRATCH + sems(6) + HALVE_SCRATCH * 2 + ACROSS_SCRATCH + [own, every], 18)
        got_two = along_x(send_two)
        gx_a, grads = expert_backward(0, 0, 2, off, x_one, d_one, weights_one)
        keep_one, send_one = call(pair_kernel, 'pair', 4, (grads,), (block(*PACKED),) * 2, HALVE_SCRATCH, 6)
        got_two, d_one = lax.optimization_barrier((got_two, d_one))
        got_one = along_x(send_one)
        gx_b, grads = expert_backward(0, 2, 2, off, x_one, d_one, weights_one)
        grad_tok, dense_one, dense_two, *reduced = call(
            exit_kernel, 'exit', 3, (gx_a, gx_b, grad_mid, dense_w1, tokens, slabs, rank, grads, keep_two, got_two) + tuple(done_two),
            (tok_block, block(24, D), block(24, D)) + (block(2, ROWS_DP, FF),) * 3 + (block(N_LOC, ROWS_DP, FF),) * 3,
            COLLECT_SCRATCH + HALVE_SCRATCH + ACROSS_SCRATCH + [pltpu.VMEM((2, 2, 2, 2, 24, D), BF16)] + dense_scratch() * 2, 18)
        grad_tok, dense_one, dense_two, *reduced = store_all(keep_one, got_one, (grad_tok, dense_one, dense_two) + tuple(reduced[3:]) + tuple(reduced[:3]))

        def shaped(gate_up_down):
            return gate_up_down[0], gate_up_down[1], jnp.swapaxes(gate_up_down[2], 1, 2)

        return (grad_tok, dense_one) + shaped(reduced[3:]) + (dense_two,) + shaped(reduced[:3])

    return jax.shard_map(local_step, mesh=mesh, in_specs=(tok_spec, tok_spec) + layer_specs + layer_specs,
                         out_specs=(tok_spec,) + grad_specs + grad_specs, check_vma=False)
```

time: 208 us -> 193 us (0.928)
  Pallas kernels: 194 us -> 184 us
  waiting for transfers between devices: 3.47 us -> 0.5 us
    pallas_call x4, Pallas kernels: 83.4 us -> 61.9 us  [plain(): pl.pallas_call(kernel, out_shape=outs, in_specs=[SMEM] + [VMEM] * (len(in...]
    pallas_call x6, Pallas kernels: 110 us -> 122 us  [the longest x5 120 us: call(): pl.pallas_call(kernel, out_shape=outs, scratch_shapes=scratch, in_specs=[...]
    ppermute x2, waiting for transfers between devices: 3.46 us -> 0.5 us  [along_x(): return lax.ppermute(sent, 'dp', [(0, 2), (2, 0), (1, 3), (3, 1)])]
  transfers between devices with their start and end apart: 5 -> 4, of which waited for: 1 -> 1; matrix products, arithmetic and copies ran while one was open for 0% -> 0% of each run, Pallas kernels for 37% -> 35%
where the time goes in v3:
time: 193 us
  Pallas kernels  184 us (95%)
  starting transfers between devices  4.66 us (2%)
    pallas_call x5, Pallas kernels, call(): pl.pallas_call(kernel, out_shape=outs, scratch_shapes=scratch, in_specs=[...  120 us
    pallas_call x4, Pallas kernels, plain(): pl.pallas_call(kernel, out_shape=outs, in_specs=[SMEM] + [VMEM] * (len(in...  61.9 us
  transfers between devices with their start and end apart: 4, of which 1 were waited for; matrix products, arithmetic and copies ran while one was open for 0% of the time, Pallas kernels for 35%

profile of v3, /device:TPU:0, one launch (start us, length us, event | category | flops | bytes accessed | tf_op | source)
XLA Modules:
  0.0 192.9 jit_solution(1804839120712037387)
XLA Ops:
  0.6 0.7 convert_bitcast_fusion
  1.4 1.6 fusion.own.u_ref
  3.0 0.7 pad_maximum_fusion.pack_ref
  3.7 0.0 copy-start.6
  3.7 0.0 copy-start.3
  3.7 0.0 copy-start.4
  3.7 0.0 copy-start.5
  3.7 22.8 %entry.1 = (bf16[4,4,256,384]{3,2,1,0:T(8,128)(2,1)S(1)}, s32[2,4,8,512]{3,2,1,0:T(8,128)S(1)}, f32[2,4,512,8]{3,2,1,0:T(8,128)S(1)}, s32[8,8]{1,0:T(8,128)S(1)}) custom-call(bf16[512,384]{1,0:T(8,128)(2,1)S(1)} %fusion.own.u_ref, f32[16,512]{1,0:T(8,128)S(1)} %pad_maximum_fusion.pack_ref), custom_call_target="tpu_custom_call" | custom-call | flops 10000000000 | bytes 4000000 | tf_op jit(solution)/shard_map/entry/pallas_call | solution.py:373
  26.5 0.0 copy-done.6
  26.5 1.6 collective-permute-start.1
  28.1 0.5 collective-permute-start
  28.6 0.0 copy-done.3
  28.6 0.0 copy-done.4
  28.6 0.0 copy-done.5
  28.6 0.0 copy-start.8
  28.6 10.0 %expert_forward.1.o_ref = bf16[4,4,256,384]{3,2,1,0:T(8,128)(2,1)S(1)} custom-call(s32[8,8]{1,0:T(8,128)S(1)} %get-tuple-element.54.off_ref, bf16[4,4,256,384]{3,2,1,0:T(8,128)(2,1)S(1)} %get-tuple-element.56.x_ref, bf16[4,672,384]{2,1,0:T(8,128)(2,1)S(1)} %bitcast.16, bf16[4,672,384]{2,1,0:T(8,128)(2,1)S(1)} %bitcast.19, bf16[4,672,384]{2,1,0:T(8,128)(2,1)S(1)} %copy-done.5), custom_call_target="tpu_custom_call" | custom-call | flops 10000000000 | bytes 10000000 | tf_op jit(solution)/shard_map/expert_forward/pallas_call | solution.py:155
  38.6 0.0 collective-permute-done.1.dy_z
  38.6 0.0 collective-permute-done.dy_y
  38.6 0.0 copy-done.8
  38.6 0.0 copy-start
  38.6 0.0 copy-start.1
  38.6 0.0 copy-start.2
  38.6 32.7 %middle.1 = (bf16[512,384]{1,0:T(8,128)(2,1)S(1)}, bf16[4,4,256,384]{3,2,1,0:T(8,128)(2,1)S(1)}, bf16[4,4,256,384]{3,2,1,0:T(8,128)(2,1)S(1)}) custom-call(bf16[4,4,256,384]{3,2,1,0:T(8,128)(2,1)S(1)} %expert_forward.1.o_ref, bf16[512,384]{1,0:T(8,128)(2,1)S(1)} %fusion.own.u_ref, bf16[384,384]{1,0:T(8,128)(2,1)S(1)} %copy-done.8, ...), custom_call_target="tpu_custom_call" | custom-call | flops 10000000000 | bytes 4000000 | tf_op jit(solution)/shard_map/middle/pallas_call | solution.py:373
  71.3 0.0 copy-done
  71.3 0.0 copy-done.1
  71.3 0.0 copy-done.2
  71.3 25.5 %expert_backward.3 = (bf16[4,4,256,384]{3,2,1,0:T(8,128)(2,1)S(1)}, bf16[4,3,2,2,96,672]{5,4,3,2,1,0:T(8,128)(2,1)S(1)}) custom-call(s32[8,8]{1,0:T(8,128)S(1)} %get-tuple-element.54.off_ref, bf16[4,4,256,384]{3,2,1,0:T(8,128)(2,1)S(1)} %get-tuple-element.60.x_ref, bf16[4,4,256,384]{3,2,1,0:T(8,128)(2,1)S(1)} %get-tuple-element.61.d_ref, ...), custom_call_target="tpu_custom_call" | custom-call | flops 35999997952 | bytes 10000000 | tf_op jit(solution)/shard_map/expert_backward/pallas_call | solution.py:155
  96.9 33.2 %turn.1 = (bf16[512,384]{1,0:T(8,128)(2,1)S(1)}, bf16[4,4,256,384]{3,2,1,0:T(8,128)(2,1)S(1)}, bf16[2,2,2,2,24,384]{5,4,3,2,1,0:T(8,128)(2,1)S(1)}, bf16[2,96,67...) custom-call(bf16[4,4,256,384]{3,2,1,0:T(8,128)(2,1)S(1)} %get-tuple-, ...), custom_call_target="tpu_custom_call" | custom-call | flops 10000000000 | bytes 4000000 | tf_op jit(solution)/shard_map/turn/pallas_call | solution.py:373
  130.1 2.5 %collective-permute-start.3 = (bf16[3,96,1344]{2,1,0:T(8,128)(2,1)S(1)}, bf16[3,96,1344]{2,1,0:T(8,128)(2,1)S(1)}, u32[]{:S(2)}, u32[]{:S(2)}) collective-permute-start(bf16[3,96,1344]{2,1,0:T(8,128)(2,1)S(1)} %get-tuple-element.70), channel_id=1, source_target_pairs={{0,2},{2,0},{1,3},{3,1},{4,6},{6,4},{5,7},{7,5},{8,10},{10,8},{9,1... | collective-permute-start | bytes 2322440 | tf_op jit(solution)/shard_map/ppermute | solution.py:628
  132.6 12.2 %expert_backward.4 = (bf16[2,4,256,384]{3,2,1,0:T(8,128)(2,1)S(1)}, bf16[2,3,2,2,96,672]{5,4,3,2,1,0:T(8,128)(2,1)S(1)}) custom-call(s32[8,8]{1,0:T(8,128)S(1)} %get-tuple-element.54.off_ref, bf16[4,4,256,384]{3,2,1,0:T(8,128)(2,1)S(1)} %get-tuple-element.56.x_ref, bf16[4,4,256,384]{3,2,1,0:T(8,128)(2,1)S(1)} %get-tuple-element.71.d_ref, ...), custom_call_target="tpu_custom_call" | custom-call | flops 17999998976 | bytes 10000000 | tf_op jit(solution)/shard_map/expert_backward/pallas_call | solution.py:155
  144.8 4.0 %pair.1 = (bf16[3,96,1344]{2,1,0:T(8,128)(2,1)S(1)}, bf16[3,96,1344]{2,1,0:T(8,128)(2,1)S(1)}) custom-call(bf16[2,3,2,2,96,672]{5,4,3,2,1,0:T(8,128)(2,1)S(1)} %get-tuple-element.66.grads), custom_call_target="tpu_custom_call" | custom-call | flops 10000000000 | bytes 4000000 | tf_op jit(solution)/shard_map/pair/pallas_call | solution.py:373
  148.8 0.0 copy-start.7
  148.9 0.0 copy-start.9
  148.9 0.1 collective-permute-start.2
  148.9 0.5 collective-permute-done.3.two_got
  149.4 14.2 %expert_backward.5 = (bf16[2,4,256,384]{3,2,1,0:T(8,128)(2,1)S(1)}, bf16[2,3,2,2,96,672]{5,4,3,2,1,0:T(8,128)(2,1)S(1)}) custom-call(s32[8,8]{1,0:T(8,128)S(1)} %get-tuple-element.54.off_ref, bf16[4,4,256,384]{3,2,1,0:T(8,128)(2,1)S(1)} %get-tuple-element.56.x_ref, bf16[4,4,256,384]{3,2,1,0:T(8,128)(2,1)S(1)} %get-tuple-element.71.d_ref, ...), custom_call_target="tpu_custom_call" | custom-call | flops 17999998976 | bytes 10000000 | tf_op jit(solution)/shard_map/expert_backward/pallas_call | solution.py:155
  163.7 0.0 copy-done.7
  163.7 0.0 copy-done.9
  163.7 26.9 %exit.1 = (bf16[512,384]{1,0:T(8,128)(2,1)S(1)}, bf16[24,384]{1,0:T(8,128)(2,1)S(1)}, bf16[24,384]{1,0:T(8,128)(2,1)S(1)}, bf16[2,96,672]{2,1,0:T(8,128)(2,1)S(1...) custom-call(bf16[2,4,256,384]{3,2,1,0:T(8,128)(2,1)S(1)} %get-tuple-, ...), custom_call_target="tpu_custom_call" | custom-call | flops 10000000000 | bytes 4000000 | tf_op jit(solution)/shard_map/exit/pallas_call | solution.py:373
  190.6 0.0 collective-permute-done.2.got
  190.6 2.0 %store.1 = (bf16[512,384]{1,0:T(8,128)(2,1)}, bf16[24,384]{1,0:T(8,128)(2,1)}, bf16[24,384]{1,0:T(8,128)(2,1)}, bf16[4,96,672]{2,1,0:T(8,128)(2,1)}, bf16[4,96,6...) custom-call(bf16[3,96,1344]{2,1,0:T(8,128)(2,1)S(1)} %get-tuple-elem, ...), custom_call_target="tpu_custom_call" | custom-call | flops 1000000000 | bytes 4000000 | tf_op jit(solution)/shard_map/store/pallas_call | solution.py:615
Async XLA Ops:
  3.7 22.8 %copy-start.6 = (bf16[512,384]{1,0:T(8,128)(2,1)S(1)}, bf16[512,384]{1,0:T(8,128)(2,1)}, u32[]{:S(2)}) copy-start(bf16[512,384]{1,0:T(8,128)(2,1)} %dy_ref.1) | copy-start | bytes 1179652
  3.7 24.9 %copy-start.3 = (bf16[4,384,672]{1,2,0:T(8,128)(2,1)S(1)}, bf16[4,384,672]{1,2,0:T(8,128)(2,1)}, u32[]{:S(2)}) copy-start(bf16[4,384,672]{1,2,0:T(8,128)(2,1)} %param.19) | copy-start | bytes 6193156
  3.7 24.9 %copy-start.4 = (bf16[4,384,672]{1,2,0:T(8,128)(2,1)S(1)}, bf16[4,384,672]{1,2,0:T(8,128)(2,1)}, u32[]{:S(2)}) copy-start(bf16[4,384,672]{1,2,0:T(8,128)(2,1)} %param.20) | copy-start | bytes 6193156
  3.7 24.9 %copy-start.5 = (bf16[4,672,384]{2,1,0:T(8,128)(2,1)S(1)}, bf16[4,672,384]{2,1,0:T(8,128)(2,1)}, u32[]{:S(2)}) copy-start(bf16[4,672,384]{2,1,0:T(8,128)(2,1)} %wd_ref.7) | copy-start | bytes 6193156
  26.5 12.0 %collective-permute-start.1 = (bf16[512,384]{1,0:T(8,128)(2,1)S(1)}, bf16[512,384]{1,0:T(8,128)(2,1)S(1)}, u32[]{:S(2)}, u32[]{:S(2)}) collective-permute-start(bf16[512,384]{1,0:T(8,128)(2,1)S(1)} %copy-done.6), channel_id=1, source_target_pairs={{0,8},{4,12},{8,0},{12,4},{1,9},{5,13},{9,1},{13,5},{2,10},{6,14},... | collective-permute-start | bytes 1179656 | tf_op jit(solution)/shard_map/ppermute | solution.py:650
  28.1 10.5 %collective-permute-start = (bf16[512,384]{1,0:T(8,128)(2,1)S(1)}, bf16[512,384]{1,0:T(8,128)(2,1)S(1)}, u32[]{:S(2)}, u32[]{:S(2)}) collective-permute-start(bf16[512,384]{1,0:T(8,128)(2,1)S(1)} %copy-done.6), channel_id=1, source_target_pairs={{0,4},{4,0},{8,12},{12,8},{1,5},{5,1},{9,13},{13,9},{2,6},{6,2},{1... | collective-permute-start | bytes 1179656 | tf_op jit(solution)/shard_map/ppermute | solution.py:650
  28.6 10.0 %copy-start.8 = (bf16[384,384]{1,0:T(8,128)(2,1)S(1)}, bf16[384,384]{1,0:T(8,128)(2,1)}, u32[]{:S(2)}) copy-start(bf16[384,384]{1,0:T(8,128)(2,1)} %dense_ref.4) | copy-start | bytes 884740
  38.6 32.7 %copy-start = (bf16[4,384,672]{1,2,0:T(8,128)(2,1)S(1)}, bf16[4,384,672]{1,2,0:T(8,128)(2,1)}, u32[]{:S(2)}) copy-start(bf16[4,384,672]{1,2,0:T(8,128)(2,1)} %param.25) | copy-start | bytes 6193156
  38.6 32.7 %copy-start.1 = (bf16[4,384,672]{1,2,0:T(8,128)(2,1)S(1)}, bf16[4,384,672]{1,2,0:T(8,128)(2,1)}, u32[]{:S(2)}) copy-start(bf16[4,384,672]{1,2,0:T(8,128)(2,1)} %param.26) | copy-start | bytes 6193156
  38.6 32.7 %copy-start.2 = (bf16[4,672,384]{2,1,0:T(8,128)(2,1)S(1)}, bf16[4,672,384]{2,1,0:T(8,128)(2,1)}, u32[]{:S(2)}) copy-start(bf16[4,672,384]{2,1,0:T(8,128)(2,1)} %wd_ref.5) | copy-start | bytes 6193156
  130.1 19.4 %collective-permute-start.3 = (bf16[3,96,1344]{2,1,0:T(8,128)(2,1)S(1)}, bf16[3,96,1344]{2,1,0:T(8,128)(2,1)S(1)}, u32[]{:S(2)}, u32[]{:S(2)}) collective-permute-start(bf16[3,96,1344]{2,1,0:T(8,128)(2,1)S(1)} %get-tuple-element.70), channel_id=1, source_target_pairs={{0,2},{2,0},{1,3},{3,1},{4,6},{6,4},{5,7},{7,5},{8,10},{10,8},{9,1... | collective-permute-start | bytes 2322440 | tf_op jit(solution)/shard_map/ppermute | solution.py:628
  148.8 14.8 %copy-start.7 = (bf16[512,384]{1,0:T(8,128)(2,1)S(1)}, bf16[512,384]{1,0:T(8,128)(2,1)}, u32[]{:S(2)}) copy-start(bf16[512,384]{1,0:T(8,128)(2,1)} %tok_ref.1) | copy-start | bytes 1179652
  148.9 14.8 %copy-start.9 = (bf16[384,384]{1,0:T(8,128)(2,1)S(1)}, bf16[384,384]{1,0:T(8,128)(2,1)}, u32[]{:S(2)}) copy-start(bf16[384,384]{1,0:T(8,128)(2,1)} %dense_ref.5) | copy-start | bytes 884740
  148.9 41.8 %collective-permute-start.2 = (bf16[3,96,1344]{2,1,0:T(8,128)(2,1)S(1)}, bf16[3,96,1344]{2,1,0:T(8,128)(2,1)S(1)}, u32[]{:S(2)}, u32[]{:S(2)}) collective-permute-start(bf16[3,96,1344]{2,1,0:T(8,128)(2,1)S(1)} %get-tuple-element.68), channel_id=1, source_target_pairs={{0,2},{2,0},{1,3},{3,1},{4,6},{6,4},{5,7},{7,5},{8,10},{10,8},{9,1... | collective-permute-start | bytes 2322440 | tf_op jit(solution)/shard_map/ppermute | solution.py:628

commit v4 on v3

--- a/solution.py
+++ b/solution.py
@@ -62,7 +62,7 @@
             off_ref[layer * N_LOC + exp, 4] = halves // 2
             off_ref[layer * N_LOC + exp, 5] = halves % 2
             off_ref[layer * N_LOC + exp, 6] = halves * (CAP // 2)
-            off_ref[layer * N_LOC + exp, 7] = (halves + 1) // 2
+            off_ref[layer * N_LOC + exp, 7] = jnp.maximum((halves + 1) // 2, 2)
 
 
 def pick(layer, rank_ref, src, exp):
@@ -163,12 +163,15 @@
                  [pltpu.VMEM((SLOTS, D), BF16)] * 2, 8, 10_000_000_000)
 
 
-def backward_kernel(layer, first, count, off_ref, x_ref, d_ref, wg_ref, wu_ref, wd_ref, out_ref, grad_ref, left, right, gx_scr):
-    x_scr, d_scr = left.at[0], left.at[1]
+def backward_kernel(layer, first, count, done, off_ref, x_ref, d_ref, wg_ref, wu_ref, wd_ref, out_ref, *refs):
+    grad_ref = refs[0] if done else None
+    left, right, gx_scr = refs[-3:]
 
     @pl.loop(first, first + count)
     def _(exp):
         row = layer * N_LOC + exp
+        slot = jnp.maximum(exp - first - done, 0)
+        x_scr, d_scr = left.at[slot, 0], left.at[slot, 1]
         packed(off_ref, row, x_ref, exp, x_scr)
         packed(off_ref, row, d_ref, exp, d_scr)
 
@@ -181,35 +184,52 @@
             swish = a_pre * sigma
             grad_a = (grad_h * b_pre * sigma * (1.0 + a_pre * (1.0 - sigma))).astype(BF16)
             grad_b = (grad_h * swish).astype(BF16)
-            right[0, rows, :] = grad_a
-            right[1, rows, :] = grad_b
-            right[2, rows, :] = (swish * b_pre).astype(BF16)
+            right[slot, 0, rows, :] = grad_a
+            right[slot, 1, rows, :] = grad_b
+            right[slot, 2, rows, :] = (swish * b_pre).astype(BF16)
             gx_scr[rows, :] = (mm(grad_a, wg_ref[exp]) + mm(grad_b, wu_ref[exp])).astype(BF16)
 
         over_rows(off_ref, row, step)
         gx_scr[tail_of(off_ref, row, CAP), :] = jnp.zeros((CAP, D), BF16)
         unpacked(off_ref, row, gx_scr, out_ref, exp - first)
-        right[:, tail_of(off_ref, row, CAP // 2), :] = jnp.zeros((3, CAP // 2, FF), BF16)
-
-        def weight_grads(depth):
-            @pl.loop(0, 3)
-            def _(mat):
-                grad = mm(left[mat // 2, 0:depth, :], right[mat, 0:depth, :], TN).astype(BF16)
-                for owner in range(4):
-                    grad_ref[exp - first, mat, owner // 2, owner % 2] = grad[ROWS_DP * owner:ROWS_DP * owner + ROWS_DP]
-
-        for blocks in range(1, 5):
-            pl.when(off_ref[row, 7] == blocks)(functools.partial(weight_grads, blocks * CAP))
-
-        @pl.when(off_ref[row, 7] == 0)
-        def _():
-            grad_ref[exp - first] = jnp.zeros(grad_ref.shape[1:], BF16)
-
-
-def expert_backward(layer, first, count, off, x_pad, d_pad, weights):
-    return plain(functools.partial(backward_kernel, layer, first, count), 'expert_backward',
-                 (off, x_pad, d_pad) + weights, (block(count, N_EP, CAP, D), block(count, 3, 2, 2, ROWS_DP, FF)),
-                 [pltpu.VMEM((2, SLOTS, D), BF16), pltpu.VMEM((3, N_EP * CAP + CAP // 2, FF), BF16), pltpu.VMEM((SLOTS, D), BF16)], 14, 9_000_000_000 * count)
+        depth, half = off_ref[row, 7], CAP // 2
+        made_here = exp < first + done
+
+        @pl.loop(off_ref[row, 4] * 2 + off_ref[row, 5], jnp.where(made_here, depth * 2, N_EP * 2))
+        def _(k):
+            rows = pl.ds(pl.multiple_of(k * half, half), half)
+            right[slot, :, rows, :] = jnp.zeros((3, half, FF), BF16)
+            left[slot, :, rows, :] = jnp.zeros((2, half, D), BF16)
+
+        if done:
+            for blocks in range(2, 5):
+                pl.when(jnp.logical_and(made_here, depth == blocks))(
+                    functools.partial(weight_grads, left, right, slot, grad_ref, exp - first, blocks * CAP))
+
+
+def weight_grads(left, right, slot, grad_ref, exp, depth):
+    @pl.loop(0, 3)
+    def _(mat):
+        grad = mm(left[slot, mat // 2, 0:depth, :], right[slot, mat, 0:depth, :], TN).astype(BF16)
+        for owner in range(4):
+            grad_ref[exp, mat, owner // 2, owner % 2] = grad[ROWS_DP * owner:ROWS_DP * owner + ROWS_DP]
+
+
+def grads_shape(count):
+    return (count, 3, 2, 2, ROWS_DP, FF)
+
+
+def expert_backward(layer, first, count, done, off, x_pad, d_pad, weights):
+    slots = max(count - done, 1)
+    factors = ((slots, 2, SLOTS, D), (slots, 3, N_EP * CAP, FF))
+    outs = (block(count, N_EP, CAP, D),) + ((block(*grads_shape(done)),) if done else ())
+    scratch = [pltpu.VMEM((SLOTS, D), BF16)]
+    if count > done:
+        outs += tuple(block(*shape) for shape in factors)
+    else:
+        scratch = [pltpu.VMEM(shape, BF16) for shape in factors] + scratch
+    return plain(functools.partial(backward_kernel, layer, first, count, done), 'expert_backward',
+                 (off, x_pad, d_pad) + weights, outs, scratch, 12 if count == done else 6, 9_000_000_000 * count)
 
 
 def remote(src, dst, sems, slot, target):
@@ -237,17 +257,20 @@
 
 
 HALF = TOK // 2
-TOP_ROWS, LOW_ROWS = pl.ds(0, HALF), pl.ds(HALF, HALF)
+QUARTER = TOK // 4
+SETS = (pl.ds(0, HALF), pl.ds(HALF, HALF))
 
 
 class Spread:
-    def __init__(self, at, own, every, sems):
-        self.direct = [remote(own.at[TOP_ROWS], every.at[1, TOP_ROWS], sems, 0, at.to_y),
-                       remote(own.at[LOW_ROWS], every.at[2, LOW_ROWS], sems, 1, at.to_z),
-                       remote(own.at[LOW_ROWS], every.at[1, LOW_ROWS], sems, 2, at.to_y),
-                       remote(own.at[TOP_ROWS], every.at[2, TOP_ROWS], sems, 3, at.to_z)]
-        self.onward = [remote(every.at[1, TOP_ROWS], every.at[3, TOP_ROWS], sems, 4, at.to_z),
-                       remote(every.at[2, LOW_ROWS], every.at[3, LOW_ROWS], sems, 5, at.to_y)]
+    def __init__(self, at, own, every, sems, k):
+        top, low = pl.ds(HALF * k, QUARTER), pl.ds(HALF * k + QUARTER, QUARTER)
+        first = 6 * k
+        self.direct = [remote(own.at[top], every.at[1, top], sems, first, at.to_y),
+                       remote(own.at[low], every.at[2, low], sems, first + 1, at.to_z),
+                       remote(own.at[low], every.at[1, low], sems, first + 2, at.to_y),
+                       remote(own.at[top], every.at[2, top], sems, first + 3, at.to_z)]
+        self.onward = [remote(every.at[1, top], every.at[3, top], sems, first + 4, at.to_z),
+                       remote(every.at[2, low], every.at[3, low], sems, first + 5, at.to_y)]
 
     def start(self):
         for copy in self.direct:
@@ -267,38 +290,52 @@
             copy.wait_send()
 
 
+class Both:
+    def __init__(self, first, second):
+        self.sets = (first, second)
+
+    def __getattr__(self, name):
+        def each(*args):
+            for one in self.sets:
+                getattr(one, name)(*args)
+        return each
+
+
 class Collect:
-    def __init__(self, at, part, got, mix_scr, sems):
-        self.part, self.got, self.mix_scr = part, got, mix_scr
-        self.direct = [remote(part.at[3, TOP_ROWS], got.at[0], sems, 0, at.to_y),
-                       remote(part.at[3, LOW_ROWS], got.at[1], sems, 1, at.to_z),
-                       remote(part.at[1, TOP_ROWS], got.at[2], sems, 2, at.to_y),
-                       remote(part.at[2, LOW_ROWS], got.at[3], sems, 3, at.to_z)]
-        self.summed = [remote(mix_scr.at[0], got.at[4], sems, 4, at.to_z),
-                       remote(mix_scr.at[1], got.at[5], sems, 5, at.to_y)]
-
-    def start(self, slot_sum):
-        self.part[3] = slot_sum(3)
+    def __init__(self, at, part, got, mix_scr, sems, k):
+        self.part, self.got, self.mix_scr, self.k = part, got, mix_scr, k
+        self.top, self.low = pl.ds(HALF * k, QUARTER), pl.ds(HALF * k + QUARTER, QUARTER)
+        self.first = first = 6 * k
+        self.direct = [remote(part.at[3, self.top], got.at[first], sems, first, at.to_y),
+                       remote(part.at[3, self.low], got.at[first + 1], sems, first + 1, at.to_z),
+                       remote(part.at[1, self.top], got.at[first + 2], sems, first + 2, at.to_y),
+                       remote(part.at[2, self.low], got.at[first + 3], sems, first + 3, at.to_z)]
+        self.summed = [remote(mix_scr.at[2 * k], got.at[first + 4], sems, first + 4, at.to_z),
+                       remote(mix_scr.at[2 * k + 1], got.at[first + 5], sems, first + 5, at.to_y)]
+
+    def far(self):
         self.direct[0].start()
         self.direct[1].start()
-        self.part[1] = slot_sum(1)
+
+    def near_y(self):
         self.direct[2].start()
-        self.part[2] = slot_sum(2)
+
+    def near_z(self):
         self.direct[3].start()
 
     def forward(self):
-        for step, (slot, rows) in enumerate(((2, TOP_ROWS), (1, LOW_ROWS))):
+        for step, (slot, rows) in enumerate(((2, self.top), (1, self.low))):
             self.direct[step].wait_recv()
-            self.mix_scr[step] = (self.part[slot, rows].astype(F32) + self.got[step].astype(F32)).astype(BF16)
+            self.mix_scr[2 * self.k + step] = (self.part[slot, rows].astype(F32) + self.got[self.first + step].astype(F32)).astype(BF16)
             self.summed[step].start()
 
     def finish(self, base):
         for copy in self.direct[2:] + self.summed:
             copy.wait_recv()
-        got = self.got
-        top = self.part[0, TOP_ROWS].astype(F32) + got[2].astype(F32) + got[4].astype(F32)
-        low = self.part[0, LOW_ROWS].astype(F32) + got[3].astype(F32) + got[5].astype(F32)
-        return (base[TOP_ROWS].astype(F32) + top).astype(BF16), (base[LOW_ROWS].astype(F32) + low).astype(BF16)
+        got, first = self.got, self.first
+        top = self.part[0, self.top].astype(F32) + got[first + 2].astype(F32) + got[first + 4].astype(F32)
+        low = self.part[0, self.low].astype(F32) + got[first + 3].astype(F32) + got[first + 5].astype(F32)
+        return (base[SETS[self.k]].astype(F32) + jnp.concatenate([top, low], axis=0)).astype(BF16)
 
     def summed_gone(self):
         for copy in self.summed:
@@ -307,6 +344,21 @@
     def drain(self):
         for copy in self.direct:
             copy.wait_send()
+
+
+def start_collect(at, part, got, mix_scr, sems, slot_sum):
+    both = Both(*[Collect(at, part, got, mix_scr, sems, k) for k in range(2)])
+    part[3] = slot_sum(3)
+    both.far()
+    part[1] = slot_sum(1)
+    both.near_y()
+    part[2] = slot_sum(2)
+    both.near_z()
+    return both
+
+
+def spread_of(at, own, every, sems):
+    return Both(*[Spread(at, own, every, sems, k) for k in range(2)])
 
 
 class Halve:
@@ -314,8 +366,8 @@
         self.at, self.grads, self.first, self.got = at, grads, first, got
         self.pair = [remote(grads.at[first + k % 2, k // 2, :, 1 - at.c], got.at[k], sems, k, at.to_c) for k in range(6)]
 
-    def start(self):
-        for copy in self.pair:
+    def start(self, exp):
+        for copy in self.pair[exp::2]:
             copy.start()
 
     def total(self, mat, side):
@@ -361,7 +413,7 @@
 
 
 PACKED = (3, ROWS_DP, 2 * FF)
-COLLECT_SCRATCH = [pltpu.VMEM((N_EP, TOK, D), BF16), pltpu.VMEM((6, HALF, D), BF16), pltpu.VMEM((2, HALF, D), BF16)] + sems(6)
+COLLECT_SCRATCH = [pltpu.VMEM((N_EP, TOK, D), BF16), pltpu.VMEM((12, QUARTER, D), BF16), pltpu.VMEM((4, QUARTER, D), BF16)] + sems(12)
 HALVE_SCRATCH = [pltpu.VMEM((6, 2, ROWS_DP, FF), BF16)] + sems(6)
 ACROSS_SCRATCH = [pltpu.VMEM(PACKED, BF16)] * 3 + sems(3)
 
@@ -386,7 +438,7 @@
              remote(packs.at[1], packs.at[3], (p_send, p_recv), 2, at.to_z)]
     small[0].start()
     small[1].start()
-    spread = Spread(at, own, every, (s_send, s_recv))
+    spread = spread_of(at, own, every, (s_send, s_recv))
     spread.start()
     packs[0] = pack_ref[...]
     small[0].wait_recv()
@@ -408,28 +460,26 @@
                   part, got, mix_scr, c_send, c_recv, u_scr, every, s_send, s_recv, dy_d, d_send, d_recv):
     at = Place()
     greet([at.to_y, at.to_z])
-    collect = Collect(at, part, got, mix_scr, (c_send, c_recv))
 
     def slot_sum(src):
         return scatter_gated(0, rank_ref, gate_ref, o_ref, src)
 
-    collect.start(slot_sum)
+    collect = start_collect(at, part, got, mix_scr, (c_send, c_recv), slot_sum)
     collect.forward()
-    onward = [remote(dy_y.at[TOP_ROWS], dy_d.at[TOP_ROWS], (d_send, d_recv), 0, at.to_z),
-              remote(dy_z.at[LOW_ROWS], dy_d.at[LOW_ROWS], (d_send, d_recv), 1, at.to_y)]
+    onward = [remote(dy_y.at[SETS[0]], dy_d.at[SETS[0]], (d_send, d_recv), 0, at.to_z),
+              remote(dy_z.at[SETS[1]], dy_d.at[SETS[1]], (d_send, d_recv), 1, at.to_y)]
     part[0] = slot_sum(0)
     for src, dy_ref in ((0, dy_own), (1, dy_y)):
         gather_scaled(1, rank_ref, gate_ref, d_pad, src, dy_ref)
     collect.summed_gone()
     for copy in onward:
         copy.start()
-    top, low = collect.finish(u_ref)
-    for rows, half in ((TOP_ROWS, top), (LOW_ROWS, low)):
-        u_scr[rows] = (half.astype(F32) + mm(half, dense_ref[...])).astype(BF16)
-    spread = Spread(at, u_scr, every, (s_send, s_recv))
-    spread.start()
-    mid_ref[TOP_ROWS] = top
-    mid_ref[LOW_ROWS] = low
+    spread = spread_of(at, u_scr, every, (s_send, s_recv))
+    for k, rows in enumerate(SETS):
+        mid = collect.sets[k].finish(u_ref)
+        u_scr[rows] = (mid.astype(F32) + mm(mid, dense_ref[...])).astype(BF16)
+        spread.sets[k].start()
+        mid_ref[rows] = mid
     gather_rows(1, rank_ref, x_pad, 0, u_scr)
     gather_scaled(1, rank_ref, gate_ref, d_pad, 2, dy_z)
     spread.forward()
@@ -445,8 +495,8 @@
     spread.finish()
 
 
-def dense_grad(x_ref, top, low):
-    return mm(x_ref[TOP_ROWS], top, TN) + mm(x_ref[LOW_ROWS], low, TN)
+def dense_grad(x_ref, halves):
+    return mm(x_ref[SETS[0]], halves[0], TN) + mm(x_ref[SETS[1]], halves[1], TN)
 
 
 def write_slabs(slabs, value):
@@ -494,41 +544,44 @@
     return [slab(2, 2, 2), slab(2, 2, 2), slab(3, 2), slab(2), slab()] + sems(5)
 
 
-def turn_kernel(gx_ref, dy_ref, dense_ref, mid_ref, rank_ref, gate_ref, grads,
+def turn_kernel(gx_ref, dy_ref, dense_ref, mid_ref, rank_ref, gate_ref, grads, left, right,
                 grad_ref, d_pad, slabs, oa, ob, oc, later_keep, later_send,
                 part, got, mix_scr, c_send, c_recv, s_send, s_recv, got_a, a_send, a_recv, got_b, b_send, b_recv,
-                keep, send, got_x, x_send, x_recv, g_scr, every):
+                keep, send, got_x, x_send, x_recv, g_scr, every, later_grads):
     at = Place()
     greet([at.to_y, at.to_z, at.to_c, at.to_x])
     now = Halve(at, grads, 0, got_a, (a_send, a_recv))
-    later = Halve(at, grads, 2, got_b, (b_send, b_recv))
-    now.start()
-    collect = Collect(at, part, got, mix_scr, (c_send, c_recv))
+    later = Halve(at, later_grads, 0, got_b, (b_send, b_recv))
+    now.start(0)
+    now.start(1)
 
     def slot_sum(src):
         return scatter_plain(1, rank_ref, (gx_ref,), src)
 
-    collect.start(slot_sum)
-    later.start()
+    collect = start_collect(at, part, got, mix_scr, (c_send, c_recv), slot_sum)
     across = Across(at, now, keep, send, got_x, (x_send, x_recv))
     across.forward(0)
     collect.forward()
     across.forward(1)
     across.forward(2)
     part[0] = slot_sum(0)
+    for exp in range(2):
+        weight_grads(left, right, exp, later_grads, exp, N_EP * CAP)
+        later.start(exp)
+    spread = spread_of(at, g_scr, every, (s_send, s_recv))
+    halves = []
+    for k, rows in enumerate(SETS):
+        halves.append(collect.sets[k].finish(dy_ref))
+        g_scr[rows] = (halves[k].astype(F32) + mm(halves[k], dense_ref[...], NT)).astype(BF16)
+        spread.sets[k].start()
+        grad_ref[rows] = g_scr[rows]
+    gather_scaled(0, rank_ref, gate_ref, d_pad, 0, g_scr)
+    write_slabs(slabs, dense_grad(mid_ref, halves))
+    spread.forward()
     for mat in range(3):
         later.wait(mat)
         later_send[mat] = later.total(mat, 1 - at.x)
         later_keep[mat] = later.total(mat, at.x)
-    top, low = collect.finish(dy_ref)
-    for rows, half in ((TOP_ROWS, top), (LOW_ROWS, low)):
-        g_scr[rows] = (half.astype(F32) + mm(half, dense_ref[...], NT)).astype(BF16)
-    spread = Spread(at, g_scr, every, (s_send, s_recv))
-    spread.start()
-    grad_ref[...] = g_scr[...]
-    gather_scaled(0, rank_ref, gate_ref, d_pad, 0, g_scr)
-    write_slabs(slabs, dense_grad(mid_ref, top, low))
-    spread.forward()
     collect.summed_gone()
     collect.drain()
     now.drain()
@@ -545,7 +598,8 @@
     at = Place()
     greet([at.to_c])
     later = Halve(at, grads, 0, got_b, (b_send, b_recv))
-    later.start()
+    later.start(0)
+    later.start(1)
     for mat in range(3):
         later.wait(mat)
         later_send[mat] = later.total(mat, 1 - at.x)
@@ -559,17 +613,17 @@
     at = Place()
     greet([at.to_y, at.to_z, at.to_d, at.to_c, at.to_x])
     now = Halve(at, grads, 0, got_a, (a_send, a_recv))
-    now.start()
+    now.start(0)
+    now.start(1)
     half = len(dense) // 2
     first, second = [DenseReduce(at, slabs, *dense[k * half:k * half + 5], dense[k * half + 5:k * half + 7])
                      for k, slabs in enumerate((slabs_one, slabs_two))]
     second.start()
-    collect = Collect(at, part, got, mix_scr, (c_send, c_recv))
 
     def slot_sum(src):
         return scatter_plain(0, rank_ref, (gx_a, gx_b), src)
 
-    collect.start(slot_sum)
+    collect = start_collect(at, part, got, mix_scr, (c_send, c_recv), slot_sum)
     across = Across(at, now, keep, send, got_x, (x_send, x_recv))
     across.forward(0)
     collect.forward()
@@ -580,12 +634,12 @@
     for mat, (out, done) in enumerate(((ta, da), (tb, db), (tc, dc))):
         store_pair(out, 2, two_keep[mat], two_got[mat])
         out[0:2] = done[...]
-    top, low = collect.finish(dy_ref)
-    write_slabs(slabs_one, dense_grad(tok_ref, top, low))
+    halves = [one.finish(dy_ref) for one in collect.sets]
+    write_slabs(slabs_one, dense_grad(tok_ref, halves))
     first.start()
     second.to_x()
-    for rows, part_rows in ((TOP_ROWS, top), (LOW_ROWS, low)):
-        dx_ref[rows] = (part_rows.astype(F32) + mm(part_rows, dense_ref[...], NT)).astype(BF16)
+    for rows, half_rows in zip(SETS, halves):
+        dx_ref[rows] = (half_rows.astype(F32) + mm(half_rows, dense_ref[...], NT)).astype(BF16)
     first.to_plane()
     collect.summed_gone()
     collect.drain()
@@ -645,27 +699,27 @@
         x_one, rank, gate, off = call(
             entry_kernel, 'entry', 0, (mixed_one, pack),
             (padded, block(2, N_EP, 8, TOK, dtype=jnp.int32), block(2, N_EP, TOK, 8, dtype=F32), block(8, 8, dtype=jnp.int32)),
-            [pltpu.VMEM((N_EP, 16, TOK), F32), every] + sems(6) + sems(3), 12)
+            [pltpu.VMEM((N_EP, 16, TOK), F32), every] + sems(12) + sems(3), 12)
         dy_later, x_one = lax.optimization_barrier((dy_out, x_one))
         dy_all = (dy_out,) + tuple(lax.ppermute(dy_later, 'ep', [(k, k ^ flip) for k in range(N_EP)]) for flip in (1, 2))
         outs = expert_forward(0, off, x_one, weights_one)
         mid_tok, x_two, d_two = call(middle_kernel, 'middle', 1, (outs, mixed_one, dense_w2, rank, gate) + dy_all,
-                                     (tok_block, padded, padded), COLLECT_SCRATCH + [own, every] + sems(6) + [own] + sems(2), 12)
-        gx, grads = expert_backward(1, 0, 4, off, x_two, d_two, weights_two)
+                                     (tok_block, padded, padded), COLLECT_SCRATCH + [own, every] + sems(12) + [own] + sems(2), 9)
+        gx, grads, left, right = expert_backward(1, 0, 4, 2, off, x_two, d_two, weights_two)
         grad_mid, d_one, slabs, *done_two, keep_two, send_two = call(
-            turn_kernel, 'turn', 2, (gx, dy_out, dense_w2, mid_tok, rank, gate, grads),
+            turn_kernel, 'turn', 2, (gx, dy_out, dense_w2, mid_tok, rank, gate, grads, left, right),
             (tok_block, padded, block(2, 2, 2, 2, 24, D)) + (block(2, ROWS_DP, FF),) * 3 + (block(*PACKED),) * 2,
-            COLLECT_SCRATCH + sems(6) + HALVE_SCRATCH * 2 + ACROSS_SCRATCH + [own, every], 18)
+            COLLECT_SCRATCH + sems(12) + HALVE_SCRATCH * 2 + ACROSS_SCRATCH + [own, every, pltpu.VMEM(grads_shape(2), BF16)], 17)
         got_two = along_x(send_two)
-        gx_a, grads = expert_backward(0, 0, 2, off, x_one, d_one, weights_one)
+        gx_a, grads = expert_backward(0, 0, 2, 2, off, x_one, d_one, weights_one)
         keep_one, send_one = call(pair_kernel, 'pair', 4, (grads,), (block(*PACKED),) * 2, HALVE_SCRATCH, 6)
         got_two, d_one = lax.optimization_barrier((got_two, d_one))
         got_one = along_x(send_one)
-        gx_b, grads = expert_backward(0, 2, 2, off, x_one, d_one, weights_one)
+        gx_b, grads = expert_backward(0, 2, 2, 2, off, x_one, d_one, weights_one)
         grad_tok, dense_one, dense_two, *reduced = call(
             exit_kernel, 'exit', 3, (gx_a, gx_b, grad_mid, dense_w1, tokens, slabs, rank, grads, keep_two, got_two) + tuple(done_two),
             (tok_block, block(24, D), block(24, D)) + (block(2, ROWS_DP, FF),) * 3 + (block(N_LOC, ROWS_DP, FF),) * 3,
-            COLLECT_SCRATCH + HALVE_SCRATCH + ACROSS_SCRATCH + [pltpu.VMEM((2, 2, 2, 2, 24, D), BF16)] + dense_scratch() * 2, 18)
+            COLLECT_SCRATCH + HALVE_SCRATCH + ACROSS_SCRATCH + [pltpu.VMEM((2, 2, 2, 2, 24, D), BF16)] + dense_scratch() * 2, 14)
         grad_tok, dense_one, dense_two, *reduced = store_all(keep_one, got_one, (grad_tok, dense_one, dense_two) + tuple(reduced[3:]) + tuple(reduced[:3]))
 
         def shaped(gate_up_down):

time: 193 us -> 189 us (0.979)
  Pallas kernels: 184 us -> 181 us
  starting transfers between devices: 4.66 us -> 2.17 us
    pallas_call x4, Pallas kernels: 61.9 us -> 56.7 us  [plain(): pl.pallas_call(kernel, out_shape=outs, in_specs=[SMEM] + [VMEM] * (len(in...]
    pallas_call x5, Pallas kernels: 120 us -> 123 us  [call(): pl.pallas_call(kernel, out_shape=outs, scratch_shapes=scratch, in_specs=[...]
    ppermute x2, starting transfers between devices: 2.6 us -> 0.11 us  [along_x(): return lax.ppermute(sent, 'dp', [(0, 2), (2, 0), (1, 3), (3, 1)])]
  transfers between devices with their start and end apart: 4 -> 4, of which waited for: 1 -> 1; matrix products, arithmetic and copies ran while one was open for 0% -> 0% of each run, Pallas kernels for 35% -> 36%
where the time goes in v4:
time: 189 us
  Pallas kernels  181 us (96%)
  starting transfers between devices  2.17 us (1%)
    pallas_call x5, Pallas kernels, call(): pl.pallas_call(kernel, out_shape=outs, scratch_shapes=scratch, in_specs=[...  123 us
    pallas_call x4, Pallas kernels, plain(): pl.pallas_call(kernel, out_shape=outs, in_specs=[SMEM] + [VMEM] * (len(in...  56.7 us
  transfers between devices with their start and end apart: 4, of which 1 were waited for; matrix products, arithmetic and copies ran while one was open for 0% of the time, Pallas kernels for 36%

profile of v4, /device:TPU:0, one launch (start us, length us, event | category | flops | bytes accessed | tf_op | source)
XLA Modules:
  0.0 188.5 jit_solution(9400432797446284780)
XLA Ops:
  0.6 0.7 convert_bitcast_fusion
  1.4 1.6 fusion.own.u_ref
  3.0 0.7 pad_maximum_fusion.pack_ref
  3.7 0.0 copy-start.6
  3.7 0.0 copy-start.3
  3.7 0.0 copy-start.4
  3.7 0.0 copy-start.5
  3.7 22.9 %entry.1 = (bf16[4,4,256,384]{3,2,1,0:T(8,128)(2,1)S(1)}, s32[2,4,8,512]{3,2,1,0:T(8,128)S(1)}, f32[2,4,512,8]{3,2,1,0:T(8,128)S(1)}, s32[8,8]{1,0:T(8,128)S(1)}) custom-call(bf16[512,384]{1,0:T(8,128)(2,1)S(1)} %fusion.own.u_ref, f32[16,512]{1,0:T(8,128)S(1)} %pad_maximum_fusion.pack_ref), custom_call_target="tpu_custom_call" | custom-call | flops 10000000000 | bytes 4000000 | tf_op jit(solution)/shard_map/entry/pallas_call | solution.py:425
  26.6 0.0 copy-done.6
  26.7 1.6 collective-permute-start.1
  28.2 0.5 collective-permute-start
  28.7 0.0 copy-done.3
  28.7 0.0 copy-done.4
  28.7 0.0 copy-done.5
  28.7 0.0 copy-start.8
  28.7 9.9 %expert_forward.1.o_ref = bf16[4,4,256,384]{3,2,1,0:T(8,128)(2,1)S(1)} custom-call(s32[8,8]{1,0:T(8,128)S(1)} %get-tuple-element.56.off_ref, bf16[4,4,256,384]{3,2,1,0:T(8,128)(2,1)S(1)} %get-tuple-element.58.x_ref, bf16[4,672,384]{2,1,0:T(8,128)(2,1)S(1)} %bitcast.16, bf16[4,672,384]{2,1,0:T(8,128)(2,1)S(1)} %bitcast.19, bf16[4,672,384]{2,1,0:T(8,128)(2,1)S(1)} %copy-done.5), custom_call_target="tpu_custom_call" | custom-call | flops 10000000000 | bytes 10000000 | tf_op jit(solution)/shard_map/expert_forward/pallas_call | solution.py:155
  38.7 0.0 collective-permute-done.1.dy_z
  38.7 0.0 collective-permute-done.dy_y
  38.7 0.0 copy-done.8
  38.7 0.0 copy-start
  38.7 0.0 copy-start.1
  38.7 0.0 copy-start.2
  38.8 33.8 %middle.1 = (bf16[512,384]{1,0:T(8,128)(2,1)S(1)}, bf16[4,4,256,384]{3,2,1,0:T(8,128)(2,1)S(1)}, bf16[4,4,256,384]{3,2,1,0:T(8,128)(2,1)S(1)}) custom-call(bf16[4,4,256,384]{3,2,1,0:T(8,128)(2,1)S(1)} %expert_forward.1.o_ref, bf16[512,384]{1,0:T(8,128)(2,1)S(1)} %fusion.own.u_ref, bf16[384,384]{1,0:T(8,128)(2,1)S(1)} %copy-done.8, ...), custom_call_target="tpu_custom_call" | custom-call | flops 10000000000 | bytes 4000000 | tf_op jit(solution)/shard_map/middle/pallas_call | solution.py:425
  72.5 0.0 copy-done
  72.5 0.0 copy-done.1
  72.5 0.0 copy-done.2
  72.5 20.6 %expert_backward.3 = (bf16[4,4,256,384]{3,2,1,0:T(8,128)(2,1)S(1)}, bf16[2,3,2,2,96,672]{5,4,3,2,1,0:T(8,128)(2,1)S(1)}, bf16[2,2,1280,384]{3,2,1,0:T(8,128)(2,1)S(1)}, bf16[2,3,1024,672]{3,2,1,0:T(8,128)(2,1)S(1)}) custom-call(s32[8,8]{1,0:T(8,128)S(1)} %get-tuple-element.56.off_ref, bf16[4,4,256,384]{3,2,1,0:T(8,128)(2,1)S(1)} %get-tuple-element.62.x_ref, ...), custom_call_target="tpu_custom_call" | custom-call | flops 35999997952 | bytes 10000000 | tf_op jit(solution)/shard_map/expert_backward/pallas_call | solution.py:155
  93.2 34.2 %turn.1 = (bf16[512,384]{1,0:T(8,128)(2,1)S(1)}, bf16[4,4,256,384]{3,2,1,0:T(8,128)(2,1)S(1)}, bf16[2,2,2,2,24,384]{5,4,3,2,1,0:T(8,128)(2,1)S(1)}, bf16[2,96,67...) custom-call(bf16[4,4,256,384]{3,2,1,0:T(8,128)(2,1)S(1)} %get-tuple-, ...), custom_call_target="tpu_custom_call" | custom-call | flops 10000000000 | bytes 4000000 | tf_op jit(solution)/shard_map/turn/pallas_call | solution.py:425
  127.4 0.0 collective-permute-start.3
  127.4 14.0 %expert_backward.4 = (bf16[2,4,256,384]{3,2,1,0:T(8,128)(2,1)S(1)}, bf16[2,3,2,2,96,672]{5,4,3,2,1,0:T(8,128)(2,1)S(1)}) custom-call(s32[8,8]{1,0:T(8,128)S(1)} %get-tuple-element.56.off_ref, bf16[4,4,256,384]{3,2,1,0:T(8,128)(2,1)S(1)} %get-tuple-element.58.x_ref, bf16[4,4,256,384]{3,2,1,0:T(8,128)(2,1)S(1)} %get-tuple-element.75.d_ref, ...), custom_call_target="tpu_custom_call" | custom-call | flops 17999998976 | bytes 10000000 | tf_op jit(solution)/shard_map/expert_backward/pallas_call | solution.py:155
  141.5 4.0 %pair.1 = (bf16[3,96,1344]{2,1,0:T(8,128)(2,1)S(1)}, bf16[3,96,1344]{2,1,0:T(8,128)(2,1)S(1)}) custom-call(bf16[2,3,2,2,96,672]{5,4,3,2,1,0:T(8,128)(2,1)S(1)} %get-tuple-element.70.grads), custom_call_target="tpu_custom_call" | custom-call | flops 10000000000 | bytes 4000000 | tf_op jit(solution)/shard_map/pair/pallas_call | solution.py:425
  145.5 0.0 copy-start.7
  145.5 0.0 copy-start.9
  145.5 0.1 collective-permute-start.2
  145.6 1.0 collective-permute-done.3.two_got
  146.5 12.1 %expert_backward.5 = (bf16[2,4,256,384]{3,2,1,0:T(8,128)(2,1)S(1)}, bf16[2,3,2,2,96,672]{5,4,3,2,1,0:T(8,128)(2,1)S(1)}) custom-call(s32[8,8]{1,0:T(8,128)S(1)} %get-tuple-element.56.off_ref, bf16[4,4,256,384]{3,2,1,0:T(8,128)(2,1)S(1)} %get-tuple-element.58.x_ref, bf16[4,4,256,384]{3,2,1,0:T(8,128)(2,1)S(1)} %get-tuple-element.75.d_ref, ...), custom_call_target="tpu_custom_call" | custom-call | flops 17999998976 | bytes 10000000 | tf_op jit(solution)/shard_map/expert_backward/pallas_call | solution.py:155
  158.6 0.0 copy-done.7
  158.7 0.0 copy-done.9
  158.7 27.6 %exit.1 = (bf16[512,384]{1,0:T(8,128)(2,1)S(1)}, bf16[24,384]{1,0:T(8,128)(2,1)S(1)}, bf16[24,384]{1,0:T(8,128)(2,1)S(1)}, bf16[2,96,672]{2,1,0:T(8,128)(2,1)S(1...) custom-call(bf16[2,4,256,384]{3,2,1,0:T(8,128)(2,1)S(1)} %get-tuple-, ...), custom_call_target="tpu_custom_call" | custom-call | flops 10000000000 | bytes 4000000 | tf_op jit(solution)/shard_map/exit/pallas_call | solution.py:425
  186.3 0.0 collective-permute-done.2.got
  186.3 2.0 %store.1 = (bf16[512,384]{1,0:T(8,128)(2,1)}, bf16[24,384]{1,0:T(8,128)(2,1)}, bf16[24,384]{1,0:T(8,128)(2,1)}, bf16[4,96,672]{2,1,0:T(8,128)(2,1)}, bf16[4,96,6...) custom-call(bf16[3,96,1344]{2,1,0:T(8,128)(2,1)S(1)} %get-tuple-elem, ...), custom_call_target="tpu_custom_call" | custom-call | flops 1000000000 | bytes 4000000 | tf_op jit(solution)/shard_map/store/pallas_call | solution.py:669
Async XLA Ops:
  3.7 23.0 %copy-start.6 = (bf16[512,384]{1,0:T(8,128)(2,1)S(1)}, bf16[512,384]{1,0:T(8,128)(2,1)}, u32[]{:S(2)}) copy-start(bf16[512,384]{1,0:T(8,128)(2,1)} %dy_ref.1) | copy-start | bytes 1179652
  3.7 25.0 %copy-start.3 = (bf16[4,384,672]{1,2,0:T(8,128)(2,1)S(1)}, bf16[4,384,672]{1,2,0:T(8,128)(2,1)}, u32[]{:S(2)}) copy-start(bf16[4,384,672]{1,2,0:T(8,128)(2,1)} %param.19) | copy-start | bytes 6193156
  3.7 25.0 %copy-start.4 = (bf16[4,384,672]{1,2,0:T(8,128)(2,1)S(1)}, bf16[4,384,672]{1,2,0:T(8,128)(2,1)}, u32[]{:S(2)}) copy-start(bf16[4,384,672]{1,2,0:T(8,128)(2,1)} %param.20) | copy-start | bytes 6193156
  3.7 25.0 %copy-start.5 = (bf16[4,672,384]{2,1,0:T(8,128)(2,1)S(1)}, bf16[4,672,384]{2,1,0:T(8,128)(2,1)}, u32[]{:S(2)}) copy-start(bf16[4,672,384]{2,1,0:T(8,128)(2,1)} %wd_ref.7) | copy-start | bytes 6193156
  26.7 12.0 %collective-permute-start.1 = (bf16[512,384]{1,0:T(8,128)(2,1)S(1)}, bf16[512,384]{1,0:T(8,128)(2,1)S(1)}, u32[]{:S(2)}, u32[]{:S(2)}) collective-permute-start(bf16[512,384]{1,0:T(8,128)(2,1)S(1)} %copy-done.6), channel_id=1, source_target_pairs={{0,8},{4,12},{8,0},{12,4},{1,9},{5,13},{9,1},{13,5},{2,10},{6,14},... | collective-permute-start | bytes 1179656 | tf_op jit(solution)/shard_map/ppermute | solution.py:704
  28.2 10.5 %collective-permute-start = (bf16[512,384]{1,0:T(8,128)(2,1)S(1)}, bf16[512,384]{1,0:T(8,128)(2,1)S(1)}, u32[]{:S(2)}, u32[]{:S(2)}) collective-permute-start(bf16[512,384]{1,0:T(8,128)(2,1)S(1)} %copy-done.6), channel_id=1, source_target_pairs={{0,4},{4,0},{8,12},{12,8},{1,5},{5,1},{9,13},{13,9},{2,6},{6,2},{1... | collective-permute-start | bytes 1179656 | tf_op jit(solution)/shard_map/ppermute | solution.py:704
  28.7 10.0 %copy-start.8 = (bf16[384,384]{1,0:T(8,128)(2,1)S(1)}, bf16[384,384]{1,0:T(8,128)(2,1)}, u32[]{:S(2)}) copy-start(bf16[384,384]{1,0:T(8,128)(2,1)} %dense_ref.4) | copy-start | bytes 884740
  38.7 33.8 %copy-start = (bf16[4,384,672]{1,2,0:T(8,128)(2,1)S(1)}, bf16[4,384,672]{1,2,0:T(8,128)(2,1)}, u32[]{:S(2)}) copy-start(bf16[4,384,672]{1,2,0:T(8,128)(2,1)} %param.25) | copy-start | bytes 6193156
  38.7 33.8 %copy-start.1 = (bf16[4,384,672]{1,2,0:T(8,128)(2,1)S(1)}, bf16[4,384,672]{1,2,0:T(8,128)(2,1)}, u32[]{:S(2)}) copy-start(bf16[4,384,672]{1,2,0:T(8,128)(2,1)} %param.26) | copy-start | bytes 6193156
  38.7 33.8 %copy-start.2 = (bf16[4,672,384]{2,1,0:T(8,128)(2,1)S(1)}, bf16[4,672,384]{2,1,0:T(8,128)(2,1)}, u32[]{:S(2)}) copy-start(bf16[4,672,384]{2,1,0:T(8,128)(2,1)} %wd_ref.5) | copy-start | bytes 6193156
  127.4 19.2 %collective-permute-start.3 = (bf16[3,96,1344]{2,1,0:T(8,128)(2,1)S(1)}, bf16[3,96,1344]{2,1,0:T(8,128)(2,1)S(1)}, u32[]{:S(2)}, u32[]{:S(2)}) collective-permute-start(bf16[3,96,1344]{2,1,0:T(8,128)(2,1)S(1)} %get-tuple-element.74), channel_id=1, source_target_pairs={{0,2},{2,0},{1,3},{3,1},{4,6},{6,4},{5,7},{7,5},{8,10},{10,8},{9,1... | collective-permute-start | bytes 2322440 | tf_op jit(solution)/shard_map/ppermute | solution.py:682
  145.5 13.1 %copy-start.7 = (bf16[512,384]{1,0:T(8,128)(2,1)S(1)}, bf16[512,384]{1,0:T(8,128)(2,1)}, u32[]{:S(2)}) copy-start(bf16[512,384]{1,0:T(8,128)(2,1)} %tok_ref.1) | copy-start | bytes 1179652
  145.5 13.1 %copy-start.9 = (bf16[384,384]{1,0:T(8,128)(2,1)S(1)}, bf16[384,384]{1,0:T(8,128)(2,1)}, u32[]{:S(2)}) copy-start(bf16[384,384]{1,0:T(8,128)(2,1)} %dense_ref.5) | copy-start | bytes 884740
  145.5 40.8 %collective-permute-start.2 = (bf16[3,96,1344]{2,1,0:T(8,128)(2,1)S(1)}, bf16[3,96,1344]{2,1,0:T(8,128)(2,1)S(1)}, u32[]{:S(2)}, u32[]{:S(2)}) collective-permute-start(bf16[3,96,1344]{2,1,0:T(8,128)(2,1)S(1)} %get-tuple-element.72), channel_id=1, source_target_pairs={{0,2},{2,0},{1,3},{3,1},{4,6},{6,4},{5,7},{7,5},{8,10},{10,8},{9,1... | collective-permute-start | bytes 2322440 | tf_op jit(solution)/shard_map/ppermute | solution.py:682

commit v5 on v4

--- a/solution.py
+++ b/solution.py
@@ -16,6 +16,10 @@
 FF = 672
 CAP = 256
 SLOTS = 5 * CAP
+HALF = TOK // 2
+QUARTER = TOK // 4
+SETS = (pl.ds(0, HALF), pl.ds(HALF, HALF))
+ALL = pl.ds(0, TOK)
 ROWS_DP = D // 4
 VMEM = pl.BlockSpec(memory_space=pltpu.VMEM)
 SMEM = pl.BlockSpec(memory_space=pltpu.SMEM)
@@ -65,13 +69,13 @@
             off_ref[layer * N_LOC + exp, 7] = jnp.maximum((halves + 1) // 2, 2)
 
 
-def pick(layer, rank_ref, src, exp):
-    row = rank_ref[layer, src, pl.ds(exp, 1), :]
-    return (lax.broadcasted_iota(jnp.int32, (CAP, TOK), 0) == row).astype(BF16)
-
-
-def gate_column(layer, gate_ref, src, exp):
-    slab = gate_ref[layer, src]
+def pick(layer, rank_ref, src, exp, toks=ALL):
+    row = rank_ref[layer, src, pl.ds(exp, 1), toks]
+    return (lax.broadcasted_iota(jnp.int32, (CAP, toks.size), 0) == row).astype(BF16)
+
+
+def gate_column(layer, gate_ref, src, exp, toks=ALL):
+    slab = gate_ref[layer, src, toks]
     lane = lax.broadcasted_iota(jnp.int32, slab.shape, 1)
     return jnp.sum(jnp.where(lane == exp, slab, 0.0), axis=1, keepdims=True)
 
@@ -80,32 +84,40 @@
     return pl.multiple_of(off_ref[row, src], 16)
 
 
-def scatter_gated(layer, rank_ref, gate_ref, o_ref, src):
+def scatter_gated(layer, rank_ref, gate_ref, o_ref, src, toks):
     total = None
     for exp in range(N_LOC):
-        term = gate_column(layer, gate_ref, src, exp) * mm(pick(layer, rank_ref, src, exp), o_ref[exp, src], TN)
+        term = gate_column(layer, gate_ref, src, exp, toks) * mm(pick(layer, rank_ref, src, exp, toks), o_ref[exp, src], TN)
         total = term if total is None else total + term
     return total.astype(BF16)
 
 
-def scatter_plain(layer, rank_ref, g_refs, src):
-    sel = jnp.concatenate([pick(layer, rank_ref, src, exp) for exp in range(N_LOC)], axis=0)
+def scatter_plain(layer, rank_ref, g_refs, src, toks):
+    sel = jnp.concatenate([pick(layer, rank_ref, src, exp, toks) for exp in range(N_LOC)], axis=0)
     per = N_LOC // len(g_refs)
     rows = [g_refs[exp // per][exp % per, src] for exp in range(N_LOC)]
     return mm(sel, jnp.concatenate(rows, axis=0), TN).astype(BF16)
 
 
-def gather_rows(layer, rank_ref, pad_ref, src, toks):
+def gather_rows(layer, rank_ref, pad_ref, src, block_ref, toks=ALL, gate_ref=None, more=False):
     @pl.loop(0, N_LOC)
     def _(exp):
-        pad_ref[exp, src] = mm(pick(layer, rank_ref, src, exp), toks[...]).astype(BF16)
-
-
-def gather_scaled(layer, rank_ref, gate_ref, pad_ref, src, toks):
-    @pl.loop(0, N_LOC)
-    def _(exp):
-        scaled = (gate_column(layer, gate_ref, src, exp) * toks[...].astype(F32)).astype(BF16)
-        pad_ref[exp, src] = mm(pick(layer, rank_ref, src, exp), scaled).astype(BF16)
+        rows = block_ref[toks]
+        if gate_ref is not None:
+            rows = (gate_column(layer, gate_ref, src, exp, toks) * rows.astype(F32)).astype(BF16)
+        picked = mm(pick(layer, rank_ref, src, exp, toks), rows)
+        if more:
+            picked = pad_ref[exp, src].astype(F32) + picked
+        pad_ref[exp, src] = picked.astype(BF16)
+
+
+def gather_others(spread, layer, rank_ref, pad_ref, every, gate_ref=None):
+    for src in (1, 2):
+        spread.arrived(src)
+        gather_rows(layer, rank_ref, pad_ref, src, every.at[src], ALL, gate_ref)
+    for k, toks in enumerate(SETS):
+        spread.sets[k].arrived(3)
+        gather_rows(layer, rank_ref, pad_ref, 3, every.at[3], toks, gate_ref, k == 1)
 
 
 def packed(off_ref, row, pad_ref, exp, scr):
@@ -253,12 +265,7 @@
     barrier = pltpu.get_barrier_semaphore()
     for target in targets:
         pl.semaphore_signal(barrier, inc=1, device_id=target, device_id_type=pl.DeviceIdType.MESH)
-    pl.semaphore_wait(barrier, len(targets))
-
-
-HALF = TOK // 2
-QUARTER = TOK // 4
-SETS = (pl.ds(0, HALF), pl.ds(HALF, HALF))
+    return functools.partial(pl.semaphore_wait, barrier, len(targets))
 
 
 class Spread:
@@ -346,76 +353,93 @@
             copy.wait_send()
 
 
-def start_collect(at, part, got, mix_scr, sems, slot_sum):
+def start_collect(at, part, got, mix_scr, sems, slot_sum, await_peers):
     both = Both(*[Collect(at, part, got, mix_scr, sems, k) for k in range(2)])
-    part[3] = slot_sum(3)
-    both.far()
-    part[1] = slot_sum(1)
+    for k, toks in enumerate(SETS):
+        part[3, toks] = slot_sum(3, toks)
+        if k == 0:
+            await_peers()
+        both.sets[k].far()
+    sum_slot(part, 1, slot_sum)
     both.near_y()
-    part[2] = slot_sum(2)
+    sum_slot(part, 2, slot_sum)
     both.near_z()
     return both
 
 
+def sum_slot(part, slot, slot_sum):
+    @pl.loop(0, 2)
+    def _(k):
+        toks = pl.ds(pl.multiple_of(k * HALF, HALF), HALF)
+        part[slot, toks] = slot_sum(slot, toks)
+
+
 def spread_of(at, own, every, sems):
     return Both(*[Spread(at, own, every, sems, k) for k in range(2)])
 
 
 class Halve:
-    def __init__(self, at, grads, first, got, sems):
-        self.at, self.grads, self.first, self.got = at, grads, first, got
-        self.pair = [remote(grads.at[first + k % 2, k // 2, :, 1 - at.c], got.at[k], sems, k, at.to_c) for k in range(6)]
+    def __init__(self, at, grads, got, sems):
+        self.at, self.grads, self.got = at, grads, got
+        self.pair = [remote(grads[k // 3].at[k % 3, :, 1 - at.c], got.at[k], sems, k, at.to_c) for k in range(6)]
 
     def start(self, exp):
-        for copy in self.pair[exp::2]:
+        for copy in self.pair[3 * exp:3 * exp + 3]:
             copy.start()
 
-    def total(self, mat, side):
-        return jnp.concatenate([self.grads[self.first + exp, mat, side, self.at.c].astype(F32) + self.got[2 * mat + exp, side].astype(F32)
-                                for exp in range(2)], axis=1).astype(BF16)
-
-    def wait(self, mat):
-        for exp in range(2):
-            self.pair[2 * mat + exp].wait_recv()
+    def wait(self, exp):
+        for copy in self.pair[3 * exp:3 * exp + 3]:
+            copy.wait_recv()
+
+    def total(self, exp, side):
+        return jnp.concatenate([self.grads[exp][mat, side, self.at.c].astype(F32) + self.got[3 * exp + mat, side].astype(F32)
+                                for mat in range(3)], axis=1).astype(BF16)
 
     def drain(self):
         for copy in self.pair:
             copy.wait_send()
 
 
-def store_pair(out, first, keep, got):
+def store_expert(outs, exp, keep, got):
     total = (keep.astype(F32) + got.astype(F32)).astype(BF16)
-    for exp in range(2):
-        out[first + exp] = total[:, FF * exp:FF * exp + FF]
+    for mat, out in enumerate(outs):
+        out[exp] = total[:, FF * mat:FF * mat + FF]
 
 
 class Across:
     def __init__(self, at, halve, keep, send, got, sems):
         self.at, self.halve, self.keep, self.send, self.got = at, halve, keep, send, got
-        self.along = [remote(send.at[mat], got.at[mat], sems, mat, at.to_x) for mat in range(3)]
-
-    def forward(self, mat):
-        self.halve.wait(mat)
-        self.send[mat] = self.halve.total(mat, 1 - self.at.x)
-        self.along[mat].start()
-        self.keep[mat] = self.halve.total(mat, self.at.x)
+        self.along = [remote(send.at[exp], got.at[exp], sems, exp, at.to_x) for exp in range(2)]
+
+    def forward(self, exp):
+        self.halve.wait(exp)
+        self.send[exp] = self.halve.total(exp, 1 - self.at.x)
+        self.along[exp].start()
+        self.keep[exp] = self.halve.total(exp, self.at.x)
 
     def finish(self, outs, first):
-        for mat in range(3):
-            self.along[mat].wait_recv()
-            store_pair(outs[mat], first, self.keep[mat], self.got[mat])
+        for exp in range(2):
+            self.along[exp].wait_recv()
+            store_expert(outs, first + exp, self.keep[exp], self.got[exp])
         for copy in self.along:
             copy.wait_send()
 
 
+def leave_totals(at, halve, keep, send):
+    for exp in range(2):
+        halve.wait(exp)
+        send[exp] = halve.total(exp, 1 - at.x)
+        keep[exp] = halve.total(exp, at.x)
+
+
 def sems(count):
     return [pltpu.SemaphoreType.DMA((count,))] * 2
 
 
-PACKED = (3, ROWS_DP, 2 * FF)
+PACKED = (2, ROWS_DP, 3 * FF)
 COLLECT_SCRATCH = [pltpu.VMEM((N_EP, TOK, D), BF16), pltpu.VMEM((12, QUARTER, D), BF16), pltpu.VMEM((4, QUARTER, D), BF16)] + sems(12)
 HALVE_SCRATCH = [pltpu.VMEM((6, 2, ROWS_DP, FF), BF16)] + sems(6)
-ACROSS_SCRATCH = [pltpu.VMEM(PACKED, BF16)] * 3 + sems(3)
+ACROSS_SCRATCH = [pltpu.VMEM(PACKED, BF16)] * 3 + sems(2)
 
 
 ANY = pl.BlockSpec(memory_space=pl.ANY)
@@ -432,7 +456,7 @@
 
 def entry_kernel(own, pack_ref, x_pad, rank_ref, gate_ref, off_ref, packs, every, s_send, s_recv, p_send, p_recv):
     at = Place()
-    greet([at.to_y, at.to_z])
+    greet([at.to_y, at.to_z])()
     small = [remote(pack_ref, packs.at[1], (p_send, p_recv), 0, at.to_y),
              remote(pack_ref, packs.at[2], (p_send, p_recv), 1, at.to_z),
              remote(packs.at[1], packs.at[3], (p_send, p_recv), 2, at.to_z)]
@@ -448,9 +472,7 @@
     route_into(packs, rank_ref, gate_ref, off_ref, at.me)
     spread.forward()
     gather_rows(0, rank_ref, x_pad, 0, own)
-    for src in range(1, N_EP):
-        spread.arrived(src)
-        gather_rows(0, rank_ref, x_pad, src, every.at[src])
+    gather_others(spread, 0, rank_ref, x_pad, every)
     spread.finish()
     for copy in small:
         copy.wait_send()
@@ -459,21 +481,23 @@
 def middle_kernel(o_ref, u_ref, dense_ref, rank_ref, gate_ref, dy_own, dy_y, dy_z, mid_ref, x_pad, d_pad,
                   part, got, mix_scr, c_send, c_recv, u_scr, every, s_send, s_recv, dy_d, d_send, d_recv):
     at = Place()
-    greet([at.to_y, at.to_z])
-
-    def slot_sum(src):
-        return scatter_gated(0, rank_ref, gate_ref, o_ref, src)
-
-    collect = start_collect(at, part, got, mix_scr, (c_send, c_recv), slot_sum)
-    collect.forward()
+    await_peers = greet([at.to_y, at.to_z])
     onward = [remote(dy_y.at[SETS[0]], dy_d.at[SETS[0]], (d_send, d_recv), 0, at.to_z),
               remote(dy_z.at[SETS[1]], dy_d.at[SETS[1]], (d_send, d_recv), 1, at.to_y)]
-    part[0] = slot_sum(0)
-    for src, dy_ref in ((0, dy_own), (1, dy_y)):
-        gather_scaled(1, rank_ref, gate_ref, d_pad, src, dy_ref)
-    collect.summed_gone()
-    for copy in onward:
-        copy.start()
+
+    def begin():
+        await_peers()
+        for copy in onward:
+            copy.start()
+
+    def slot_sum(src, toks):
+        return scatter_gated(0, rank_ref, gate_ref, o_ref, src, toks)
+
+    collect = start_collect(at, part, got, mix_scr, (c_send, c_recv), slot_sum, begin)
+    gather_rows(1, rank_ref, d_pad, 0, dy_own, ALL, gate_ref)
+    collect.forward()
+    sum_slot(part, 0, slot_sum)
+    gather_rows(1, rank_ref, d_pad, 1, dy_y, ALL, gate_ref)
     spread = spread_of(at, u_scr, every, (s_send, s_recv))
     for k, rows in enumerate(SETS):
         mid = collect.sets[k].finish(u_ref)
@@ -481,17 +505,16 @@
         spread.sets[k].start()
         mid_ref[rows] = mid
     gather_rows(1, rank_ref, x_pad, 0, u_scr)
-    gather_scaled(1, rank_ref, gate_ref, d_pad, 2, dy_z)
+    gather_rows(1, rank_ref, d_pad, 2, dy_z, ALL, gate_ref)
     spread.forward()
     for copy in onward:
         copy.wait_recv()
-    gather_scaled(1, rank_ref, gate_ref, d_pad, 3, dy_d)
+    gather_rows(1, rank_ref, d_pad, 3, dy_d, ALL, gate_ref)
+    collect.summed_gone()
     collect.drain()
     for copy in onward:
         copy.wait_send()
-    for src in range(1, N_EP):
-        spread.arrived(src)
-        gather_rows(1, rank_ref, x_pad, src, every.at[src])
+    gather_others(spread, 1, rank_ref, x_pad, every)
     spread.finish()
 
 
@@ -549,22 +572,24 @@
                 part, got, mix_scr, c_send, c_recv, s_send, s_recv, got_a, a_send, a_recv, got_b, b_send, b_recv,
                 keep, send, got_x, x_send, x_recv, g_scr, every, later_grads):
     at = Place()
-    greet([at.to_y, at.to_z, at.to_c, at.to_x])
-    now = Halve(at, grads, 0, got_a, (a_send, a_recv))
-    later = Halve(at, later_grads, 0, got_b, (b_send, b_recv))
-    now.start(0)
-    now.start(1)
-
-    def slot_sum(src):
-        return scatter_plain(1, rank_ref, (gx_ref,), src)
-
-    collect = start_collect(at, part, got, mix_scr, (c_send, c_recv), slot_sum)
+    await_peers = greet([at.to_y, at.to_z, at.to_c, at.to_x])
+    now = Halve(at, (grads.at[0], grads.at[1]), got_a, (a_send, a_recv))
+    later = Halve(at, (later_grads.at[0], later_grads.at[1]), got_b, (b_send, b_recv))
+
+    def begin():
+        await_peers()
+        now.start(0)
+        now.start(1)
+
+    def slot_sum(src, toks):
+        return scatter_plain(1, rank_ref, (gx_ref,), src, toks)
+
+    collect = start_collect(at, part, got, mix_scr, (c_send, c_recv), slot_sum, begin)
     across = Across(at, now, keep, send, got_x, (x_send, x_recv))
     across.forward(0)
     collect.forward()
     across.forward(1)
-    across.forward(2)
-    part[0] = slot_sum(0)
+    sum_slot(part, 0, slot_sum)
     for exp in range(2):
         weight_grads(left, right, exp, later_grads, exp, N_EP * CAP)
         later.start(exp)
@@ -575,64 +600,59 @@
         g_scr[rows] = (halves[k].astype(F32) + mm(halves[k], dense_ref[...], NT)).astype(BF16)
         spread.sets[k].start()
         grad_ref[rows] = g_scr[rows]
-    gather_scaled(0, rank_ref, gate_ref, d_pad, 0, g_scr)
+    gather_rows(0, rank_ref, d_pad, 0, g_scr, ALL, gate_ref)
     write_slabs(slabs, dense_grad(mid_ref, halves))
     spread.forward()
-    for mat in range(3):
-        later.wait(mat)
-        later_send[mat] = later.total(mat, 1 - at.x)
-        later_keep[mat] = later.total(mat, at.x)
+    leave_totals(at, later, later_keep, later_send)
     collect.summed_gone()
     collect.drain()
     now.drain()
     later.drain()
-    for src in range(1, N_EP):
-        spread.arrived(src)
-        if src == 3:
-            across.finish((oa, ob, oc), 0)
-        gather_scaled(0, rank_ref, gate_ref, d_pad, src, every.at[src])
+    across.finish((oa, ob, oc), 0)
+    gather_others(spread, 0, rank_ref, d_pad, every, gate_ref)
     spread.finish()
 
 
 def pair_kernel(grads, later_keep, later_send, got_b, b_send, b_recv):
     at = Place()
-    greet([at.to_c])
-    later = Halve(at, grads, 0, got_b, (b_send, b_recv))
+    greet([at.to_c])()
+    later = Halve(at, (grads.at[0], grads.at[1]), got_b, (b_send, b_recv))
     later.start(0)
     later.start(1)
-    for mat in range(3):
-        later.wait(mat)
-        later_send[mat] = later.total(mat, 1 - at.x)
-        later_keep[mat] = later.total(mat, at.x)
+    leave_totals(at, later, later_keep, later_send)
     later.drain()
 
 
-def exit_kernel(gx_a, gx_b, dy_ref, dense_ref, tok_ref, slabs_two, rank_ref, grads, two_keep, two_got, da, db, dc,
+def exit_kernel(gx_a, gx_b, dy_ref, dense_ref, tok_ref, slabs_two, rank_ref, grads, left, right, two_keep, two_got, da, db, dc,
                 dx_ref, dense_one, dense_two, oa, ob, oc, ta, tb, tc,
-                part, got, mix_scr, c_send, c_recv, got_a, a_send, a_recv, keep, send, got_x, x_send, x_recv, slabs_one, *dense):
+                part, got, mix_scr, c_send, c_recv, got_a, a_send, a_recv, keep, send, got_x, x_send, x_recv, slabs_one, last_grads, *dense):
     at = Place()
-    greet([at.to_y, at.to_z, at.to_d, at.to_c, at.to_x])
-    now = Halve(at, grads, 0, got_a, (a_send, a_recv))
-    now.start(0)
-    now.start(1)
+    await_peers = greet([at.to_y, at.to_z, at.to_d, at.to_c, at.to_x])
+    now = Halve(at, (grads.at[0], last_grads.at[0]), got_a, (a_send, a_recv))
     half = len(dense) // 2
     first, second = [DenseReduce(at, slabs, *dense[k * half:k * half + 5], dense[k * half + 5:k * half + 7])
                      for k, slabs in enumerate((slabs_one, slabs_two))]
-    second.start()
-
-    def slot_sum(src):
-        return scatter_plain(0, rank_ref, (gx_a, gx_b), src)
-
-    collect = start_collect(at, part, got, mix_scr, (c_send, c_recv), slot_sum)
+
+    def begin():
+        await_peers()
+        now.start(0)
+        second.start()
+
+    def slot_sum(src, toks):
+        return scatter_plain(0, rank_ref, (gx_a, gx_b), src, toks)
+
+    collect = start_collect(at, part, got, mix_scr, (c_send, c_recv), slot_sum, begin)
     across = Across(at, now, keep, send, got_x, (x_send, x_recv))
     across.forward(0)
+    weight_grads(left, right, 0, last_grads, 0, N_EP * CAP)
+    now.start(1)
     collect.forward()
     second.to_plane()
     across.forward(1)
-    across.forward(2)
-    part[0] = slot_sum(0)
-    for mat, (out, done) in enumerate(((ta, da), (tb, db), (tc, dc))):
-        store_pair(out, 2, two_keep[mat], two_got[mat])
+    sum_slot(part, 0, slot_sum)
+    for exp in range(2):
+        store_expert((ta, tb, tc), 2 + exp, two_keep[exp], two_got[exp])
+    for out, done in ((ta, da), (tb, db), (tc, dc)):
         out[0:2] = done[...]
     halves = [one.finish(dy_ref) for one in collect.sets]
     write_slabs(slabs_one, dense_grad(tok_ref, halves))
@@ -655,8 +675,9 @@
     copies = [pltpu.make_async_copy(values[k], outs[k] if k < count - 3 else outs[k].at[2:4], sem.at[k]) for k in range(count)]
     for copy in copies:
         copy.start()
+    for exp in range(2):
+        store_expert([made.at[mat] for mat in range(3)], exp, keep[exp], got[exp])
     for mat in range(3):
-        store_pair(made.at[mat], 0, keep[mat], got[mat])
         copies.append(pltpu.make_async_copy(made.at[mat], outs[count - 3 + mat].at[0:2], sem.at[count + mat]))
         copies[-1].start()
     for copy in copies:
@@ -715,11 +736,11 @@
         keep_one, send_one = call(pair_kernel, 'pair', 4, (grads,), (block(*PACKED),) * 2, HALVE_SCRATCH, 6)
         got_two, d_one = lax.optimization_barrier((got_two, d_one))
         got_one = along_x(send_one)
-        gx_b, grads = expert_backward(0, 2, 2, 2, off, x_one, d_one, weights_one)
+        gx_b, grads, left, right = expert_backward(0, 2, 2, 1, off, x_one, d_one, weights_one)
         grad_tok, dense_one, dense_two, *reduced = call(
-            exit_kernel, 'exit', 3, (gx_a, gx_b, grad_mid, dense_w1, tokens, slabs, rank, grads, keep_two, got_two) + tuple(done_two),
+            exit_kernel, 'exit', 3, (gx_a, gx_b, grad_mid, dense_w1, tokens, slabs, rank, grads, left, right, keep_two, got_two) + tuple(done_two),
             (tok_block, block(24, D), block(24, D)) + (block(2, ROWS_DP, FF),) * 3 + (block(N_LOC, ROWS_DP, FF),) * 3,
-            COLLECT_SCRATCH + HALVE_SCRATCH + ACROSS_SCRATCH + [pltpu.VMEM((2, 2, 2, 2, 24, D), BF16)] + dense_scratch() * 2, 14)
+            COLLECT_SCRATCH + HALVE_SCRATCH + ACROSS_SCRATCH + [pltpu.VMEM((2, 2, 2, 2, 24, D), BF16), pltpu.VMEM(grads_shape(1), BF16)] + dense_scratch() * 2, 15)
         grad_tok, dense_one, dense_two, *reduced = store_all(keep_one, got_one, (grad_tok, dense_one, dense_two) + tuple(reduced[3:]) + tuple(reduced[:3]))
 
         def shaped(gate_up_down):

time: 189 us -> 185 us (0.979)
  Pallas kernels: 181 us -> 176 us
  starting transfers between devices: 2.17 us -> 4.13 us
    pallas_call x5, Pallas kernels: 123 us -> 117 us  [call(): pl.pallas_call(kernel, out_shape=outs, scratch_shapes=scratch, in_specs=[...]
    ppermute x2, starting transfers between devices: 0.11 us -> 2.07 us  [along_x(): return lax.ppermute(sent, 'dp', [(0, 2), (2, 0), (1, 3), (3, 1)])]
  transfers between devices with their start and end apart: 4 -> 4, of which waited for: 1 -> 0; matrix products, arithmetic and copies ran while one was open for 0% -> 0% of each run, Pallas kernels for 36% -> 36%
where the time goes in v5:
time: 185 us; the launch traced here: 184 us
  Pallas kernels  176 us (95%)
  starting transfers between devices  4.13 us (2%)
    pallas_call x5, Pallas kernels, call(): pl.pallas_call(kernel, out_shape=outs, scratch_shapes=scratch, in_specs=[...  117 us
    pallas_call x4, Pallas kernels, plain(): pl.pallas_call(kernel, out_shape=outs, in_specs=[SMEM] + [VMEM] * (len(in...  57.3 us
  transfers between devices with their start and end apart: 4, of which 0 were waited for; matrix products, arithmetic and copies ran while one was open for 0% of the time, Pallas kernels for 36%

profile of v5, /device:TPU:0, one launch (start us, length us, event | category | flops | bytes accessed | tf_op | source)
XLA Modules:
  0.0 184.5 jit_solution(515142212049852341)
XLA Ops:
  0.6 0.7 convert_bitcast_fusion
  1.4 1.6 fusion.own.u_ref
  3.0 0.7 pad_maximum_fusion.pack_ref
  3.7 0.0 copy-start.6
  3.7 0.0 copy-start.3
  3.7 0.0 copy-start.4
  3.7 0.0 copy-start.5
  3.7 22.6 %entry.1 = (bf16[4,4,256,384]{3,2,1,0:T(8,128)(2,1)S(1)}, s32[2,4,8,512]{3,2,1,0:T(8,128)S(1)}, f32[2,4,512,8]{3,2,1,0:T(8,128)S(1)}, s32[8,8]{1,0:T(8,128)S(1)}) custom-call(bf16[512,384]{1,0:T(8,128)(2,1)S(1)} %fusion.own.u_ref, f32[16,512]{1,0:T(8,128)S(1)} %pad_maximum_fusion.pack_ref), custom_call_target="tpu_custom_call" | custom-call | flops 10000000000 | bytes 4000000 | tf_op jit(solution)/shard_map/entry/pallas_call | solution.py:449
  26.4 0.0 copy-done.6
  26.4 1.6 collective-permute-start.1
  27.9 0.5 collective-permute-start
  28.4 0.0 copy-done.3
  28.4 0.0 copy-done.4
  28.4 0.0 copy-done.5
  28.4 0.0 copy-start.8
  28.5 10.8 %expert_forward.1.o_ref = bf16[4,4,256,384]{3,2,1,0:T(8,128)(2,1)S(1)} custom-call(s32[8,8]{1,0:T(8,128)S(1)} %get-tuple-element.58.off_ref, bf16[4,4,256,384]{3,2,1,0:T(8,128)(2,1)S(1)} %get-tuple-element.60.x_ref, bf16[4,672,384]{2,1,0:T(8,128)(2,1)S(1)} %bitcast.16, bf16[4,672,384]{2,1,0:T(8,128)(2,1)S(1)} %bitcast.19, bf16[4,672,384]{2,1,0:T(8,128)(2,1)S(1)} %copy-done.5), custom_call_target="tpu_custom_call" | custom-call | flops 10000000000 | bytes 10000000 | tf_op jit(solution)/shard_map/expert_forward/pallas_call | solution.py:167
  39.2 0.0 collective-permute-done.1.dy_z
  39.2 0.0 collective-permute-done.dy_y
  39.2 0.0 copy-done.8
  39.2 0.0 copy-start
  39.3 0.0 copy-start.1
  39.3 0.0 copy-start.2
  39.3 32.7 %middle.1 = (bf16[512,384]{1,0:T(8,128)(2,1)S(1)}, bf16[4,4,256,384]{3,2,1,0:T(8,128)(2,1)S(1)}, bf16[4,4,256,384]{3,2,1,0:T(8,128)(2,1)S(1)}) custom-call(bf16[4,4,256,384]{3,2,1,0:T(8,128)(2,1)S(1)} %expert_forward.1.o_ref, bf16[512,384]{1,0:T(8,128)(2,1)S(1)} %fusion.own.u_ref, bf16[384,384]{1,0:T(8,128)(2,1)S(1)} %copy-done.8, ...), custom_call_target="tpu_custom_call" | custom-call | flops 10000000000 | bytes 4000000 | tf_op jit(solution)/shard_map/middle/pallas_call | solution.py:449
  72.0 0.0 copy-done
  72.0 0.0 copy-done.1
  72.0 0.0 copy-done.2
  72.0 20.7 %expert_backward.3 = (bf16[4,4,256,384]{3,2,1,0:T(8,128)(2,1)S(1)}, bf16[2,3,2,2,96,672]{5,4,3,2,1,0:T(8,128)(2,1)S(1)}, bf16[2,2,1280,384]{3,2,1,0:T(8,128)(2,1)S(1)}, bf16[2,3,1024,672]{3,2,1,0:T(8,128)(2,1)S(1)}) custom-call(s32[8,8]{1,0:T(8,128)S(1)} %get-tuple-element.58.off_ref, bf16[4,4,256,384]{3,2,1,0:T(8,128)(2,1)S(1)} %get-tuple-element.64.x_ref, ...), custom_call_target="tpu_custom_call" | custom-call | flops 35999997952 | bytes 10000000 | tf_op jit(solution)/shard_map/expert_backward/pallas_call | solution.py:167
  92.7 31.6 %turn.1 = (bf16[512,384]{1,0:T(8,128)(2,1)S(1)}, bf16[4,4,256,384]{3,2,1,0:T(8,128)(2,1)S(1)}, bf16[2,2,2,2,24,384]{5,4,3,2,1,0:T(8,128)(2,1)S(1)}, bf16[2,96,67...) custom-call(bf16[4,4,256,384]{3,2,1,0:T(8,128)(2,1)S(1)} %get-tuple-, ...), custom_call_target="tpu_custom_call" | custom-call | flops 10000000000 | bytes 4000000 | tf_op jit(solution)/shard_map/turn/pallas_call | solution.py:449
  124.4 2.0 %collective-permute-start.3 = (bf16[2,96,2016]{2,1,0:T(8,128)(2,1)S(1)}, bf16[2,96,2016]{2,1,0:T(8,128)(2,1)S(1)}, u32[]{:S(2)}, u32[]{:S(2)}) collective-permute-start(bf16[2,96,2016]{2,1,0:T(8,128)(2,1)S(1)} %get-tuple-element.76), channel_id=1, source_target_pairs={{0,2},{2,0},{1,3},{3,1},{4,6},{6,4},{5,7},{7,5},{8,10},{10,8},{9,1... | collective-permute-start | bytes 2322440 | tf_op jit(solution)/shard_map/ppermute | solution.py:703
  126.4 14.0 %expert_backward.4 = (bf16[2,4,256,384]{3,2,1,0:T(8,128)(2,1)S(1)}, bf16[2,3,2,2,96,672]{5,4,3,2,1,0:T(8,128)(2,1)S(1)}) custom-call(s32[8,8]{1,0:T(8,128)S(1)} %get-tuple-element.58.off_ref, bf16[4,4,256,384]{3,2,1,0:T(8,128)(2,1)S(1)} %get-tuple-element.60.x_ref, bf16[4,4,256,384]{3,2,1,0:T(8,128)(2,1)S(1)} %get-tuple-element.77.d_ref, ...), custom_call_target="tpu_custom_call" | custom-call | flops 17999998976 | bytes 10000000 | tf_op jit(solution)/shard_map/expert_backward/pallas_call | solution.py:167
  140.4 4.2 %pair.1 = (bf16[2,96,2016]{2,1,0:T(8,128)(2,1)S(1)}, bf16[2,96,2016]{2,1,0:T(8,128)(2,1)S(1)}) custom-call(bf16[2,3,2,2,96,672]{5,4,3,2,1,0:T(8,128)(2,1)S(1)} %get-tuple-element.72.grads), custom_call_target="tpu_custom_call" | custom-call | flops 10000000000 | bytes 4000000 | tf_op jit(solution)/shard_map/pair/pallas_call | solution.py:449
  144.6 0.0 copy-start.7
  144.6 0.0 copy-start.9
  144.6 0.0 collective-permute-start.2
  144.6 0.0 collective-permute-done.3.two_got
  144.6 11.9 %expert_backward.5 = (bf16[2,4,256,384]{3,2,1,0:T(8,128)(2,1)S(1)}, bf16[1,3,2,2,96,672]{5,4,3,2,1,0:T(8,128)(2,1)S(1)}, bf16[1,2,1280,384]{3,2,1,0:T(8,128)(2,1)S(1)}, bf16[1,3,1024,672]{3,2,1,0:T(8,128)(2,1)S(1)}) custom-call(s32[8,8]{1,0:T(8,128)S(1)} %get-tuple-element.58.off_ref, bf16[4,4,256,384]{3,2,1,0:T(8,128)(2,1)S(1)} %get-tuple-element.60.x_ref, ...), custom_call_target="tpu_custom_call" | custom-call | flops 17999998976 | bytes 10000000 | tf_op jit(solution)/shard_map/expert_backward/pallas_call | solution.py:167
  156.5 0.0 copy-done.7
  156.5 0.0 copy-done.9
  156.5 25.7 %exit.1 = (bf16[512,384]{1,0:T(8,128)(2,1)S(1)}, bf16[24,384]{1,0:T(8,128)(2,1)S(1)}, bf16[24,384]{1,0:T(8,128)(2,1)S(1)}, bf16[2,96,672]{2,1,0:T(8,128)(2,1)S(1...) custom-call(bf16[2,4,256,384]{3,2,1,0:T(8,128)(2,1)S(1)} %get-tuple-, ...), custom_call_target="tpu_custom_call" | custom-call | flops 10000000000 | bytes 4000000 | tf_op jit(solution)/shard_map/exit/pallas_call | solution.py:449
  182.3 0.0 collective-permute-done.2.got
  182.3 2.0 %store.1 = (bf16[512,384]{1,0:T(8,128)(2,1)}, bf16[24,384]{1,0:T(8,128)(2,1)}, bf16[24,384]{1,0:T(8,128)(2,1)}, bf16[4,96,672]{2,1,0:T(8,128)(2,1)}, bf16[4,96,6...) custom-call(bf16[2,96,2016]{2,1,0:T(8,128)(2,1)S(1)} %get-tuple-elem, ...), custom_call_target="tpu_custom_call" | custom-call | flops 1000000000 | bytes 4000000 | tf_op jit(solution)/shard_map/store/pallas_call | solution.py:690
Async XLA Ops:
  3.7 22.7 %copy-start.6 = (bf16[512,384]{1,0:T(8,128)(2,1)S(1)}, bf16[512,384]{1,0:T(8,128)(2,1)}, u32[]{:S(2)}) copy-start(bf16[512,384]{1,0:T(8,128)(2,1)} %dy_ref.1) | copy-start | bytes 1179652
  3.7 24.7 %copy-start.3 = (bf16[4,384,672]{1,2,0:T(8,128)(2,1)S(1)}, bf16[4,384,672]{1,2,0:T(8,128)(2,1)}, u32[]{:S(2)}) copy-start(bf16[4,384,672]{1,2,0:T(8,128)(2,1)} %param.19) | copy-start | bytes 6193156
  3.7 24.7 %copy-start.4 = (bf16[4,384,672]{1,2,0:T(8,128)(2,1)S(1)}, bf16[4,384,672]{1,2,0:T(8,128)(2,1)}, u32[]{:S(2)}) copy-start(bf16[4,384,672]{1,2,0:T(8,128)(2,1)} %param.20) | copy-start | bytes 6193156
  3.7 24.7 %copy-start.5 = (bf16[4,672,384]{2,1,0:T(8,128)(2,1)S(1)}, bf16[4,672,384]{2,1,0:T(8,128)(2,1)}, u32[]{:S(2)}) copy-start(bf16[4,672,384]{2,1,0:T(8,128)(2,1)} %wd_ref.7) | copy-start | bytes 6193156
  26.4 12.8 %collective-permute-start.1 = (bf16[512,384]{1,0:T(8,128)(2,1)S(1)}, bf16[512,384]{1,0:T(8,128)(2,1)S(1)}, u32[]{:S(2)}, u32[]{:S(2)}) collective-permute-start(bf16[512,384]{1,0:T(8,128)(2,1)S(1)} %copy-done.6), channel_id=1, source_target_pairs={{0,8},{4,12},{8,0},{12,4},{1,9},{5,13},{9,1},{13,5},{2,10},{6,14},... | collective-permute-start | bytes 1179656 | tf_op jit(solution)/shard_map/ppermute | solution.py:725
  27.9 11.3 %collective-permute-start = (bf16[512,384]{1,0:T(8,128)(2,1)S(1)}, bf16[512,384]{1,0:T(8,128)(2,1)S(1)}, u32[]{:S(2)}, u32[]{:S(2)}) collective-permute-start(bf16[512,384]{1,0:T(8,128)(2,1)S(1)} %copy-done.6), channel_id=1, source_target_pairs={{0,4},{4,0},{8,12},{12,8},{1,5},{5,1},{9,13},{13,9},{2,6},{6,2},{1... | collective-permute-start | bytes 1179656 | tf_op jit(solution)/shard_map/ppermute | solution.py:725
  28.4 10.8 %copy-start.8 = (bf16[384,384]{1,0:T(8,128)(2,1)S(1)}, bf16[384,384]{1,0:T(8,128)(2,1)}, u32[]{:S(2)}) copy-start(bf16[384,384]{1,0:T(8,128)(2,1)} %dense_ref.4) | copy-start | bytes 884740
  39.2 32.7 %copy-start = (bf16[4,384,672]{1,2,0:T(8,128)(2,1)S(1)}, bf16[4,384,672]{1,2,0:T(8,128)(2,1)}, u32[]{:S(2)}) copy-start(bf16[4,384,672]{1,2,0:T(8,128)(2,1)} %param.25) | copy-start | bytes 6193156
  39.3 32.7 %copy-start.1 = (bf16[4,384,672]{1,2,0:T(8,128)(2,1)S(1)}, bf16[4,384,672]{1,2,0:T(8,128)(2,1)}, u32[]{:S(2)}) copy-start(bf16[4,384,672]{1,2,0:T(8,128)(2,1)} %param.26) | copy-start | bytes 6193156
  39.3 32.7 %copy-start.2 = (bf16[4,672,384]{2,1,0:T(8,128)(2,1)S(1)}, bf16[4,672,384]{2,1,0:T(8,128)(2,1)}, u32[]{:S(2)}) copy-start(bf16[4,672,384]{2,1,0:T(8,128)(2,1)} %wd_ref.5) | copy-start | bytes 6193156
  124.4 20.3 %collective-permute-start.3 = (bf16[2,96,2016]{2,1,0:T(8,128)(2,1)S(1)}, bf16[2,96,2016]{2,1,0:T(8,128)(2,1)S(1)}, u32[]{:S(2)}, u32[]{:S(2)}) collective-permute-start(bf16[2,96,2016]{2,1,0:T(8,128)(2,1)S(1)} %get-tuple-element.76), channel_id=1, source_target_pairs={{0,2},{2,0},{1,3},{3,1},{4,6},{6,4},{5,7},{7,5},{8,10},{10,8},{9,1... | collective-permute-start | bytes 2322440 | tf_op jit(solution)/shard_map/ppermute | solution.py:703
  144.6 12.0 %copy-start.7 = (bf16[512,384]{1,0:T(8,128)(2,1)S(1)}, bf16[512,384]{1,0:T(8,128)(2,1)}, u32[]{:S(2)}) copy-start(bf16[512,384]{1,0:T(8,128)(2,1)} %tok_ref.1) | copy-start | bytes 1179652
  144.6 12.0 %copy-start.9 = (bf16[384,384]{1,0:T(8,128)(2,1)S(1)}, bf16[384,384]{1,0:T(8,128)(2,1)}, u32[]{:S(2)}) copy-start(bf16[384,384]{1,0:T(8,128)(2,1)} %dense_ref.5) | copy-start | bytes 884740
  144.6 37.7 %collective-permute-start.2 = (bf16[2,96,2016]{2,1,0:T(8,128)(2,1)S(1)}, bf16[2,96,2016]{2,1,0:T(8,128)(2,1)S(1)}, u32[]{:S(2)}, u32[]{:S(2)}) collective-permute-start(bf16[2,96,2016]{2,1,0:T(8,128)(2,1)S(1)} %get-tuple-element.74), channel_id=1, source_target_pairs={{0,2},{2,0},{1,3},{3,1},{4,6},{6,4},{5,7},{7,5},{8,10},{10,8},{9,1... | collective-permute-start | bytes 2322440 | tf_op jit(solution)/shard_map/ppermute | solution.py:703

commit v6 on v5

--- a/solution.py
+++ b/solution.py
@@ -190,15 +190,16 @@
         def step(rows):
             x_blk = x_scr[rows, :]
             a_pre = mm(x_blk, wg_ref[exp], NT)
-            b_pre = mm(x_blk, wu_ref[exp], NT)
             grad_h = mm(d_scr[rows, :], wd_ref[exp], NT).astype(BF16).astype(F32)
             sigma = jax.nn.sigmoid(a_pre)
             swish = a_pre * sigma
-            grad_a = (grad_h * b_pre * sigma * (1.0 + a_pre * (1.0 - sigma))).astype(BF16)
             grad_b = (grad_h * swish).astype(BF16)
+            right[slot, 1, rows, :] = grad_b
+            slope = grad_h * (sigma + swish * (1.0 - sigma))
+            b_pre = mm(x_blk, wu_ref[exp], NT)
+            right[slot, 2, rows, :] = (swish * b_pre).astype(BF16)
+            grad_a = (slope * b_pre).astype(BF16)
             right[slot, 0, rows, :] = grad_a
-            right[slot, 1, rows, :] = grad_b
-            right[slot, 2, rows, :] = (swish * b_pre).astype(BF16)
             gx_scr[rows, :] = (mm(grad_a, wg_ref[exp]) + mm(grad_b, wu_ref[exp])).astype(BF16)
 
         over_rows(off_ref, row, step)

time: 185 us -> 183 us (0.989)
  Pallas kernels: 176 us -> 173 us
    pallas_call x4, Pallas kernels: 57.3 us -> 52.1 us  [plain(): pl.pallas_call(kernel, out_shape=outs, in_specs=[SMEM] + [VMEM] * (len(in...]
  transfers between devices with their start and end apart: 4 -> 4, of which waited for: 0 -> 0; matrix products, arithmetic and copies ran while one was open for 0% -> 0% of each run, Pallas kernels for 36% -> 34%
where the time goes in v6:
time: 183 us; the launch traced here: 182 us
  Pallas kernels  173 us (95%)
  starting transfers between devices  5.55 us (3%)
    pallas_call x5, Pallas kernels, call(): pl.pallas_call(kernel, out_shape=outs, scratch_shapes=scratch, in_specs=[...  118 us
    pallas_call x4, Pallas kernels, plain(): pl.pallas_call(kernel, out_shape=outs, in_specs=[SMEM] + [VMEM] * (len(in...  52.1 us
  transfers between devices with their start and end apart: 4, of which 0 were waited for; matrix products, arithmetic and copies ran while one was open for 0% of the time, Pallas kernels for 34%

profile of v6, /device:TPU:0, one launch (start us, length us, event | category | flops | bytes accessed | tf_op | source)
XLA Modules:
  0.0 182.3 jit_solution(9205902806257520766)
XLA Ops:
  0.6 0.7 convert_bitcast_fusion
  1.4 1.6 fusion.own.u_ref
  3.0 0.7 pad_maximum_fusion.pack_ref
  3.7 0.0 copy-start.6
  3.7 0.0 copy-start.3
  3.7 0.0 copy-start.4
  3.7 0.0 copy-start.5
  3.7 22.6 %entry.1 = (bf16[4,4,256,384]{3,2,1,0:T(8,128)(2,1)S(1)}, s32[2,4,8,512]{3,2,1,0:T(8,128)S(1)}, f32[2,4,512,8]{3,2,1,0:T(8,128)S(1)}, s32[8,8]{1,0:T(8,128)S(1)}) custom-call(bf16[512,384]{1,0:T(8,128)(2,1)S(1)} %fusion.own.u_ref, f32[16,512]{1,0:T(8,128)S(1)} %pad_maximum_fusion.pack_ref), custom_call_target="tpu_custom_call" | custom-call | flops 10000000000 | bytes 4000000 | tf_op jit(solution)/shard_map/entry/pallas_call | solution.py:450
  26.4 0.0 copy-done.6
  26.4 1.6 collective-permute-start.1
  27.9 0.5 collective-permute-start
  28.4 0.0 copy-done.3
  28.4 0.0 copy-done.4
  28.4 0.0 copy-done.5
  28.4 0.0 copy-start.8
  28.5 9.9 %expert_forward.1.o_ref = bf16[4,4,256,384]{3,2,1,0:T(8,128)(2,1)S(1)} custom-call(s32[8,8]{1,0:T(8,128)S(1)} %get-tuple-element.58.off_ref, bf16[4,4,256,384]{3,2,1,0:T(8,128)(2,1)S(1)} %get-tuple-element.60.x_ref, bf16[4,672,384]{2,1,0:T(8,128)(2,1)S(1)} %bitcast.16, bf16[4,672,384]{2,1,0:T(8,128)(2,1)S(1)} %bitcast.19, bf16[4,672,384]{2,1,0:T(8,128)(2,1)S(1)} %copy-done.5), custom_call_target="tpu_custom_call" | custom-call | flops 10000000000 | bytes 10000000 | tf_op jit(solution)/shard_map/expert_forward/pallas_call | solution.py:167
  38.4 0.0 collective-permute-done.1.dy_z
  38.4 0.0 collective-permute-done.dy_y
  38.4 0.0 copy-done.8
  38.4 0.0 copy-start
  38.4 0.0 copy-start.1
  38.5 0.0 copy-start.2
  38.5 33.0 %middle.1 = (bf16[512,384]{1,0:T(8,128)(2,1)S(1)}, bf16[4,4,256,384]{3,2,1,0:T(8,128)(2,1)S(1)}, bf16[4,4,256,384]{3,2,1,0:T(8,128)(2,1)S(1)}) custom-call(bf16[4,4,256,384]{3,2,1,0:T(8,128)(2,1)S(1)} %expert_forward.1.o_ref, bf16[512,384]{1,0:T(8,128)(2,1)S(1)} %fusion.own.u_ref, bf16[384,384]{1,0:T(8,128)(2,1)S(1)} %copy-done.8, ...), custom_call_target="tpu_custom_call" | custom-call | flops 10000000000 | bytes 4000000 | tf_op jit(solution)/shard_map/middle/pallas_call | solution.py:450
  71.5 0.0 copy-done
  71.5 0.0 copy-done.1
  71.5 0.0 copy-done.2
  71.5 20.2 %expert_backward.3 = (bf16[4,4,256,384]{3,2,1,0:T(8,128)(2,1)S(1)}, bf16[2,3,2,2,96,672]{5,4,3,2,1,0:T(8,128)(2,1)S(1)}, bf16[2,2,1280,384]{3,2,1,0:T(8,128)(2,1)S(1)}, bf16[2,3,1024,672]{3,2,1,0:T(8,128)(2,1)S(1)}) custom-call(s32[8,8]{1,0:T(8,128)S(1)} %get-tuple-element.58.off_ref, bf16[4,4,256,384]{3,2,1,0:T(8,128)(2,1)S(1)} %get-tuple-element.64.x_ref, ...), custom_call_target="tpu_custom_call" | custom-call | flops 35999997952 | bytes 10000000 | tf_op jit(solution)/shard_map/expert_backward/pallas_call | solution.py:167
  91.7 33.6 %turn.1 = (bf16[512,384]{1,0:T(8,128)(2,1)S(1)}, bf16[4,4,256,384]{3,2,1,0:T(8,128)(2,1)S(1)}, bf16[2,2,2,2,24,384]{5,4,3,2,1,0:T(8,128)(2,1)S(1)}, bf16[2,96,67...) custom-call(bf16[4,4,256,384]{3,2,1,0:T(8,128)(2,1)S(1)} %get-tuple-, ...), custom_call_target="tpu_custom_call" | custom-call | flops 10000000000 | bytes 4000000 | tf_op jit(solution)/shard_map/turn/pallas_call | solution.py:450
  125.3 0.5 collective-permute-start.3
  125.8 11.2 %expert_backward.4 = (bf16[2,4,256,384]{3,2,1,0:T(8,128)(2,1)S(1)}, bf16[2,3,2,2,96,672]{5,4,3,2,1,0:T(8,128)(2,1)S(1)}) custom-call(s32[8,8]{1,0:T(8,128)S(1)} %get-tuple-element.58.off_ref, bf16[4,4,256,384]{3,2,1,0:T(8,128)(2,1)S(1)} %get-tuple-element.60.x_ref, bf16[4,4,256,384]{3,2,1,0:T(8,128)(2,1)S(1)} %get-tuple-element.77.d_ref, ...), custom_call_target="tpu_custom_call" | custom-call | flops 17999998976 | bytes 10000000 | tf_op jit(solution)/shard_map/expert_backward/pallas_call | solution.py:167
  137.0 4.2 %pair.1 = (bf16[2,96,2016]{2,1,0:T(8,128)(2,1)S(1)}, bf16[2,96,2016]{2,1,0:T(8,128)(2,1)S(1)}) custom-call(bf16[2,3,2,2,96,672]{5,4,3,2,1,0:T(8,128)(2,1)S(1)} %get-tuple-element.72.grads), custom_call_target="tpu_custom_call" | custom-call | flops 10000000000 | bytes 4000000 | tf_op jit(solution)/shard_map/pair/pallas_call | solution.py:450
  141.1 0.0 copy-start.7
  141.1 0.0 copy-start.9
  141.2 3.0 %collective-permute-start.2 = (bf16[2,96,2016]{2,1,0:T(8,128)(2,1)S(1)}, bf16[2,96,2016]{2,1,0:T(8,128)(2,1)S(1)}, u32[]{:S(2)}, u32[]{:S(2)}) collective-permute-start(bf16[2,96,2016]{2,1,0:T(8,128)(2,1)S(1)} %get-tuple-element.74), channel_id=1, source_target_pairs={{0,2},{2,0},{1,3},{3,1},{4,6},{6,4},{5,7},{7,5},{8,10},{10,8},{9,1... | collective-permute-start | bytes 2322440 | tf_op jit(solution)/shard_map/ppermute | solution.py:704
  144.2 0.0 collective-permute-done.3.two_got
  144.2 10.8 %expert_backward.5 = (bf16[2,4,256,384]{3,2,1,0:T(8,128)(2,1)S(1)}, bf16[1,3,2,2,96,672]{5,4,3,2,1,0:T(8,128)(2,1)S(1)}, bf16[1,2,1280,384]{3,2,1,0:T(8,128)(2,1)S(1)}, bf16[1,3,1024,672]{3,2,1,0:T(8,128)(2,1)S(1)}) custom-call(s32[8,8]{1,0:T(8,128)S(1)} %get-tuple-element.58.off_ref, bf16[4,4,256,384]{3,2,1,0:T(8,128)(2,1)S(1)} %get-tuple-element.60.x_ref, ...), custom_call_target="tpu_custom_call" | custom-call | flops 17999998976 | bytes 10000000 | tf_op jit(solution)/shard_map/expert_backward/pallas_call | solution.py:167
  155.0 0.0 copy-done.7
  155.0 0.0 copy-done.9
  155.0 25.1 %exit.1 = (bf16[512,384]{1,0:T(8,128)(2,1)S(1)}, bf16[24,384]{1,0:T(8,128)(2,1)S(1)}, bf16[24,384]{1,0:T(8,128)(2,1)S(1)}, bf16[2,96,672]{2,1,0:T(8,128)(2,1)S(1...) custom-call(bf16[2,4,256,384]{3,2,1,0:T(8,128)(2,1)S(1)} %get-tuple-, ...), custom_call_target="tpu_custom_call" | custom-call | flops 10000000000 | bytes 4000000 | tf_op jit(solution)/shard_map/exit/pallas_call | solution.py:450
  180.1 0.0 collective-permute-done.2.got
  180.1 2.0 %store.1 = (bf16[512,384]{1,0:T(8,128)(2,1)}, bf16[24,384]{1,0:T(8,128)(2,1)}, bf16[24,384]{1,0:T(8,128)(2,1)}, bf16[4,96,672]{2,1,0:T(8,128)(2,1)}, bf16[4,96,6...) custom-call(bf16[2,96,2016]{2,1,0:T(8,128)(2,1)S(1)} %get-tuple-elem, ...), custom_call_target="tpu_custom_call" | custom-call | flops 1000000000 | bytes 4000000 | tf_op jit(solution)/shard_map/store/pallas_call | solution.py:691
Async XLA Ops:
  3.7 22.7 %copy-start.6 = (bf16[512,384]{1,0:T(8,128)(2,1)S(1)}, bf16[512,384]{1,0:T(8,128)(2,1)}, u32[]{:S(2)}) copy-start(bf16[512,384]{1,0:T(8,128)(2,1)} %dy_ref.1) | copy-start | bytes 1179652
  3.7 24.7 %copy-start.3 = (bf16[4,384,672]{1,2,0:T(8,128)(2,1)S(1)}, bf16[4,384,672]{1,2,0:T(8,128)(2,1)}, u32[]{:S(2)}) copy-start(bf16[4,384,672]{1,2,0:T(8,128)(2,1)} %param.19) | copy-start | bytes 6193156
  3.7 24.7 %copy-start.4 = (bf16[4,384,672]{1,2,0:T(8,128)(2,1)S(1)}, bf16[4,384,672]{1,2,0:T(8,128)(2,1)}, u32[]{:S(2)}) copy-start(bf16[4,384,672]{1,2,0:T(8,128)(2,1)} %param.20) | copy-start | bytes 6193156
  3.7 24.7 %copy-start.5 = (bf16[4,672,384]{2,1,0:T(8,128)(2,1)S(1)}, bf16[4,672,384]{2,1,0:T(8,128)(2,1)}, u32[]{:S(2)}) copy-start(bf16[4,672,384]{2,1,0:T(8,128)(2,1)} %wd_ref.7) | copy-start | bytes 6193156
  26.4 12.0 %collective-permute-start.1 = (bf16[512,384]{1,0:T(8,128)(2,1)S(1)}, bf16[512,384]{1,0:T(8,128)(2,1)S(1)}, u32[]{:S(2)}, u32[]{:S(2)}) collective-permute-start(bf16[512,384]{1,0:T(8,128)(2,1)S(1)} %copy-done.6), channel_id=1, source_target_pairs={{0,8},{4,12},{8,0},{12,4},{1,9},{5,13},{9,1},{13,5},{2,10},{6,14},... | collective-permute-start | bytes 1179656 | tf_op jit(solution)/shard_map/ppermute | solution.py:726
  27.9 10.5 %collective-permute-start = (bf16[512,384]{1,0:T(8,128)(2,1)S(1)}, bf16[512,384]{1,0:T(8,128)(2,1)S(1)}, u32[]{:S(2)}, u32[]{:S(2)}) collective-permute-start(bf16[512,384]{1,0:T(8,128)(2,1)S(1)} %copy-done.6), channel_id=1, source_target_pairs={{0,4},{4,0},{8,12},{12,8},{1,5},{5,1},{9,13},{13,9},{2,6},{6,2},{1... | collective-permute-start | bytes 1179656 | tf_op jit(solution)/shard_map/ppermute | solution.py:726
  28.4 10.0 %copy-start.8 = (bf16[384,384]{1,0:T(8,128)(2,1)S(1)}, bf16[384,384]{1,0:T(8,128)(2,1)}, u32[]{:S(2)}) copy-start(bf16[384,384]{1,0:T(8,128)(2,1)} %dense_ref.4) | copy-start | bytes 884740
  38.4 33.0 %copy-start = (bf16[4,384,672]{1,2,0:T(8,128)(2,1)S(1)}, bf16[4,384,672]{1,2,0:T(8,128)(2,1)}, u32[]{:S(2)}) copy-start(bf16[4,384,672]{1,2,0:T(8,128)(2,1)} %param.25) | copy-start | bytes 6193156
  38.4 33.0 %copy-start.1 = (bf16[4,384,672]{1,2,0:T(8,128)(2,1)S(1)}, bf16[4,384,672]{1,2,0:T(8,128)(2,1)}, u32[]{:S(2)}) copy-start(bf16[4,384,672]{1,2,0:T(8,128)(2,1)} %param.26) | copy-start | bytes 6193156
  38.5 33.0 %copy-start.2 = (bf16[4,672,384]{2,1,0:T(8,128)(2,1)S(1)}, bf16[4,672,384]{2,1,0:T(8,128)(2,1)}, u32[]{:S(2)}) copy-start(bf16[4,672,384]{2,1,0:T(8,128)(2,1)} %wd_ref.5) | copy-start | bytes 6193156
  125.3 18.9 %collective-permute-start.3 = (bf16[2,96,2016]{2,1,0:T(8,128)(2,1)S(1)}, bf16[2,96,2016]{2,1,0:T(8,128)(2,1)S(1)}, u32[]{:S(2)}, u32[]{:S(2)}) collective-permute-start(bf16[2,96,2016]{2,1,0:T(8,128)(2,1)S(1)} %get-tuple-element.76), channel_id=1, source_target_pairs={{0,2},{2,0},{1,3},{3,1},{4,6},{6,4},{5,7},{7,5},{8,10},{10,8},{9,1... | collective-permute-start | bytes 2322440 | tf_op jit(solution)/shard_map/ppermute | solution.py:704
  141.1 13.8 %copy-start.7 = (bf16[512,384]{1,0:T(8,128)(2,1)S(1)}, bf16[512,384]{1,0:T(8,128)(2,1)}, u32[]{:S(2)}) copy-start(bf16[512,384]{1,0:T(8,128)(2,1)} %tok_ref.1) | copy-start | bytes 1179652
  141.1 13.8 %copy-start.9 = (bf16[384,384]{1,0:T(8,128)(2,1)S(1)}, bf16[384,384]{1,0:T(8,128)(2,1)}, u32[]{:S(2)}) copy-start(bf16[384,384]{1,0:T(8,128)(2,1)} %dense_ref.5) | copy-start | bytes 884740
  141.2 38.9 %collective-permute-start.2 = (bf16[2,96,2016]{2,1,0:T(8,128)(2,1)S(1)}, bf16[2,96,2016]{2,1,0:T(8,128)(2,1)S(1)}, u32[]{:S(2)}, u32[]{:S(2)}) collective-permute-start(bf16[2,96,2016]{2,1,0:T(8,128)(2,1)S(1)} %get-tuple-element.74), channel_id=1, source_target_pairs={{0,2},{2,0},{1,3},{3,1},{4,6},{6,4},{5,7},{7,5},{8,10},{10,8},{9,1... | collective-permute-start | bytes 2322440 | tf_op jit(solution)/shard_map/ppermute | solution.py:704

commit v7 on v6

--- a/solution.py
+++ b/solution.py
@@ -716,7 +716,8 @@
         padded = block(N_LOC, N_EP, CAP, D)
         every = pltpu.VMEM((N_EP, TOK, D), BF16)
         own = pltpu.VMEM((TOK, D), BF16)
-        pack = jnp.concatenate([route_idx1.T.astype(F32), route_idx2.T.astype(F32), route_gate1.T, route_gate2.T], axis=0)
+        place = lambda part, k: jnp.pad(part, ((0, 0), (4 * k, 12 - 4 * k)))
+        pack = ((place(route_idx1, 0) + place(route_idx2, 1)).astype(F32) + (place(route_gate1, 2) + place(route_gate2, 3))).T
         mixed_one = (tokens.astype(F32) + jnp.dot(tokens, dense_w1, preferred_element_type=F32)).astype(BF16)
         x_one, rank, gate, off = call(
             entry_kernel, 'entry', 0, (mixed_one, pack),

time: 183 us -> 181 us (0.989)
  starting transfers between devices: 5.55 us -> 2.78 us
  Pallas kernels: 173 us -> 175 us
    pallas_call x5, Pallas kernels: 118 us -> 122 us  [call(): pl.pallas_call(kernel, out_shape=outs, scratch_shapes=scratch, in_specs=[...]
    ppermute x2, starting transfers between devices: 3.49 us -> 0.72 us  [along_x(): return lax.ppermute(sent, 'dp', [(0, 2), (2, 0), (1, 3), (3, 1)])]
  transfers between devices with their start and end apart: 4 -> 4, of which waited for: 0 -> 0; matrix products, arithmetic and copies ran while one was open for 0% -> 0% of each run, Pallas kernels for 34% -> 36%
where the time goes in v7:
time: 181 us
  Pallas kernels  175 us (97%)
  starting transfers between devices  2.78 us (2%)
    pallas_call x5, Pallas kernels, call(): pl.pallas_call(kernel, out_shape=outs, scratch_shapes=scratch, in_specs=[...  122 us
    pallas_call x4, Pallas kernels, plain(): pl.pallas_call(kernel, out_shape=outs, in_specs=[SMEM] + [VMEM] * (len(in...  51 us
  transfers between devices with their start and end apart: 4, of which 0 were waited for; matrix products, arithmetic and copies ran while one was open for 0% of the time, Pallas kernels for 36%

profile of v7, /device:TPU:0, one launch (start us, length us, event | category | flops | bytes accessed | tf_op | source)
XLA Modules:
  0.0 181.0 jit_solution(11827499963664221943)
XLA Ops:
  0.6 1.6 fusion.own.u_ref
  2.2 0.8 add_bitcast_fusion.pack_ref
  3.0 0.0 copy-start.6
  3.0 0.0 copy-start.3
  3.0 0.0 copy-start.4
  3.0 0.0 copy-start.5
  3.1 22.6 %entry.1 = (bf16[4,4,256,384]{3,2,1,0:T(8,128)(2,1)S(1)}, s32[2,4,8,512]{3,2,1,0:T(8,128)S(1)}, f32[2,4,512,8]{3,2,1,0:T(8,128)S(1)}, s32[8,8]{1,0:T(8,128)S(1)}) custom-call(bf16[512,384]{1,0:T(8,128)(2,1)S(1)} %fusion.own.u_ref, f32[16,512]{1,0:T(8,128)S(1)} %add_bitcast_fusion.pack_ref), custom_call_target="tpu_custom_call" | custom-call | flops 10000000000 | bytes 4000000 | tf_op jit(solution)/shard_map/entry/pallas_call | solution.py:450
  25.7 0.0 copy-done.6
  25.7 1.6 collective-permute-start.1
  27.2 0.5 collective-permute-start
  27.8 0.0 copy-done.3
  27.8 0.0 copy-done.4
  27.8 0.0 copy-done.5
  27.8 0.0 copy-start.8
  27.8 10.4 %expert_forward.1.o_ref = bf16[4,4,256,384]{3,2,1,0:T(8,128)(2,1)S(1)} custom-call(s32[8,8]{1,0:T(8,128)S(1)} %get-tuple-element.58.off_ref, bf16[4,4,256,384]{3,2,1,0:T(8,128)(2,1)S(1)} %get-tuple-element.60.x_ref, bf16[4,672,384]{2,1,0:T(8,128)(2,1)S(1)} %bitcast.12, bf16[4,672,384]{2,1,0:T(8,128)(2,1)S(1)} %bitcast.15, bf16[4,672,384]{2,1,0:T(8,128)(2,1)S(1)} %copy-done.5), custom_call_target="tpu_custom_call" | custom-call | flops 10000000000 | bytes 10000000 | tf_op jit(solution)/shard_map/expert_forward/pallas_call | solution.py:167
  38.2 0.0 collective-permute-done.1.dy_z
  38.2 0.0 collective-permute-done.dy_y
  38.2 0.0 copy-done.8
  38.2 0.0 copy-start
  38.2 0.0 copy-start.1
  38.2 0.0 copy-start.2
  38.2 34.2 %middle.1 = (bf16[512,384]{1,0:T(8,128)(2,1)S(1)}, bf16[4,4,256,384]{3,2,1,0:T(8,128)(2,1)S(1)}, bf16[4,4,256,384]{3,2,1,0:T(8,128)(2,1)S(1)}) custom-call(bf16[4,4,256,384]{3,2,1,0:T(8,128)(2,1)S(1)} %expert_forward.1.o_ref, bf16[512,384]{1,0:T(8,128)(2,1)S(1)} %fusion.own.u_ref, bf16[384,384]{1,0:T(8,128)(2,1)S(1)} %copy-done.8, ...), custom_call_target="tpu_custom_call" | custom-call | flops 10000000000 | bytes 4000000 | tf_op jit(solution)/shard_map/middle/pallas_call | solution.py:450
  72.5 0.0 copy-done
  72.5 0.0 copy-done.1
  72.5 0.0 copy-done.2
  72.5 17.6 %expert_backward.3 = (bf16[4,4,256,384]{3,2,1,0:T(8,128)(2,1)S(1)}, bf16[2,3,2,2,96,672]{5,4,3,2,1,0:T(8,128)(2,1)S(1)}, bf16[2,2,1280,384]{3,2,1,0:T(8,128)(2,1)S(1)}, bf16[2,3,1024,672]{3,2,1,0:T(8,128)(2,1)S(1)}) custom-call(s32[8,8]{1,0:T(8,128)S(1)} %get-tuple-element.58.off_ref, bf16[4,4,256,384]{3,2,1,0:T(8,128)(2,1)S(1)} %get-tuple-element.64.x_ref, ...), custom_call_target="tpu_custom_call" | custom-call | flops 35999997952 | bytes 10000000 | tf_op jit(solution)/shard_map/expert_backward/pallas_call | solution.py:167
  90.1 33.9 %turn.1 = (bf16[512,384]{1,0:T(8,128)(2,1)S(1)}, bf16[4,4,256,384]{3,2,1,0:T(8,128)(2,1)S(1)}, bf16[2,2,2,2,24,384]{5,4,3,2,1,0:T(8,128)(2,1)S(1)}, bf16[2,96,67...) custom-call(bf16[4,4,256,384]{3,2,1,0:T(8,128)(2,1)S(1)} %get-tuple-, ...), custom_call_target="tpu_custom_call" | custom-call | flops 10000000000 | bytes 4000000 | tf_op jit(solution)/shard_map/turn/pallas_call | solution.py:450
  124.0 0.3 collective-permute-start.3
  124.4 12.6 %expert_backward.4 = (bf16[2,4,256,384]{3,2,1,0:T(8,128)(2,1)S(1)}, bf16[2,3,2,2,96,672]{5,4,3,2,1,0:T(8,128)(2,1)S(1)}) custom-call(s32[8,8]{1,0:T(8,128)S(1)} %get-tuple-element.58.off_ref, bf16[4,4,256,384]{3,2,1,0:T(8,128)(2,1)S(1)} %get-tuple-element.60.x_ref, bf16[4,4,256,384]{3,2,1,0:T(8,128)(2,1)S(1)} %get-tuple-element.77.d_ref, ...), custom_call_target="tpu_custom_call" | custom-call | flops 17999998976 | bytes 10000000 | tf_op jit(solution)/shard_map/expert_backward/pallas_call | solution.py:167
  136.9 4.2 %pair.1 = (bf16[2,96,2016]{2,1,0:T(8,128)(2,1)S(1)}, bf16[2,96,2016]{2,1,0:T(8,128)(2,1)S(1)}) custom-call(bf16[2,3,2,2,96,672]{5,4,3,2,1,0:T(8,128)(2,1)S(1)} %get-tuple-element.72.grads), custom_call_target="tpu_custom_call" | custom-call | flops 10000000000 | bytes 4000000 | tf_op jit(solution)/shard_map/pair/pallas_call | solution.py:450
  141.1 0.0 copy-start.7
  141.1 0.0 copy-start.9
  141.1 0.4 collective-permute-start.2
  141.5 0.0 collective-permute-done.3.two_got
  141.5 10.4 %expert_backward.5 = (bf16[2,4,256,384]{3,2,1,0:T(8,128)(2,1)S(1)}, bf16[1,3,2,2,96,672]{5,4,3,2,1,0:T(8,128)(2,1)S(1)}, bf16[1,2,1280,384]{3,2,1,0:T(8,128)(2,1)S(1)}, bf16[1,3,1024,672]{3,2,1,0:T(8,128)(2,1)S(1)}) custom-call(s32[8,8]{1,0:T(8,128)S(1)} %get-tuple-element.58.off_ref, bf16[4,4,256,384]{3,2,1,0:T(8,128)(2,1)S(1)} %get-tuple-element.60.x_ref, ...), custom_call_target="tpu_custom_call" | custom-call | flops 17999998976 | bytes 10000000 | tf_op jit(solution)/shard_map/expert_backward/pallas_call | solution.py:167
  151.9 0.0 copy-done.7
  151.9 0.0 copy-done.9
  152.0 26.8 %exit.1 = (bf16[512,384]{1,0:T(8,128)(2,1)S(1)}, bf16[24,384]{1,0:T(8,128)(2,1)S(1)}, bf16[24,384]{1,0:T(8,128)(2,1)S(1)}, bf16[2,96,672]{2,1,0:T(8,128)(2,1)S(1...) custom-call(bf16[2,4,256,384]{3,2,1,0:T(8,128)(2,1)S(1)} %get-tuple-, ...), custom_call_target="tpu_custom_call" | custom-call | flops 10000000000 | bytes 4000000 | tf_op jit(solution)/shard_map/exit/pallas_call | solution.py:450
  178.8 0.0 collective-permute-done.2.got
  178.8 2.0 %store.1 = (bf16[512,384]{1,0:T(8,128)(2,1)}, bf16[24,384]{1,0:T(8,128)(2,1)}, bf16[24,384]{1,0:T(8,128)(2,1)}, bf16[4,96,672]{2,1,0:T(8,128)(2,1)}, bf16[4,96,6...) custom-call(bf16[2,96,2016]{2,1,0:T(8,128)(2,1)S(1)} %get-tuple-elem, ...), custom_call_target="tpu_custom_call" | custom-call | flops 1000000000 | bytes 4000000 | tf_op jit(solution)/shard_map/store/pallas_call | solution.py:691
Async XLA Ops:
  3.0 22.7 %copy-start.6 = (bf16[512,384]{1,0:T(8,128)(2,1)S(1)}, bf16[512,384]{1,0:T(8,128)(2,1)}, u32[]{:S(2)}) copy-start(bf16[512,384]{1,0:T(8,128)(2,1)} %dy_ref.1) | copy-start | bytes 1179652
  3.0 24.7 %copy-start.3 = (bf16[4,384,672]{1,2,0:T(8,128)(2,1)S(1)}, bf16[4,384,672]{1,2,0:T(8,128)(2,1)}, u32[]{:S(2)}) copy-start(bf16[4,384,672]{1,2,0:T(8,128)(2,1)} %param.19) | copy-start | bytes 6193156
  3.0 24.7 %copy-start.4 = (bf16[4,384,672]{1,2,0:T(8,128)(2,1)S(1)}, bf16[4,384,672]{1,2,0:T(8,128)(2,1)}, u32[]{:S(2)}) copy-start(bf16[4,384,672]{1,2,0:T(8,128)(2,1)} %param.20) | copy-start | bytes 6193156
  3.0 24.7 %copy-start.5 = (bf16[4,672,384]{2,1,0:T(8,128)(2,1)S(1)}, bf16[4,672,384]{2,1,0:T(8,128)(2,1)}, u32[]{:S(2)}) copy-start(bf16[4,672,384]{2,1,0:T(8,128)(2,1)} %wd_ref.7) | copy-start | bytes 6193156
  25.7 12.5 %collective-permute-start.1 = (bf16[512,384]{1,0:T(8,128)(2,1)S(1)}, bf16[512,384]{1,0:T(8,128)(2,1)S(1)}, u32[]{:S(2)}, u32[]{:S(2)}) collective-permute-start(bf16[512,384]{1,0:T(8,128)(2,1)S(1)} %copy-done.6), channel_id=1, source_target_pairs={{0,8},{4,12},{8,0},{12,4},{1,9},{5,13},{9,1},{13,5},{2,10},{6,14},... | collective-permute-start | bytes 1179656 | tf_op jit(solution)/shard_map/ppermute | solution.py:727
  27.2 10.9 %collective-permute-start = (bf16[512,384]{1,0:T(8,128)(2,1)S(1)}, bf16[512,384]{1,0:T(8,128)(2,1)S(1)}, u32[]{:S(2)}, u32[]{:S(2)}) collective-permute-start(bf16[512,384]{1,0:T(8,128)(2,1)S(1)} %copy-done.6), channel_id=1, source_target_pairs={{0,4},{4,0},{8,12},{12,8},{1,5},{5,1},{9,13},{13,9},{2,6},{6,2},{1... | collective-permute-start | bytes 1179656 | tf_op jit(solution)/shard_map/ppermute | solution.py:727
  27.8 10.4 %copy-start.8 = (bf16[384,384]{1,0:T(8,128)(2,1)S(1)}, bf16[384,384]{1,0:T(8,128)(2,1)}, u32[]{:S(2)}) copy-start(bf16[384,384]{1,0:T(8,128)(2,1)} %dense_ref.4) | copy-start | bytes 884740
  38.2 34.3 %copy-start = (bf16[4,384,672]{1,2,0:T(8,128)(2,1)S(1)}, bf16[4,384,672]{1,2,0:T(8,128)(2,1)}, u32[]{:S(2)}) copy-start(bf16[4,384,672]{1,2,0:T(8,128)(2,1)} %param.25) | copy-start | bytes 6193156
  38.2 34.3 %copy-start.1 = (bf16[4,384,672]{1,2,0:T(8,128)(2,1)S(1)}, bf16[4,384,672]{1,2,0:T(8,128)(2,1)}, u32[]{:S(2)}) copy-start(bf16[4,384,672]{1,2,0:T(8,128)(2,1)} %param.26) | copy-start | bytes 6193156
  38.2 34.3 %copy-start.2 = (bf16[4,672,384]{2,1,0:T(8,128)(2,1)S(1)}, bf16[4,672,384]{2,1,0:T(8,128)(2,1)}, u32[]{:S(2)}) copy-start(bf16[4,672,384]{2,1,0:T(8,128)(2,1)} %wd_ref.5) | copy-start | bytes 6193156
  124.0 17.5 %collective-permute-start.3 = (bf16[2,96,2016]{2,1,0:T(8,128)(2,1)S(1)}, bf16[2,96,2016]{2,1,0:T(8,128)(2,1)S(1)}, u32[]{:S(2)}, u32[]{:S(2)}) collective-permute-start(bf16[2,96,2016]{2,1,0:T(8,128)(2,1)S(1)} %get-tuple-element.76), channel_id=1, source_target_pairs={{0,2},{2,0},{1,3},{3,1},{4,6},{6,4},{5,7},{7,5},{8,10},{10,8},{9,1... | collective-permute-start | bytes 2322440 | tf_op jit(solution)/shard_map/ppermute | solution.py:704
  141.1 10.8 %copy-start.7 = (bf16[512,384]{1,0:T(8,128)(2,1)S(1)}, bf16[512,384]{1,0:T(8,128)(2,1)}, u32[]{:S(2)}) copy-start(bf16[512,384]{1,0:T(8,128)(2,1)} %tok_ref.1) | copy-start | bytes 1179652
  141.1 10.8 %copy-start.9 = (bf16[384,384]{1,0:T(8,128)(2,1)S(1)}, bf16[384,384]{1,0:T(8,128)(2,1)}, u32[]{:S(2)}) copy-start(bf16[384,384]{1,0:T(8,128)(2,1)} %dense_ref.5) | copy-start | bytes 884740
  141.1 37.7 %collective-permute-start.2 = (bf16[2,96,2016]{2,1,0:T(8,128)(2,1)S(1)}, bf16[2,96,2016]{2,1,0:T(8,128)(2,1)S(1)}, u32[]{:S(2)}, u32[]{:S(2)}) collective-permute-start(bf16[2,96,2016]{2,1,0:T(8,128)(2,1)S(1)} %get-tuple-element.74), channel_id=1, source_target_pairs={{0,2},{2,0},{1,3},{3,1},{4,6},{6,4},{5,7},{7,5},{8,10},{10,8},{9,1... | collective-permute-start | bytes 2322440 | tf_op jit(solution)/shard_map/ppermute | solution.py:704
